TPU v7x, 256 devices: a whole 4x4x8 slice. The times are simulated.
256 devices in a mesh: lat: 16 (over y, x), lon: 16 (over z, core).
Axes of the slice: x: 4, y: 4, z: 8, core: 2. Of those that a mesh axis runs over, the one named last changes fastest.
Arguments:
- fine_nodes: float32 [2, 512, 512, 512], P(None, 'lat', 'lon'), may hold values from -6 to 6
- mid_nodes: float32 [2, 128, 128, 512], P(None, 'lat', 'lon'), may hold values from -6 to 6
- coarse_nodes: float32 [2, 32, 32, 512], P(None, 'lat', 'lon'), may hold values from -6 to 6
- edge_flags: int32 [8, 512, 512], P(None, 'lat', 'lon'), may hold values 0 or 1
- proc_weights: bfloat16 [3, 4, 512, 512], replicated, may hold values from -0.25 to 0.25
- bridge_weights: bfloat16 [4, 512, 512], replicated, may hold values from -0.25 to 0.25
- proc_biases: float32 [3, 512], replicated, may hold values from -3 to 3
Outputs:
- refined: float32 [2, 512, 512, 512], P(None, 'lat', 'lon')
- fine_average: bfloat16 [2, 512, 512, 512], P(None, 'lat', 'lon')
All inputs are finite; a program needn't handle non-finite values. No bound on the sum of `edge_flags` on one device may be relied on, other than what follows from the above.
Results may differ from a plain program's by a relative error of at most 0.005.
Values may be sent and summed in bfloat16 or wider, within the bound.
No kernel may reach another device: no remote copies, remote signals or barrier semaphores. Data moves between devices by JAX's collectives and lax.ppermute only.
A program may use at most 128 MiB of HBM per device.

v0:
```python
import jax
import jax.numpy as jnp
from jax import lax
from jax.sharding import PartitionSpec as P

offsets = ((-1, -1), (-1, 0), (-1, 1), (0, -1), (0, 1), (1, -1), (1, 0), (1, 1))


def padded_2(block, sides, width):
    for axis, dim in sides:
        count = lax.axis_size(axis)
        forward = [(i, i + 1) for i in range(count - 1)]
        forward.append((count - 1, 0))
        backward = [(target, source) for source, target in forward]
        low = lax.ppermute(
            lax.slice_in_dim(block, block.shape[dim] - width, None, axis=dim), axis, forward
        )
        high = lax.ppermute(lax.slice_in_dim(block, 0, width, axis=dim), axis, backward)
        block = jnp.concatenate([low, block, high], axis=dim)
    return block


def project(values, matrix):
    shape = values.shape
    flat = values.reshape(-1, shape[-1])
    result = jnp.dot(flat, matrix, preferred_element_type=jnp.float32)
    return result.reshape(shape[:-1] + (matrix.shape[1],))


def level_pass(states, flag_grid, weights, biases, border, row_start, total_rows):
    rows = states.shape[1]
    cols = states.shape[2]
    operand = states.astype(jnp.bfloat16)
    receiver = project(operand, weights[0])
    sender = project(operand, weights[1]).astype(jnp.bfloat16)
    padded = border(sender)
    row_ids = row_start + jnp.arange(rows, dtype=jnp.int32)
    summed = jnp.zeros(states.shape, jnp.float32)
    for direction, (step_lat, step_lon) in enumerate(offsets):
        inside = ((row_ids + step_lat >= 0) & (row_ids + step_lat < total_rows)).astype(
            jnp.float32
        )[:, None]
        if flag_grid is None:
            usable = inside
        else:
            usable = inside * flag_grid[direction].astype(jnp.float32)
        nearby = padded[
            :, 1 + step_lat : 1 + step_lat + rows, 1 + step_lon : 1 + step_lon + cols
        ].astype(jnp.float32)
        hidden = jax.nn.silu(receiver + nearby + biases).astype(jnp.bfloat16)
        message = jax.nn.silu(project(hidden, weights[2]))
        summed = summed + usable[None, :, :, None] * message
    average = (summed * 0.125).astype(jnp.bfloat16)
    return (states + project(average, weights[3]), average)


def fine_border(sender):
    return padded_2(sender, (("lat", 1), ("lon", 2)), 1)


def mid_border(sender):
    return padded_2(sender, (("lat", 1), ("lon", 2)), 1)


def coarse_border(sender):
    return padded_2(sender, (("lat", 1), ("lon", 2)), 1)


def pooled(states):
    samples, rows, cols, features = states.shape
    blocks = states.reshape(samples, rows // 4, 4, cols // 4, 4, features)
    return jnp.mean(blocks, axis=(2, 4)).astype(jnp.bfloat16)


def expand(values):
    return jnp.repeat(jnp.repeat(values, 4, axis=1), 4, axis=2)


def local(
    fine_nodes, mid_nodes, coarse_nodes, edge_flags, proc_weights, bridge_weights, proc_biases
):
    lat_index = lax.axis_index("lat")
    lat_count = lax.axis_size("lat")
    fine_rows = fine_nodes.shape[1]
    mid_rows = mid_nodes.shape[1]
    coarse_rows = coarse_nodes.shape[1]
    fine_one, fine_average = level_pass(
        fine_nodes,
        edge_flags,
        proc_weights[0],
        proc_biases[0],
        fine_border,
        lat_index * fine_rows,
        fine_rows * lat_count,
    )
    mid_zero = mid_nodes + jax.nn.silu(project(pooled(fine_one), bridge_weights[0]))
    mid_one, unused_mid = level_pass(
        mid_zero,
        None,
        proc_weights[1],
        proc_biases[1],
        mid_border,
        lat_index * mid_rows,
        mid_rows * lat_count,
    )
    coarse_zero = coarse_nodes + jax.nn.silu(project(pooled(mid_one), bridge_weights[1]))
    coarse_one, unused_coarse = level_pass(
        coarse_zero,
        None,
        proc_weights[2],
        proc_biases[2],
        coarse_border,
        lat_index * coarse_rows,
        coarse_rows * lat_count,
    )
    lifted = jax.nn.silu(project(coarse_one.astype(jnp.bfloat16), bridge_weights[2]))
    mid_two = mid_one + expand(lifted)
    spread = jax.nn.silu(project(mid_two.astype(jnp.bfloat16), bridge_weights[3]))
    return (fine_one + expand(spread), fine_average)


def solution(mesh):
    placed = (
        P(None, "lat", "lon", None),
        P(None, "lat", "lon", None),
        P(None, "lat", "lon", None),
        P(None, "lat", "lon"),
        P(),
        P(),
        P(),
    )
    return jax.shard_map(
        local,
        mesh=mesh,
        in_specs=placed,
        out_specs=(P(None, "lat", "lon", None), P(None, "lat", "lon", None)),
        check_vma=False,
    )
```

profile of v0, /device:TPU:30, one launch (start us, length us, event | category | flops | bytes accessed | tf_op | source)
XLA Modules:
  0.0 141.5 jit_solution(1405798278900557515)
XLA Ops:
  0.6 3.7 %convolution_convert_fusion = bf16[2,32,32,512]{3,2,1,0:T(8,128)(2,1)S(1)} fusion(f32[2,32,32,512]{3,2,1,0:T(8,128)} %param.7, bf16[3,4,512,512]{3,2,1,0:T(8,128)(2,1)} %param.11), kind=kOutput, calls=%fused_computation.22 | convolution fusion | flops 1075838976 | bytes 6815744 | tf_op jit(solution)/shard_map/dot_general | solution.py:26
  4.4 1.9 %collective-permute-start = (bf16[2,1,32,512]{3,2,1,0:T(8,128)(2,1)S(1)}, bf16[2,1,32,512]{3,2,1,0:T(8,128)(2,1)S(1)}, u32[]{:S(2)}, u32[]{:S(2)}) collective-permute-start(bf16[2,1,32,512]{3,2,1,0:T(8,128)(2,1)S(1)} %get-tuple-element.6), channel_id=1, source_target_pairs={{0,16},{16,32},{32,48},{48,64},{64,80},{80,96},{96,112},{112,128},... | collective-permute-start | bytes 196616 | tf_op jit(solution)/shard_map/ppermute | solution.py:15
  6.5 4.3 %fusion.11 = f32[2,32,32,512]{3,2,1,0:T(8,128)} fusion(f32[2,32,32,512]{3,2,1,0:T(8,128)S(1)} %copy-done, bf16[3,4,512,512]{3,2,1,0:T(8,128)(2,1)} %param.11), kind=kOutput, calls=%fused_computation.30 | convolution fusion | flops 1074790400 | bytes 8912896 | tf_op jit(solution)/shard_map/dot_general | solution.py:26
  11.0 2.9 %collective-permute-done.1 = bf16[2,1,32,512]{3,2,1,0:T(8,128)(2,1)S(1)} collective-permute-done((bf16[2,1,32,512]{3,2,1,0:T(8,128)(2,1)S(1)}, bf16[2,1,32,512]{3,2,1,0:T(8,128)(2,1)S(1)}, u32[]{:S(2)}, u32[]{:S(2)}) %collective-permute-start.1) | collective-permute-done | bytes 65568 | tf_op jit(solution)/shard_map/ppermute | solution.py:18
  14.1 2.9 %collective-permute-start.3 = (bf16[2,34,1,512]{3,2,1,0:T(2,128)(2,1)S(1)}, bf16[2,34,1,512]{3,2,1,0:T(2,128)(2,1)S(1)}, u32[]{:S(2)}, u32[]{:S(2)}) collective-permute-start(bf16[2,34,1,512]{3,2,1,0:T(2,128)(2,1)S(1)} %get-tuple-element.4), channel_id=1, source_target_pairs={{1,0},{2,1},{3,2},{4,3},{5,4},{6,5},{7,6},{8,7},{9,8},{10,9},{11,1... | collective-permute-start | bytes 208904 | tf_op jit(solution)/shard_map/ppermute | solution.py:18
  17.1 5.8 %fusion.6 = f32[2,32,32,512]{3,2,1,0:T(8,128)} fusion(f32[2,32,32,512]{3,2,1,0:T(8,128)} %fusion.11, bf16[2,32,32,512]{3,2,1,0:T(8,128)(2,1)S(1)} %convolution_convert_fusion, bf16[2,1,32,512]{3,2,1,0:T(8,128)(2,1)S(1)} %collective-permute-done, f32[512]{0:T(512)S(1)} %bitcast.220, bf16[3,4,512,512]{3,2,1,0:T(8,128)(2,1)} %param.11), kind=kOutput, calls=%fused_computation.20 | convolution fusion | flops 1083179008 | bytes 11077632 | tf_op jit(solution)/shard_map/dot_general | solution.py:26
  22.9 3.4 %fusion.7 = f32[2,32,32,512]{3,2,1,0:T(8,128)} fusion(f32[2,32,32,512]{3,2,1,0:T(8,128)S(1)} %copy-done.2, bf16[2,1,32,512]{3,2,1,0:T(8,128)(2,1)S(1)} %collective-permute-done.1, bf16[2,32,32,512]{3,2,1,0:T(8,128)(2,1)S(1)} %convolution_convert_fusion, f32[512]{0:T(512)S(1)} %bitcast.221, bf16[3,4,512,512]{3,2,1,0:T(8,128)(2,1)S(1)} %bitcast.202), kind=kOutput, calls=%fused_computation.21 | convolution fusion | flops 1083179008 | bytes 11077632 | tf_op jit(solution)/shard_map/dot_general | solution.py:26
  26.4 1.6 %pad_maximum_fusion = (bf16[2,34,33,512]{3,2,1,0:T(8,128)(2,1)S(1)}, bf16[2,34,33,512]{3,2,1,0:T(8,128)(2,1)S(1)}) fusion(bf16[2,34,1,512]{3,2,1,0:T(2,128)(2,1)S(1)} %collective-permute-done.3, bf16[2,1,32,512]{3,2,1,0:T(8,128)(2,1)S(1)} %collective-permute-done.1, bf16[2,32,32,512]{3,2,1,0:T(8,128)(2,1)S(1)} %convolution_convert_fusion, ...), kind=kLoop, calls=%fused_computation.10 | loop fusion | flops 18382848 | bytes 6963200 | tf_op jit(solution)/shard_map/concatenate | solution.py:19
  28.0 3.4 %fusion = f32[2,32,32,512]{3,2,1,0:T(8,128)} fusion(f32[2,32,32,512]{3,2,1,0:T(8,128)S(1)} %copy-done.2, bf16[2,34,33,512]{3,2,1,0:T(8,128)(2,1)S(1)} %get-tuple-element.3, f32[512]{0:T(512)S(1)} %bitcast.222, bf16[3,4,512,512]{3,2,1,0:T(8,128)(2,1)S(1)} %bitcast.202), kind=kOutput, calls=%fused_computation.14 | convolution fusion | flops 1082130432 | bytes 11012096 | tf_op jit(solution)/shard_map/dot_general | solution.py:26
  31.4 3.4 %fusion.2 = f32[2,32,32,512]{3,2,1,0:T(8,128)} fusion(f32[2,32,32,512]{3,2,1,0:T(8,128)S(1)} %copy-done.2, bf16[2,34,33,512]{3,2,1,0:T(8,128)(2,1)S(1)} %get-tuple-element.3, f32[512]{0:T(512)S(1)} %bitcast.223, bf16[3,4,512,512]{3,2,1,0:T(8,128)(2,1)S(1)} %bitcast.202), kind=kOutput, calls=%fused_computation.16 | convolution fusion | flops 1082130432 | bytes 11012096 | tf_op jit(solution)/shard_map/dot_general | solution.py:26
  34.8 3.7 %fusion.1 = f32[2,32,32,512]{3,2,1,0:T(8,128)} fusion(f32[2,32,32,512]{3,2,1,0:T(8,128)S(1)} %copy-done.2, bf16[2,34,33,512]{3,2,1,0:T(8,128)(2,1)S(1)} %get-tuple-element.2, f32[512]{0:T(512)S(1)} %bitcast.224, bf16[3,4,512,512]{3,2,1,0:T(8,128)(2,1)S(1)} %bitcast.202), kind=kOutput, calls=%fused_computation.15 | convolution fusion | flops 1082130432 | bytes 11012096 | tf_op jit(solution)/shard_map/dot_general | solution.py:26
  38.5 3.8 %fusion.3 = f32[2,32,32,512]{3,2,1,0:T(8,128)} fusion(f32[2,32,32,512]{3,2,1,0:T(8,128)S(1)} %copy-done.2, bf16[2,34,33,512]{3,2,1,0:T(8,128)(2,1)S(1)} %get-tuple-element.2, f32[512]{0:T(512)S(1)} %bitcast.225, bf16[3,4,512,512]{3,2,1,0:T(8,128)(2,1)S(1)} %bitcast.202), kind=kOutput, calls=%fused_computation.17 | convolution fusion | flops 1082130432 | bytes 11012096 | tf_op jit(solution)/shard_map/dot_general | solution.py:26
  42.4 3.4 %fusion.4 = f32[2,32,32,512]{3,2,1,0:T(8,128)} fusion(f32[2,32,32,512]{3,2,1,0:T(8,128)S(1)} %copy-done.2, bf16[2,34,33,512]{3,2,1,0:T(8,128)(2,1)S(1)} %get-tuple-element.3, f32[512]{0:T(512)S(1)} %bitcast.226, bf16[3,4,512,512]{3,2,1,0:T(8,128)(2,1)S(1)} %bitcast.202), kind=kOutput, calls=%fused_computation.18 | convolution fusion | flops 1082130432 | bytes 11012096 | tf_op jit(solution)/shard_map/dot_general | solution.py:26
  45.7 15.6 %multiply_convert_fusion = bf16[2,32,32,512]{3,2,1,0:T(8,128)(2,1)S(1)} fusion(f32[2,32,32,512]{3,2,1,0:T(8,128)} %fusion.7, f32[2,32,32,512]{3,2,1,0:T(8,128)} %fusion.4, f32[2,32,32,512]{3,2,1,0:T(8,128)} %fusion.3, f32[2,32,32,512]{3,2,1,0:T(8,128)} %fusion.2, f32[2,32,32,512]{3,2,1,0:T(8,128)} %fusion.1, f32[2,32,32,512]{3,2,1,0:T(8,128)} %fusion.6, ...), kind=kOutput, calls=%fused_computation | convolution fusion | flops 1133510656 | bytes 38406144 | tf_op jit(solution)/shard_map/dot_general | solution.py:26
  61.3 3.3 %convolution_add_fusion = f32[2,32,32,512]{3,2,1,0:T(8,128)} fusion(f32[2,32,32,512]{3,2,1,0:T(8,128)S(1)} %copy-done.1, bf16[2,32,32,512]{3,2,1,0:T(8,128)(2,1)S(1)} %multiply_convert_fusion, bf16[3,4,512,512]{3,2,1,0:T(8,128)(2,1)S(1)} %bitcast.202), kind=kOutput, calls=%fused_computation.11 | convolution fusion | flops 1074790400 | bytes 11010048 | tf_op jit(solution)/shard_map/dot_general | solution.py:26
  64.6 5.2 %reshape.439 = f32[2,8,4,8,4,512]{5,4,3,2,1,0:T(4,128)} reshape(f32[2,32,32,512]{3,2,1,0:T(8,128)} %convolution_add_fusion) | data formatting | bytes 8388608 | tf_op jit(solution)/shard_map/reshape | solution.py:71
  69.7 3.6 %reduce_sum.18 = f32[2,8,8,512]{3,2,1,0:T(8,128)S(1)} reduce(f32[2,8,4,8,4,512]{5,4,3,2,1,0:T(4,128)} %reshape.439, f32[]{:T(128)} %constant.90.clone.1), dimensions={2,4}, to_apply=%region_0.1 | reduce | flops 983040 | bytes 4456452 | tf_op jit(solution)/shard_map/reduce_sum | solution.py:72
  73.3 1.3 multiply_add_fusion.1
  76.0 2.8 %collective-permute-start.4 = (bf16[2,1,8,512]{3,2,1,0:T(8,128)(2,1)S(1)}, bf16[2,1,8,512]{3,2,1,0:T(8,128)(2,1)S(1)}, u32[]{:S(2)}, u32[]{:S(2)}) collective-permute-start(bf16[2,1,8,512]{3,2,1,0:T(8,128)(2,1)S(1)} %get-tuple-element.20), channel_id=1, source_target_pairs={{0,16},{16,32},{32,48},{48,64},{64,80},{80,96},{96,112},{112,128},... | collective-permute-start | bytes 49160 | tf_op jit(solution)/shard_map/ppermute | solution.py:15
  80.2 5.6 %collective-permute-done.5 = bf16[2,1,8,512]{3,2,1,0:T(8,128)(2,1)S(1)} collective-permute-done((bf16[2,1,8,512]{3,2,1,0:T(8,128)(2,1)S(1)}, bf16[2,1,8,512]{3,2,1,0:T(8,128)(2,1)S(1)}, u32[]{:S(2)}, u32[]{:S(2)}) %collective-permute-start.5) | collective-permute-done | bytes 16416 | tf_op jit(solution)/shard_map/ppermute | solution.py:18
  85.9 2.9 %collective-permute-start.7 = (bf16[2,10,1,512]{3,2,1,0:T(2,128)(2,1)S(1)}, bf16[2,10,1,512]{3,2,1,0:T(2,128)(2,1)S(1)}, u32[]{:S(2)}, u32[]{:S(2)}) collective-permute-start(bf16[2,10,1,512]{3,2,1,0:T(2,128)(2,1)S(1)} %get-tuple-element.10), channel_id=1, source_target_pairs={{1,0},{2,1},{3,2},{4,3},{5,4},{6,5},{7,6},{8,7},{9,8},{10,9},{11,1... | collective-permute-start | bytes 61448 | tf_op jit(solution)/shard_map/ppermute | solution.py:18
  95.5 1.3 fusion.54
  98.1 2.0 %convolution_add_fusion.1 = f32[2,8,8,512]{3,2,1,0:T(8,128)S(1)} fusion(f32[2,8,8,512]{3,2,1,0:T(8,128)S(1)} %multiply_add_fusion.1, bf16[3,4,512,512]{3,2,1,0:T(8,128)(2,1)} %param.11, f32[2,8,8,512]{3,2,1,0:T(8,128)S(1)} %fusion.50, f32[2,8,8,512]{3,2,1,0:T(8,128)S(1)} %fusion.52, f32[2,8,8,512]{3,2,1,0:T(8,128)S(1)} %fusion.54, ...), kind=kOutput, calls=%fused_computation.23 | convolution fusion | flops 137887744 | bytes 3804672 | tf_op jit(solution)/shard_map/dot_general | solution.py:26
  102.9 2.0 %collective-permute-start.9 = (bf16[2,1,2,512]{3,2,1,0:T(2,128)(2,1)S(1)}, bf16[2,1,2,512]{3,2,1,0:T(2,128)(2,1)S(1)}, u32[]{:S(2)}, u32[]{:S(2)}) collective-permute-start(bf16[2,1,2,512]{3,2,1,0:T(2,128)(2,1)S(1)} %get-tuple-element.30), channel_id=1, source_target_pairs={{16,0},{32,16},{48,32},{64,48},{80,64},{96,80},{112,96},{128,112},... | collective-permute-start | bytes 12296 | tf_op jit(solution)/shard_map/ppermute | solution.py:18
  106.5 3.4 %collective-permute-done.9 = bf16[2,1,2,512]{3,2,1,0:T(2,128)(2,1)S(1)} collective-permute-done((bf16[2,1,2,512]{3,2,1,0:T(2,128)(2,1)S(1)}, bf16[2,1,2,512]{3,2,1,0:T(2,128)(2,1)S(1)}, u32[]{:S(2)}, u32[]{:S(2)}) %collective-permute-start.9) | collective-permute-done | bytes 4128 | tf_op jit(solution)/shard_map/ppermute | solution.py:18
  110.0 2.9 %collective-permute-start.11 = (bf16[2,4,1,512]{3,2,1,0:T(2,128)(2,1)S(1)}, bf16[2,4,1,512]{3,2,1,0:T(2,128)(2,1)S(1)}, u32[]{:S(2)}, u32[]{:S(2)}) collective-permute-start(bf16[2,4,1,512]{3,2,1,0:T(2,128)(2,1)S(1)} %get-tuple-element.27), channel_id=1, source_target_pairs={{1,0},{2,1},{3,2},{4,3},{5,4},{6,5},{7,6},{8,7},{9,8},{10,9},{11,1... | collective-permute-start | bytes 24584 | tf_op jit(solution)/shard_map/ppermute | solution.py:18
  121.9 1.3 multiply_convert_fusion.38
  123.2 1.6 %divide_multiply_fusion.1 = f32[2,2,2,512]{3,2,1,0:T(2,128)S(1)} fusion(bf16[4,512,512]{2,1,0:T(8,128)(2,1)} %param.12, f32[2,2,2,512]{3,2,1,0:T(2,128)S(1)} %fusion.198, bf16[2,2,2,512]{3,2,1,0:T(2,128)(2,1)S(1)} %multiply_convert_fusion.38, bf16[3,4,512,512]{3,2,1,0:T(8,128)(2,1)} %param.11), kind=kOutput, calls=%fused_computation.226 | convolution fusion | flops 8413184 | bytes 1089536 | tf_op jit(solution)/shard_map/dot_general | solution.py:26
  125.0 1.3 divide_multiply_fusion
  126.5 2.7 %broadcast_in_dim.11 = f32[2,32,8,4,512]{4,3,2,1,0:T(4,128)} broadcast(f32[2,32,8,512]{3,2,1,0:T(8,128)S(1)} %bitcast.200), dimensions={0,1,2,4} | broadcast | bytes 5242880 | tf_op jit(solution)/shard_map/broadcast_in_dim | solution.py:76
  129.2 5.4 %reshape.444 = f32[2,32,32,512]{3,2,1,0:T(8,128)} reshape(f32[2,32,8,4,512]{4,3,2,1,0:T(4,128)} %broadcast_in_dim.11) | data formatting | bytes 8388608 | tf_op jit(solution)/shard_map/reshape | solution.py:76
  134.6 6.9 %add.736 = f32[2,32,32,512]{3,2,1,0:T(8,128)} add(f32[2,32,32,512]{3,2,1,0:T(8,128)} %convolution_add_fusion, f32[2,32,32,512]{3,2,1,0:T(8,128)} %reshape.444) | non-fusion elementwise | flops 1048576 | bytes 12582912 | tf_op jit(solution)/shard_map/add | solution.py:119
  (76 shorter events, 24.9 us)
Async XLA Ops:
  0.6 5.8 %copy-start = (f32[2,32,32,512]{3,2,1,0:T(8,128)S(1)}, f32[2,32,32,512]{3,2,1,0:T(8,128)}, u32[]{:S(2)}) copy-start(f32[2,32,32,512]{3,2,1,0:T(8,128)} %param.7) | copy-start | bytes 12582916
  4.4 6.6 %collective-permute-start = (bf16[2,1,32,512]{3,2,1,0:T(8,128)(2,1)S(1)}, bf16[2,1,32,512]{3,2,1,0:T(8,128)(2,1)S(1)}, u32[]{:S(2)}, u32[]{:S(2)}) collective-permute-start(bf16[2,1,32,512]{3,2,1,0:T(8,128)(2,1)S(1)} %get-tuple-element.6), channel_id=1, source_target_pairs={{0,16},{16,32},{32,48},{48,64},{64,80},{80,96},{96,112},{112,128},... | collective-permute-start | bytes 196616 | tf_op jit(solution)/shard_map/ppermute | solution.py:15
  6.3 4.6 %copy-start.5 = (f32[3,512]{1,0:T(4,128)S(1)}, f32[3,512]{1,0:T(4,128)}, u32[]{:S(2)}) copy-start(f32[3,512]{1,0:T(4,128)} %param.13) | copy-start | bytes 18436
  6.3 4.6 %copy-start.4 = (s32[8,32,32]{2,1,0:T(8,128)S(1)}, s32[8,32,32]{2,1,0:T(8,128)}, u32[]{:S(2)}) copy-start(s32[8,32,32]{2,1,0:T(8,128)} %param.10) | copy-start | bytes 98308
  6.3 7.6 %collective-permute-start.1 = (bf16[2,1,32,512]{3,2,1,0:T(8,128)(2,1)S(1)}, bf16[2,1,32,512]{3,2,1,0:T(8,128)(2,1)S(1)}, u32[]{:S(2)}, u32[]{:S(2)}) collective-permute-start(bf16[2,1,32,512]{3,2,1,0:T(8,128)(2,1)S(1)} %get-tuple-element.7), channel_id=1, source_target_pairs={{16,0},{32,16},{48,32},{64,48},{80,64},{96,80},{112,96},{128,112},... | collective-permute-start | bytes 196616 | tf_op jit(solution)/shard_map/ppermute | solution.py:18
  13.9 9.0 %slice-start = ((s8[6291456]{0:T(1024)(128)(4,1)}), s8[4194304]{0:T(1024)(128)(4,1)S(1)}, s32[]{:S(2)}) async-start(s8[6291456]{0:T(1024)(128)(4,1)} %bitcast.201), calls=%async_computation | async-start | bytes 8388608
  14.1 12.3 %collective-permute-start.2 = (bf16[2,34,1,512]{3,2,1,0:T(2,128)(2,1)S(1)}, bf16[2,34,1,512]{3,2,1,0:T(2,128)(2,1)S(1)}, u32[]{:S(2)}, u32[]{:S(2)}) collective-permute-start(bf16[2,34,1,512]{3,2,1,0:T(2,128)(2,1)S(1)} %get-tuple-element.5), channel_id=1, source_target_pairs={{0,1},{1,2},{2,3},{3,4},{4,5},{5,6},{6,7},{7,8},{8,9},{9,10},{10,1... | collective-permute-start | bytes 208904 | tf_op jit(solution)/shard_map/ppermute | solution.py:15
  14.1 12.3 %collective-permute-start.3 = (bf16[2,34,1,512]{3,2,1,0:T(2,128)(2,1)S(1)}, bf16[2,34,1,512]{3,2,1,0:T(2,128)(2,1)S(1)}, u32[]{:S(2)}, u32[]{:S(2)}) collective-permute-start(bf16[2,34,1,512]{3,2,1,0:T(2,128)(2,1)S(1)} %get-tuple-element.4), channel_id=1, source_target_pairs={{1,0},{2,1},{3,2},{4,3},{5,4},{6,5},{7,6},{8,7},{9,8},{10,9},{11,1... | collective-permute-start | bytes 208904 | tf_op jit(solution)/shard_map/ppermute | solution.py:18
  17.1 5.9 %copy-start.2 = (f32[2,32,32,512]{3,2,1,0:T(8,128)S(1)}, f32[2,32,32,512]{3,2,1,0:T(8,128)}, u32[]{:S(2)}) copy-start(f32[2,32,32,512]{3,2,1,0:T(8,128)} %fusion.11) | copy-start | bytes 12582916
  17.1 5.9 %slice-start.1 = ((s8[6291456]{0:T(1024)(128)(4,1)}), s8[2097152]{0:T(1024)(128)(4,1)S(1)}, s32[]{:S(2)}) async-start(s8[6291456]{0:T(1024)(128)(4,1)} %bitcast.201), calls=%async_computation.1 | async-start | bytes 4194304
  45.7 15.6 %copy-start.1 = (f32[2,32,32,512]{3,2,1,0:T(8,128)S(1)}, f32[2,32,32,512]{3,2,1,0:T(8,128)}, u32[]{:S(2)}) copy-start(f32[2,32,32,512]{3,2,1,0:T(8,128)} %param.7) | copy-start | bytes 12582916
  61.3 3.3 %copy-start.3 = (bf16[2,32,32,512]{3,2,1,0:T(8,128)(2,1)}, bf16[2,32,32,512]{3,2,1,0:T(8,128)(2,1)S(1)}, u32[]{:S(2)}) copy-start(bf16[2,32,32,512]{3,2,1,0:T(8,128)(2,1)S(1)} %multiply_convert_fusion) | copy-start | bytes 6291460
  69.7 3.6 %copy-start.6 = (f32[2,8,8,512]{3,2,1,0:T(8,128)S(1)}, f32[2,8,8,512]{3,2,1,0:T(8,128)}, u32[]{:S(2)}) copy-start(f32[2,8,8,512]{3,2,1,0:T(8,128)} %param.8) | copy-start | bytes 786436
  76.0 4.2 %collective-permute-start.4 = (bf16[2,1,8,512]{3,2,1,0:T(8,128)(2,1)S(1)}, bf16[2,1,8,512]{3,2,1,0:T(8,128)(2,1)S(1)}, u32[]{:S(2)}, u32[]{:S(2)}) collective-permute-start(bf16[2,1,8,512]{3,2,1,0:T(8,128)(2,1)S(1)} %get-tuple-element.20), channel_id=1, source_target_pairs={{0,16},{16,32},{32,48},{48,64},{64,80},{80,96},{96,112},{112,128},... | collective-permute-start | bytes 49160 | tf_op jit(solution)/shard_map/ppermute | solution.py:15
  78.7 7.1 %collective-permute-start.5 = (bf16[2,1,8,512]{3,2,1,0:T(8,128)(2,1)S(1)}, bf16[2,1,8,512]{3,2,1,0:T(8,128)(2,1)S(1)}, u32[]{:S(2)}, u32[]{:S(2)}) collective-permute-start(bf16[2,1,8,512]{3,2,1,0:T(8,128)(2,1)S(1)} %get-tuple-element.21), channel_id=1, source_target_pairs={{16,0},{32,16},{48,32},{64,48},{80,64},{96,80},{112,96},{128,112},... | collective-permute-start | bytes 49160 | tf_op jit(solution)/shard_map/ppermute | solution.py:18
  85.8 5.6 %collective-permute-start.6 = (bf16[2,10,1,512]{3,2,1,0:T(2,128)(2,1)S(1)}, bf16[2,10,1,512]{3,2,1,0:T(2,128)(2,1)S(1)}, u32[]{:S(2)}, u32[]{:S(2)}) collective-permute-start(bf16[2,10,1,512]{3,2,1,0:T(2,128)(2,1)S(1)} %get-tuple-element.11), channel_id=1, source_target_pairs={{0,1},{1,2},{2,3},{3,4},{4,5},{5,6},{6,7},{7,8},{8,9},{9,10},{10,1... | collective-permute-start | bytes 61448 | tf_op jit(solution)/shard_map/ppermute | solution.py:15
  85.9 5.5 %collective-permute-start.7 = (bf16[2,10,1,512]{3,2,1,0:T(2,128)(2,1)S(1)}, bf16[2,10,1,512]{3,2,1,0:T(2,128)(2,1)S(1)}, u32[]{:S(2)}, u32[]{:S(2)}) collective-permute-start(bf16[2,10,1,512]{3,2,1,0:T(2,128)(2,1)S(1)} %get-tuple-element.10), channel_id=1, source_target_pairs={{1,0},{2,1},{3,2},{4,3},{5,4},{6,5},{7,6},{8,7},{9,8},{10,9},{11,1... | collective-permute-start | bytes 61448 | tf_op jit(solution)/shard_map/ppermute | solution.py:18
  98.1 2.2 %copy-start.7 = (f32[2,2,2,512]{3,2,1,0:T(2,128)S(1)}, f32[2,2,2,512]{3,2,1,0:T(2,128)}, u32[]{:S(2)}) copy-start(f32[2,2,2,512]{3,2,1,0:T(2,128)} %param.9) | copy-start | bytes 49156
  102.8 3.7 %collective-permute-start.8 = (bf16[2,1,2,512]{3,2,1,0:T(2,128)(2,1)S(1)}, bf16[2,1,2,512]{3,2,1,0:T(2,128)(2,1)S(1)}, u32[]{:S(2)}, u32[]{:S(2)}) collective-permute-start(bf16[2,1,2,512]{3,2,1,0:T(2,128)(2,1)S(1)} %get-tuple-element.29), channel_id=1, source_target_pairs={{0,16},{16,32},{32,48},{48,64},{64,80},{80,96},{96,112},{112,128},... | collective-permute-start | bytes 12296 | tf_op jit(solution)/shard_map/ppermute | solution.py:15
  102.9 7.0 %collective-permute-start.9 = (bf16[2,1,2,512]{3,2,1,0:T(2,128)(2,1)S(1)}, bf16[2,1,2,512]{3,2,1,0:T(2,128)(2,1)S(1)}, u32[]{:S(2)}, u32[]{:S(2)}) collective-permute-start(bf16[2,1,2,512]{3,2,1,0:T(2,128)(2,1)S(1)} %get-tuple-element.30), channel_id=1, source_target_pairs={{16,0},{32,16},{48,32},{64,48},{80,64},{96,80},{112,96},{128,112},... | collective-permute-start | bytes 12296 | tf_op jit(solution)/shard_map/ppermute | solution.py:18
  110.0 5.5 %collective-permute-start.10 = (bf16[2,4,1,512]{3,2,1,0:T(2,128)(2,1)S(1)}, bf16[2,4,1,512]{3,2,1,0:T(2,128)(2,1)S(1)}, u32[]{:S(2)}, u32[]{:S(2)}) collective-permute-start(bf16[2,4,1,512]{3,2,1,0:T(2,128)(2,1)S(1)} %get-tuple-element.28), channel_id=1, source_target_pairs={{0,1},{1,2},{2,3},{3,4},{4,5},{5,6},{6,7},{7,8},{8,9},{9,10},{10,1... | collective-permute-start | bytes 24584 | tf_op jit(solution)/shard_map/ppermute | solution.py:15
  110.0 8.0 %collective-permute-start.11 = (bf16[2,4,1,512]{3,2,1,0:T(2,128)(2,1)S(1)}, bf16[2,4,1,512]{3,2,1,0:T(2,128)(2,1)S(1)}, u32[]{:S(2)}, u32[]{:S(2)}) collective-permute-start(bf16[2,4,1,512]{3,2,1,0:T(2,128)(2,1)S(1)} %get-tuple-element.27), channel_id=1, source_target_pairs={{1,0},{2,1},{3,2},{4,3},{5,4},{6,5},{7,6},{8,7},{9,8},{10,9},{11,1... | collective-permute-start | bytes 24584 | tf_op jit(solution)/shard_map/ppermute | solution.py:18
where the time goes:
time: 143 us; the launch traced here: 142 us
  matrix products  85.7 us (60%)
  starting transfers between devices  15.8 us (11%)
  local copies, waits for them, and re-layouts  13.7 us (10%)
  other arithmetic  12.7 us (9%)
  waiting for transfers between devices  12.4 us (9%)
    dot_general x35, matrix products, project(): result = jnp.dot(flat, matrix, preferred_element_type=jnp.float32)  85.7 us
    ppermute x6, waiting for transfers between devices, padded_2(): lax.ppermute(lax.slice_in_dim(block, 0, width, axis=dim), axis, backward)  11.9 us
    ppermute x6, starting transfers between devices, padded_2(): lax.ppermute(lax.slice_in_dim(block, 0, width, axis=dim), axis, backward)  11 us
    add x1, other arithmetic, local(): return (fine_one + expand(spread), fine_average)  6.92 us
    reshape x2, local copies, waits for them, and re-layouts, expand(): return jnp.repeat(jnp.repeat(values, 4, axis=1), 4, axis=2)  5.48 us
    reshape x2, local copies, waits for them, and re-layouts, pooled(): blocks = states.reshape(samples, rows // 4, 4, cols // 4, 4, features)  5.22 us
    ppermute x6, starting transfers between devices, padded_2(): lax.ppermute(lax.slice_in_dim(block, block.shape[dim] - width, None, axis...  4.82 us
    reduce_sum x2, other arithmetic, pooled(): return jnp.mean(blocks, axis=(2, 4)).astype(jnp.bfloat16)  3.66 us
  transfers between devices with their start and end apart: 12, of which 5 were waited for; matrix products, arithmetic and copies ran while one was open for 17% of the time, Pallas kernels for 0%

commit v1 on v0

v1 whole, which is shorter than its diff:
```python
import functools
import jax
import jax.numpy as jnp
import numpy as np
from jax import lax
from jax.experimental import pallas as pl
from jax.experimental.pallas import tpu as pltpu
from jax.sharding import PartitionSpec as P

D = 512
BF = jnp.bfloat16
F32 = jnp.float32
OFFS = ((-1, -1), (-1, 0), (-1, 1), (0, -1), (0, 1), (1, -1), (1, 0), (1, 1))
PRB = 8
RB = 8


def mm(a, b):
    return jnp.dot(a, b, preferred_element_type=F32)


def gate(half):
    return half + half * jnp.tanh(half)


def pool_rows(x, g, tmp):
    tall = (x[4 * g] + x[4 * g + 1]) + (x[4 * g + 2] + x[4 * g + 3])
    parts = []
    for lane in range(4):
        tmp[g, lane] = tall[:, lane * 128:(lane + 1) * 128]
        part = tmp[g, lane, pl.ds(0, 8, stride=4), :]
        for t in range(1, 4):
            part = part + tmp[g, lane, pl.ds(t, 8, stride=4), :]
        parts.append(part)
    return jnp.concatenate(parts, axis=1)


def prep_kernel(s_ref, w_ref, c_ref, r_out, t_out, ps_out, tmp):
    x = s_ref[0]
    op = x.reshape(PRB * 32, D).astype(BF)
    r = mm(op, w_ref[0, 0])
    r_out[0] = (0.5 * (r + c_ref[0:1, :])).astype(BF).reshape(PRB, 32, D)
    t_out[0] = (0.5 * mm(op, w_ref[0, 1])).astype(BF).reshape(PRB, 32, D)
    for g in range(PRB // 4):
        ps_out[0, g] = pool_rows(x, g, tmp)


def prep(fine, pw, pb):
    return pl.pallas_call(
        prep_kernel,
        name="prep",
        grid=(2, 32 // PRB),
        in_specs=[
            pl.BlockSpec((1, PRB, 32, D), lambda b, i: (b, i, 0, 0)),
            pl.BlockSpec((1, 2, D, D), lambda b, i: (0, 0, 0, 0)),
            pl.BlockSpec((3, D), lambda b, i: (0, 0)),
        ],
        out_specs=[
            pl.BlockSpec((1, PRB, 32, D), lambda b, i: (b, i, 0, 0)),
            pl.BlockSpec((1, PRB, 32, D), lambda b, i: (b, i, 0, 0)),
            pl.BlockSpec((1, PRB // 4, 8, D), lambda b, i: (b, i, 0, 0)),
        ],
        out_shape=[
            jax.ShapeDtypeStruct((2, 32, 32, D), BF),
            jax.ShapeDtypeStruct((2, 32, 32, D), BF),
            jax.ShapeDtypeStruct((2, 8, 8, D), F32),
        ],
        scratch_shapes=[pltpu.VMEM((8, 4, 32, 128), F32)],
        compiler_params=pltpu.CompilerParams(vmem_limit_bytes=32 << 20),
        cost_estimate=pl.CostEstimate(flops=2 * 2 * 2048 * D * D, bytes_accessed=10 << 20, transcendentals=0),
    )(fine, pw, pb)


def stack_rows(parts, shape):
    rows = lax.broadcasted_iota(jnp.int32, shape, 0)
    out = jnp.zeros(shape, F32)
    for i, part in enumerate(parts):
        out = jnp.where(rows == i, jnp.broadcast_to(part.astype(F32), shape), out)
    return out


def edge_kernel(r_ref, t_ref, up_ref, down_ref, left_ref, right_ref, ul_ref, ur_ref, dl_ref, dr_ref,
                mask_ref, w_ref, b0_ref, ps_ref, mid_ref, pick_ref,
                avg_out, mz_out, *rest):
    rim_outs, (sh, hs, tmp, pa) = rest[:8], rest[8:]
    b = pl.program_id(0)
    blk = pl.program_id(1)

    @pl.when(blk == 0)
    def _():
        rim = jnp.concatenate([up_ref[0], down_ref[0], left_ref[0], right_ref[0]], axis=0)
        hs[0:128, :] = (0.5 * mm(rim, w_ref[0, 1])).astype(BF).astype(F32)
        corners = stack_rows([ul_ref[0], ur_ref[0], dl_ref[0], dr_ref[0]], (8, D)).astype(BF)
        hs[128:136, :] = (0.5 * mm(corners, w_ref[0, 1])).astype(BF).astype(F32)
        rows = lax.broadcasted_iota(jnp.int32, (32, D), 0)

        def put(i, x, left, right):
            sh[1, i] = x.astype(BF)
            sh[0, i] = jnp.where(rows == 0, jnp.broadcast_to(left, (32, D)), pltpu.roll(x, 1, 0)).astype(BF)
            sh[2, i] = jnp.where(rows == 31, jnp.broadcast_to(right, (32, D)), pltpu.roll(x, 31, 0)).astype(BF)

        put(0, hs[0:32, :], hs[128:129, :], hs[129:130, :])
        put(33, hs[32:64, :], hs[130:131, :], hs[131:132, :])

        @pl.loop(0, 32)
        def _(i):
            put(i + 1, t_ref[0, i].astype(F32), hs[pl.ds(64 + i, 1), :], hs[pl.ds(96 + i, 1), :])

    row0 = blk * RB
    rv = r_ref[0].reshape(RB * 32, D)
    acc = None
    for k, (p, q) in enumerate(OFFS):
        sv = sh[q + 1, pl.ds(row0 + 1 + p, RB)].reshape(RB * 32, D)
        x = rv + sv
        m = mask_ref[k].reshape(RB * 32, 128)
        h = gate(x) * jnp.concatenate([m] * 4, axis=1)
        g = 0.5 * mm(h, w_ref[0, 2])
        msg = gate(g)
        acc = msg if acc is None else acc + msg
    avg = (acc * 0.125).astype(BF)
    av = avg.reshape(RB, 32, D)
    avg_out[0] = av
    af = av.astype(F32)
    for g in range(RB // 4):
        pa[b, blk * (RB // 4) + g] = pool_rows(af, g, tmp)

    @pl.when((b == 1) & (blk == 32 // RB - 1))
    def _():
        mean_avg = (pa[...].reshape(128, D) * 0.0625).astype(BF)
        pooled = (ps_ref[...].reshape(128, D) * 0.0625 + mm(mean_avg, w_ref[0, 3])).astype(BF)
        mz = mid_ref[...].reshape(128, D) + gate(0.5 * mm(pooled, b0_ref[0]))
        mz_out[...] = mz
        rims = mm(pick_ref[...], mz.astype(BF)).astype(BF)
        for d in range(8):
            rim_outs[d][...] = rims[16 * d:16 * d + 16]


def edge(r, t, rim, mask, pw, bw, ps, mid, pick):
    whole = lambda *shape: pl.BlockSpec(shape, lambda b, i: (0,) * len(shape))
    return pl.pallas_call(
        edge_kernel,
        name="edge",
        grid=(2, 32 // RB),
        in_specs=[
            pl.BlockSpec((1, RB, 32, D), lambda b, i: (b, i, 0, 0)),
            pl.BlockSpec((1, 32, 32, D), lambda b, i: (b, 0, 0, 0)),
        ]
        + [pl.BlockSpec((1, 32, D), lambda b, i: (b, 0, 0))] * 4
        + [pl.BlockSpec((1, 1, D), lambda b, i: (b, 0, 0))] * 4
        + [
            pl.BlockSpec((8, RB, 32, 128), lambda b, i: (0, i, 0, 0)),
            whole(1, 4, D, D),
            whole(1, D, D),
            whole(2, 8, 8, D),
            whole(2, 8, 8, D),
            whole(128, 128),
        ],
        out_specs=[
            pl.BlockSpec((1, RB, 32, D), lambda b, i: (b, i, 0, 0)),
            whole(128, D),
        ]
        + [whole(16, D)] * 8,
        out_shape=[
            jax.ShapeDtypeStruct((2, 32, 32, D), BF),
            jax.ShapeDtypeStruct((128, D), F32),
        ]
        + [jax.ShapeDtypeStruct((16, D), BF)] * 8,
        scratch_shapes=[
            pltpu.VMEM((3, 34, 32, D), BF),
            pltpu.VMEM((136, D), F32),
            pltpu.VMEM((8, 4, 32, 128), F32),
            pltpu.VMEM((2, 8, 8, D), F32),
        ],
        compiler_params=pltpu.CompilerParams(vmem_limit_bytes=48 << 20),
        cost_estimate=pl.CostEstimate(flops=2 * 8 * 2048 * D * D, bytes_accessed=16 << 20, transcendentals=16 << 20),
    )(r, t, *rim, mask, pw, bw, ps, mid, pick)


def middle_kernel(inner_ref, mz_ref, *refs):
    rim_refs = refs[:8]
    w_ref, c_ref, b1_ref, coarse_ref, gather_ref, mean_ref, mo_out, cz_out, czb_out = refs[8:]
    mz = mz_ref[...]
    own = mz.astype(BF)
    recv = 0.5 * (mm(own, w_ref[0, 0]) + c_ref[1:2, :])
    states = jnp.concatenate([own] + [ref[...] for ref in rim_refs], axis=0)
    send = (0.5 * mm(states, w_ref[0, 1])).astype(BF)
    near = mm(gather_ref[...], send)
    hidden = gate(near.reshape(8, 128, D) + recv[None]).astype(BF).reshape(1024, D)
    msg = gate(0.5 * mm(hidden, w_ref[0, 2])).reshape(8, 128, D)
    lat = (lax.broadcasted_iota(jnp.int32, (128, D), 0) // 8) % 8
    up = jnp.where(lat == 0, inner_ref[0], 1.0)
    down = jnp.where(lat == 7, inner_ref[1], 1.0)
    total = up * (msg[0] + msg[1] + msg[2]) + (msg[3] + msg[4]) + down * (msg[5] + msg[6] + msg[7])
    avg = (0.125 * total).astype(BF)
    mo = mz + mm(avg, w_ref[0, 3])
    mo_out[...] = mo
    pooled = jnp.dot(mean_ref[...], mo, preferred_element_type=F32, precision=lax.Precision.HIGHEST)
    cz = coarse_ref[...] + gate(0.5 * mm(pooled.astype(BF), b1_ref[0]))
    cz_out[...] = cz
    czb_out[...] = cz.astype(BF)


VM = pl.BlockSpec(memory_space=pltpu.VMEM)


def level_block(level):
    return pl.BlockSpec((1, 4, D, D), lambda i: (level, 0, 0, 0))


def bridge_block(index):
    return pl.BlockSpec((1, D, D), lambda i: (index, 0, 0))


def full(*shape):
    return pl.BlockSpec(shape, lambda i: (0,) * len(shape))


def middle(inner, mz, rim, pw, pb, bw, coarse, gather, mean):
    return pl.pallas_call(
        middle_kernel,
        name="middle",
        grid=(1,),
        in_specs=[pl.BlockSpec(memory_space=pltpu.SMEM), full(128, D)]
        + [full(16, D)] * 8
        + [level_block(1), full(3, D), bridge_block(1), full(8, D), full(1024, 256), full(8, 128)],
        out_specs=[full(128, D), full(8, D), full(8, D)],
        out_shape=[
            jax.ShapeDtypeStruct((128, D), F32),
            jax.ShapeDtypeStruct((8, D), F32),
            jax.ShapeDtypeStruct((8, D), BF),
        ],
        compiler_params=pltpu.CompilerParams(vmem_limit_bytes=24 << 20),
        cost_estimate=pl.CostEstimate(flops=2 * 12 * 128 * D * D, bytes_accessed=5 << 20, transcendentals=1 << 20),
    )(inner, mz, *rim, pw, pb, bw, coarse, gather, mean)


def coarse_kernel(inner_ref, cz_ref, *refs):
    rim_refs = refs[:8]
    w_ref, c_ref, b2_ref, b3_ref, mo_ref, gather_ref, lift_ref, spread_out = refs[8:]
    cz = cz_ref[...]
    own = cz.astype(BF)
    recv = 0.5 * (mm(own, w_ref[0, 0]) + c_ref[2:3, :])
    pieces = [cz] + [ref[...].astype(F32) for ref in rim_refs] + [jnp.zeros((56, D), F32)]
    send = (0.5 * mm(jnp.concatenate(pieces, axis=0).astype(BF), w_ref[0, 1])).astype(BF)
    near = mm(gather_ref[...], send)
    hidden = gate(near.reshape(8, 8, D) + recv[None]).astype(BF).reshape(64, D)
    msg = gate(0.5 * mm(hidden, w_ref[0, 2])).reshape(8, 8, D)
    lat = (lax.broadcasted_iota(jnp.int32, (8, D), 0) // 2) % 2
    up = jnp.where(lat == 0, inner_ref[0], 1.0)
    down = jnp.where(lat == 1, inner_ref[1], 1.0)
    total = up * (msg[0] + msg[1] + msg[2]) + (msg[3] + msg[4]) + down * (msg[5] + msg[6] + msg[7])
    avg = (0.125 * total).astype(BF)
    co = cz + mm(avg, w_ref[0, 3])
    lifted = gate(0.5 * mm(co.astype(BF), b2_ref[0]))
    high = lifted.astype(BF).astype(F32)
    both = jnp.concatenate([high, lifted - high], axis=0).astype(BF)
    two = mo_ref[...] + mm(lift_ref[...], both)
    spread_out[...] = gate(0.5 * mm(two.astype(BF), b3_ref[0])).reshape(2, 8, 8, D)


def coarsest(inner, cz, rim, pw, pb, bw, mo, gather, lift):
    return pl.pallas_call(
        coarse_kernel,
        name="coarsest",
        grid=(1,),
        in_specs=[pl.BlockSpec(memory_space=pltpu.SMEM), full(8, D)]
        + [full(8, D)] * 8
        + [level_block(2), full(3, D), bridge_block(2), bridge_block(3), full(128, D), full(64, 128), full(128, 16)],
        out_specs=full(2, 8, 8, D),
        out_shape=jax.ShapeDtypeStruct((2, 8, 8, D), F32),
        compiler_params=pltpu.CompilerParams(vmem_limit_bytes=24 << 20),
        cost_estimate=pl.CostEstimate(flops=2 * 2 * 128 * D * D, bytes_accessed=4 << 20, transcendentals=1 << 18),
    )(inner, cz, *rim, pw, pb, bw, bw, mo, gather, lift)


FRB = 8


def finish_kernel(s_ref, avg_ref, w_ref, spread_ref, out_ref):
    one = mm(avg_ref[0].reshape(FRB * 32, D), w_ref[0, 0]).reshape(FRB, 32, D)
    first = lax.broadcasted_iota(jnp.int32, (8, D), 0) < 4
    for g in range(FRB // 4):
        parts = []
        for t in range(4):
            low = jnp.broadcast_to(spread_ref[0, g, 2 * t:2 * t + 1, :], (8, D))
            high = jnp.broadcast_to(spread_ref[0, g, 2 * t + 1:2 * t + 2, :], (8, D))
            parts.append(jnp.where(first, low, high))
        wide = jnp.concatenate(parts, axis=0)
        for i in range(4 * g, 4 * g + 4):
            out_ref[0, i] = s_ref[0, i] + one[i] + wide


def finish(fine, avg, pw, spread):
    block = pl.BlockSpec((1, FRB, 32, D), lambda b, i: (b, i, 0, 0))
    return pl.pallas_call(
        finish_kernel,
        name="finish",
        grid=(2, 32 // FRB),
        in_specs=[
            block,
            block,
            pl.BlockSpec((1, 1, D, D), lambda b, i: (0, 3, 0, 0)),
            pl.BlockSpec((1, FRB // 4, 8, D), lambda b, i: (b, i, 0, 0)),
        ],
        out_specs=block,
        out_shape=jax.ShapeDtypeStruct((2, 32, 32, D), F32),
        compiler_params=pltpu.CompilerParams(vmem_limit_bytes=24 << 20),
        cost_estimate=pl.CostEstimate(flops=2 * 2048 * D * D, bytes_accessed=10 << 20, transcendentals=0),
    )(fine, avg, pw, spread)


def place_middle():
    pick = np.zeros((128, 128), np.float32)
    for d, (p, q) in enumerate(OFFS):
        for b in range(2):
            rows = [0] if p < 0 else [7] if p > 0 else range(8)
            cols = [0] if q < 0 else [7] if q > 0 else range(8)
            for n, (i, j) in enumerate((i, j) for i in rows for j in cols):
                pick[16 * d + 8 * b + n, 64 * b + 8 * i + j] = 1
    gather = np.zeros((1024, 256), np.float32)
    for k, (p, q) in enumerate(OFFS):
        for b in range(2):
            for i in range(8):
                for j in range(8):
                    y, x = i + p, j + q
                    dy = (y > 7) - (y < 0)
                    dx = (x > 7) - (x < 0)
                    if (dy, dx) == (0, 0):
                        source = 64 * b + 8 * y + x
                    else:
                        n = 0 if dy and dx else x if dy else y
                        source = 128 + 16 * OFFS.index((dy, dx)) + 8 * b + n
                    gather[128 * k + 64 * b + 8 * i + j, source] = 1
    mean = np.zeros((8, 128), np.float32)
    for b in range(2):
        for i in range(8):
            for j in range(8):
                mean[4 * b + 2 * (i // 4) + j // 4, 64 * b + 8 * i + j] = 1 / 16
    return pick, gather, mean


def place_coarse():
    gather = np.zeros((64, 128), np.float32)
    for k, (p, q) in enumerate(OFFS):
        for b in range(2):
            for i in range(2):
                for j in range(2):
                    y, x = i + p, j + q
                    dy = (y > 1) - (y < 0)
                    dx = (x > 1) - (x < 0)
                    base = 0 if (dy, dx) == (0, 0) else 8 + 8 * OFFS.index((dy, dx))
                    gather[8 * k + 4 * b + 2 * i + j, base + 4 * b + 2 * (y % 2) + x % 2] = 1
    lift = np.zeros((128, 16), np.float32)
    for b in range(2):
        for i in range(8):
            for j in range(8):
                source = 4 * b + 2 * (i // 4) + j // 4
                lift[64 * b + 8 * i + j, source] = 1
                lift[64 * b + 8 * i + j, 8 + source] = 1
    return gather, lift


def exchange(pieces):
    rows, cols = lax.axis_size("lat"), lax.axis_size("lon")
    out = []
    for d, (p, q) in enumerate(OFFS):
        perm = []
        for y in range(rows):
            for x in range(cols):
                source = y + p
                if 0 <= source < rows:
                    perm.append((source * cols + (x + q) % cols, y * cols + x))
        out.append(lax.ppermute(pieces[7 - d], ("lat", "lon"), perm))
    return out


def local(fine, mid, coarse, flags, pw, bw, pb):
    edge_of = {-1: slice(0, 1), 1: slice(-1, None), 0: slice(None)}
    pieces = []
    for p, q in OFFS:
        part = fine[:, edge_of[p], edge_of[q], :].astype(BF)
        pieces.append(part.reshape(2, -1, D))
    rim = exchange(pieces)
    lat = lax.axis_index("lat")
    rows = lax.axis_size("lat")
    inner = jnp.stack([lat > 0, lat < rows - 1]).astype(F32)
    index = jnp.arange(32)
    step = jnp.asarray([p for p, q in OFFS])[:, None]
    where = lat * 32 + index[None, :] + step
    live = flags.astype(BF) * ((where >= 0) & (where < rows * 32)).astype(BF)[:, :, None]
    mask = jnp.broadcast_to(live[..., None], (8, 32, 32, 128))
    pick, gather, mean = place_middle()
    gather_c, lift = place_coarse()
    r, t, ps = prep(fine, pw, pb)
    ul, up, ur, left, right, dl, down, dr = rim
    avg, mz, *send = edge(r, t, (up, down, left, right, ul, ur, dl, dr), mask, pw, bw, ps, mid, jnp.asarray(pick, BF))
    rim = exchange(send)
    mo, cz, czb = middle(inner, mz, rim, pw, pb, bw, coarse.reshape(8, D), jnp.asarray(gather, BF), jnp.asarray(mean, F32))
    rim = exchange([czb] * 8)
    spread = coarsest(inner, cz, rim, pw, pb, bw, mo, jnp.asarray(gather_c, BF), jnp.asarray(lift, BF))
    return finish(fine, avg, pw, spread), avg


def solution(mesh):
    node = P(None, "lat", "lon", None)
    return jax.shard_map(
        local,
        mesh=mesh,
        in_specs=(node, node, node, P(None, "lat", "lon"), P(), P(), P()),
        out_specs=(node, node),
        check_vma=False,
    )
```

time: 143 us -> 137 us (0.958)
  the two profiles are of different devices: /device:TPU:30 before, /device:TPU:111 now
where the time goes in v1:
time: 137 us
  starting transfers between devices  77.2 us (56%)
  Pallas kernels  33.7 us (25%)
  local copies, waits for them, and re-layouts  16.4 us (12%)
  waiting for transfers between devices  7.99 us (6%)
    ppermute x24, starting transfers between devices, exchange(): out.append(lax.ppermute(pieces[7 - d], ('lat', 'lon'), perm))  77.2 us
    pallas_call x1, Pallas kernels, edge(): pl.pallas_call(edge_kernel, name='edge', grid=(2, 32 // RB), in_specs=[pl...  20.9 us
    unnamed x37, local copies, waits for them, and re-layouts  13.9 us
    ppermute x24, waiting for transfers between devices, exchange(): out.append(lax.ppermute(pieces[7 - d], ('lat', 'lon'), perm))  7.99 us
    pallas_call x1, Pallas kernels, finish(): pl.pallas_call(finish_kernel, name='finish', grid=(2, 32 // FRB), in_spec...  4.69 us
    pallas_call x1, Pallas kernels, prep(): pl.pallas_call(prep_kernel, name='prep', grid=(2, 32 // PRB), in_specs=[p...  3.65 us
  transfers between devices with their start and end apart: 24, of which 3 were waited for; matrix products, arithmetic and copies ran while one was open for 0% of the time, Pallas kernels for 3%

profile of v1, /device:TPU:111, one launch (start us, length us, event | category | flops | bytes accessed | tf_op | source)
XLA Modules:
  0.0 136.7 jit_solution(16957764744034632994)
XLA Ops:
  0.7 4.5 %copy.64 = bf16[2,32,32,512]{3,1,0,2:T(8,128)(2,1)S(1)} copy(f32[2,32,32,512]{3,2,1,0:T(8,128)} %s_ref.3) | data formatting | bytes 6291456 | tf_op args[0]
  5.1 6.2 %collective-permute-start.4 = (bf16[2,1,512]{2,1,0:T(2,128)(2,1)S(1)}, bf16[2,1,512]{2,1,0:T(2,128)(2,1)S(1)}, u32[]{:S(2)}, u32[]{:S(2)}) collective-permute-start(bf16[2,1,512]{2,1,0:T(2,128)(2,1)S(1)} %get-tuple-element.37), channel_id=1, source_target_pairs={{15,16},{0,17},{1,18},{2,19},{3,20},{4,21},{5,22},{6,23},{7,24},{8... | collective-permute-start | bytes 6152 | tf_op jit(solution)/shard_map/ppermute | solution.py:373
  11.4 1.9 %collective-permute-start.5 = (bf16[2,1,512]{2,1,0:T(2,128)(2,1)S(1)}, bf16[2,1,512]{2,1,0:T(2,128)(2,1)S(1)}, u32[]{:S(2)}, u32[]{:S(2)}) collective-permute-start(bf16[2,1,512]{2,1,0:T(2,128)(2,1)S(1)} %get-tuple-element.36), channel_id=1, source_target_pairs={{1,16},{2,17},{3,18},{4,19},{5,20},{6,21},{7,22},{8,23},{9,24},{10... | collective-permute-start | bytes 6152 | tf_op jit(solution)/shard_map/ppermute | solution.py:373
  13.3 5.8 %collective-permute-start.6 = (bf16[2,1,512]{2,1,0:T(2,128)(2,1)S(1)}, bf16[2,1,512]{2,1,0:T(2,128)(2,1)S(1)}, u32[]{:S(2)}, u32[]{:S(2)}) collective-permute-start(bf16[2,1,512]{2,1,0:T(2,128)(2,1)S(1)} %get-tuple-element.35), channel_id=1, source_target_pairs={{31,0},{16,1},{17,2},{18,3},{19,4},{20,5},{21,6},{22,7},{23,8},{24... | collective-permute-start | bytes 6152 | tf_op jit(solution)/shard_map/ppermute | solution.py:373
  19.1 1.9 %collective-permute-start.7 = (bf16[2,1,512]{2,1,0:T(2,128)(2,1)S(1)}, bf16[2,1,512]{2,1,0:T(2,128)(2,1)S(1)}, u32[]{:S(2)}, u32[]{:S(2)}) collective-permute-start(bf16[2,1,512]{2,1,0:T(2,128)(2,1)S(1)} %get-tuple-element.34), channel_id=1, source_target_pairs={{17,0},{18,1},{19,2},{20,3},{21,4},{22,5},{23,6},{24,7},{25,8},{26... | collective-permute-start | bytes 6152 | tf_op jit(solution)/shard_map/ppermute | solution.py:373
  21.3 5.2 %collective-permute-start = (bf16[2,32,512]{2,1,0:T(8,128)(2,1)S(1)}, bf16[2,32,512]{2,1,0:T(8,128)(2,1)S(1)}, u32[]{:S(2)}, u32[]{:S(2)}) collective-permute-start(bf16[2,32,512]{2,1,0:T(8,128)(2,1)S(1)} %bitcast.22), channel_id=1, source_target_pairs={{0,16},{1,17},{2,18},{3,19},{4,20},{5,21},{6,22},{7,23},{8,24},{9,... | collective-permute-start | bytes 196616 | tf_op jit(solution)/shard_map/ppermute | solution.py:373
  26.8 1.9 %collective-permute-start.1 = (bf16[2,32,512]{2,1,0:T(8,128)(2,1)S(1)}, bf16[2,32,512]{2,1,0:T(8,128)(2,1)S(1)}, u32[]{:S(2)}, u32[]{:S(2)}) collective-permute-start(bf16[2,32,512]{2,1,0:T(8,128)(2,1)S(1)} %bitcast.23), channel_id=1, source_target_pairs={{16,0},{17,1},{18,2},{19,3},{20,4},{21,5},{22,6},{23,7},{24,8},{25... | collective-permute-start | bytes 196616 | tf_op jit(solution)/shard_map/ppermute | solution.py:373
  28.7 3.2 %collective-permute-start.2 = (bf16[2,32,512]{2,1,0:T(8,128)(2,1)S(1)}, bf16[2,32,512]{2,1,0:T(8,128)(2,1)S(1)}, u32[]{:S(2)}, u32[]{:S(2)}) collective-permute-start(bf16[2,32,512]{2,1,0:T(8,128)(2,1)S(1)} %get-tuple-element.39), channel_id=1, source_target_pairs={{15,0},{0,1},{1,2},{2,3},{3,4},{4,5},{5,6},{6,7},{7,8},{8,9},{9,10... | collective-permute-start | bytes 196616 | tf_op jit(solution)/shard_map/ppermute | solution.py:373
  31.9 2.8 %copy-done = bf16[3,4,512,512]{3,2,1,0:T(8,128)(2,1)S(1)} copy-done((bf16[3,4,512,512]{3,2,1,0:T(8,128)(2,1)S(1)}, bf16[3,4,512,512]{3,2,1,0:T(8,128)(2,1)}, u32[]{:S(2)}) %copy-start) | copy-done | bytes 6291480
  34.7 2.2 %copy-done.2 = f32[2,32,32,512]{3,2,1,0:T(8,128)S(1)} copy-done((f32[2,32,32,512]{3,2,1,0:T(8,128)S(1)}, f32[2,32,32,512]{3,2,1,0:T(8,128)}, u32[]{:S(2)}) %copy-start.2) | copy-done | bytes 4194328
  36.9 3.6 %prep.1 = (bf16[2,32,32,512]{3,2,1,0:T(8,128)(2,1)S(1)}, bf16[2,32,32,512]{3,2,1,0:T(8,128)(2,1)S(1)}, f32[2,8,8,512]{3,2,1,0:T(8,128)S(1)}) custom-call(f32[2,32,32,512]{3,2,1,0:T(8,128)S(1)} %copy-done.2, bf16[3,4,512,512]{3,2,1,0:T(8,128)(2,1)S(1)} %copy-done, f32[3,512]{1,0:T(4,128)S(1)} %copy-done.7), custom_call_target="tpu_custom_call" | custom-call | flops 2147483648 | bytes 10485760 | tf_op jit(solution)/shard_map/prep/pallas_call | solution.py:49
  40.6 2.2 %broadcast_in_dim.2.mask_ref = bf16[8,32,32,128]{3,2,1,0:T(8,128)(2,1)} broadcast(bf16[8,32,32]{2,1,0:T(8,128)(2,1)S(1)} %convert_multiply_fusion), dimensions={0,1,2} | broadcast | bytes 2113536 | tf_op jit(solution)/shard_map/broadcast_in_dim | solution.py:391
  42.9 20.9 %edge.1 = (bf16[2,32,32,512]{3,2,1,0:T(8,128)(2,1)}, f32[128,512]{1,0:T(8,128)S(1)}, bf16[16,512]{1,0:T(8,128)(2,1)S(1)}, bf16[16,512]{1,0:T(8,128)(2,1)S(1)}, b...) custom-call(bf16[2,32,32,512]{3,2,1,0:T(8,128)(2,1)S(1)} %get-tuple-, ...), custom_call_target="tpu_custom_call" | custom-call | flops 8589934592 | bytes 16777216 | tf_op jit(solution)/shard_map/edge/pallas_call | solution.py:140
  63.8 2.7 %collective-permute-start.10 = (bf16[16,512]{1,0:T(8,128)(2,1)S(1)}, bf16[16,512]{1,0:T(8,128)(2,1)S(1)}, u32[]{:S(2)}, u32[]{:S(2)}) collective-permute-start(bf16[16,512]{1,0:T(8,128)(2,1)S(1)} %get-tuple-element.25), channel_id=1, source_target_pairs={{1,16},{2,17},{3,18},{4,19},{5,20},{6,21},{7,22},{8,23},{9,24},{10... | collective-permute-start | bytes 49160 | tf_op jit(solution)/shard_map/ppermute | solution.py:373
  66.5 5.8 %collective-permute-start.11 = (bf16[16,512]{1,0:T(8,128)(2,1)S(1)}, bf16[16,512]{1,0:T(8,128)(2,1)S(1)}, u32[]{:S(2)}, u32[]{:S(2)}) collective-permute-start(bf16[16,512]{1,0:T(8,128)(2,1)S(1)} %get-tuple-element.26), channel_id=1, source_target_pairs={{15,0},{0,1},{1,2},{2,3},{3,4},{4,5},{5,6},{6,7},{7,8},{8,9},{9,10... | collective-permute-start | bytes 49160 | tf_op jit(solution)/shard_map/ppermute | solution.py:373
  72.2 2.2 %collective-permute-start.13 = (bf16[16,512]{1,0:T(8,128)(2,1)S(1)}, bf16[16,512]{1,0:T(8,128)(2,1)S(1)}, u32[]{:S(2)}, u32[]{:S(2)}) collective-permute-start(bf16[16,512]{1,0:T(8,128)(2,1)S(1)} %get-tuple-element.28), channel_id=1, source_target_pairs={{31,0},{16,1},{17,2},{18,3},{19,4},{20,5},{21,6},{22,7},{23,8},{24... | collective-permute-start | bytes 49160 | tf_op jit(solution)/shard_map/ppermute | solution.py:373
  74.4 2.1 %collective-permute-start.14 = (bf16[16,512]{1,0:T(8,128)(2,1)S(1)}, bf16[16,512]{1,0:T(8,128)(2,1)S(1)}, u32[]{:S(2)}, u32[]{:S(2)}) collective-permute-start(bf16[16,512]{1,0:T(8,128)(2,1)S(1)} %get-tuple-element.29), channel_id=1, source_target_pairs={{16,0},{17,1},{18,2},{19,3},{20,4},{21,5},{22,6},{23,7},{24,8},{25... | collective-permute-start | bytes 49160 | tf_op jit(solution)/shard_map/ppermute | solution.py:373
  76.5 2.2 %collective-permute-start.15 = (bf16[16,512]{1,0:T(8,128)(2,1)S(1)}, bf16[16,512]{1,0:T(8,128)(2,1)S(1)}, u32[]{:S(2)}, u32[]{:S(2)}) collective-permute-start(bf16[16,512]{1,0:T(8,128)(2,1)S(1)} %get-tuple-element.30), channel_id=1, source_target_pairs={{17,0},{18,1},{19,2},{20,3},{21,4},{22,5},{23,6},{24,7},{25,8},{26... | collective-permute-start | bytes 49160 | tf_op jit(solution)/shard_map/ppermute | solution.py:373
  78.7 7.8 %collective-permute-start.8 = (bf16[16,512]{1,0:T(8,128)(2,1)S(1)}, bf16[16,512]{1,0:T(8,128)(2,1)S(1)}, u32[]{:S(2)}, u32[]{:S(2)}) collective-permute-start(bf16[16,512]{1,0:T(8,128)(2,1)S(1)} %get-tuple-element.23), channel_id=1, source_target_pairs={{15,16},{0,17},{1,18},{2,19},{3,20},{4,21},{5,22},{6,23},{7,24},{8... | collective-permute-start | bytes 49160 | tf_op jit(solution)/shard_map/ppermute | solution.py:373
  86.5 5.5 %collective-permute-start.9 = (bf16[16,512]{1,0:T(8,128)(2,1)S(1)}, bf16[16,512]{1,0:T(8,128)(2,1)S(1)}, u32[]{:S(2)}, u32[]{:S(2)}) collective-permute-start(bf16[16,512]{1,0:T(8,128)(2,1)S(1)} %get-tuple-element.24), channel_id=1, source_target_pairs={{0,16},{1,17},{2,18},{3,19},{4,20},{5,21},{6,22},{7,23},{8,24},{9,... | collective-permute-start | bytes 49160 | tf_op jit(solution)/shard_map/ppermute | solution.py:373
  92.8 2.8 %copy-done.1 = bf16[3,4,512,512]{3,2,1,0:T(8,128)(2,1)S(1)} copy-done((bf16[3,4,512,512]{3,2,1,0:T(8,128)(2,1)S(1)}, bf16[3,4,512,512]{3,2,1,0:T(8,128)(2,1)}, u32[]{:S(2)}) %copy-start.1) | copy-done | bytes 6291480
  95.6 2.7 %middle.1 = (f32[128,512]{1,0:T(8,128)S(1)}, f32[8,512]{1,0:T(8,128)S(1)}, bf16[8,512]{1,0:T(8,128)(2,1)S(1)}) custom-call(f32[2]{0:T(128)S(1)} %add_convert_fusion.inner_ref, f32[128,512]{1,0:T(8,128)S(1)} %get-tuple-element.22.mz_ref, bf16[16,512]{1,0:T(8,128)(2,1)S(1)} %collective-permute-done.8.refs_0_, ...), custom_call_target="tpu_custom_call" | custom-call | flops 805306368 | bytes 5242880 | tf_op jit(solution)/shard_map/middle/pallas_call | solution.py:219
  98.3 5.1 %collective-permute-start.16 = (bf16[8,512]{1,0:T(8,128)(2,1)S(1)}, bf16[8,512]{1,0:T(8,128)(2,1)S(1)}, u32[]{:S(2)}, u32[]{:S(2)}) collective-permute-start(bf16[8,512]{1,0:T(8,128)(2,1)S(1)} %get-tuple-element.32), channel_id=1, source_target_pairs={{15,16},{0,17},{1,18},{2,19},{3,20},{4,21},{5,22},{6,23},{7,24},{8... | collective-permute-start | bytes 24584 | tf_op jit(solution)/shard_map/ppermute | solution.py:373
  103.4 2.6 %collective-permute-start.17 = (bf16[8,512]{1,0:T(8,128)(2,1)S(1)}, bf16[8,512]{1,0:T(8,128)(2,1)S(1)}, u32[]{:S(2)}, u32[]{:S(2)}) collective-permute-start(bf16[8,512]{1,0:T(8,128)(2,1)S(1)} %get-tuple-element.32), channel_id=1, source_target_pairs={{0,16},{1,17},{2,18},{3,19},{4,20},{5,21},{6,22},{7,23},{8,24},{9,... | collective-permute-start | bytes 24584 | tf_op jit(solution)/shard_map/ppermute | solution.py:373
  106.0 1.9 %collective-permute-start.18 = (bf16[8,512]{1,0:T(8,128)(2,1)S(1)}, bf16[8,512]{1,0:T(8,128)(2,1)S(1)}, u32[]{:S(2)}, u32[]{:S(2)}) collective-permute-start(bf16[8,512]{1,0:T(8,128)(2,1)S(1)} %get-tuple-element.32), channel_id=1, source_target_pairs={{1,16},{2,17},{3,18},{4,19},{5,20},{6,21},{7,22},{8,23},{9,24},{10... | collective-permute-start | bytes 24584 | tf_op jit(solution)/shard_map/ppermute | solution.py:373
  107.9 3.2 %collective-permute-start.19 = (bf16[8,512]{1,0:T(8,128)(2,1)S(1)}, bf16[8,512]{1,0:T(8,128)(2,1)S(1)}, u32[]{:S(2)}, u32[]{:S(2)}) collective-permute-start(bf16[8,512]{1,0:T(8,128)(2,1)S(1)} %get-tuple-element.32), channel_id=1, source_target_pairs={{15,0},{0,1},{1,2},{2,3},{3,4},{4,5},{5,6},{6,7},{7,8},{8,9},{9,10... | collective-permute-start | bytes 24584 | tf_op jit(solution)/shard_map/ppermute | solution.py:373
  111.1 5.5 %collective-permute-start.21 = (bf16[8,512]{1,0:T(8,128)(2,1)S(1)}, bf16[8,512]{1,0:T(8,128)(2,1)S(1)}, u32[]{:S(2)}, u32[]{:S(2)}) collective-permute-start(bf16[8,512]{1,0:T(8,128)(2,1)S(1)} %get-tuple-element.32), channel_id=1, source_target_pairs={{31,0},{16,1},{17,2},{18,3},{19,4},{20,5},{21,6},{22,7},{23,8},{24... | collective-permute-start | bytes 24584 | tf_op jit(solution)/shard_map/ppermute | solution.py:373
  116.6 2.7 %collective-permute-start.22 = (bf16[8,512]{1,0:T(8,128)(2,1)S(1)}, bf16[8,512]{1,0:T(8,128)(2,1)S(1)}, u32[]{:S(2)}, u32[]{:S(2)}) collective-permute-start(bf16[8,512]{1,0:T(8,128)(2,1)S(1)} %get-tuple-element.32), channel_id=1, source_target_pairs={{16,0},{17,1},{18,2},{19,3},{20,4},{21,5},{22,6},{23,7},{24,8},{25... | collective-permute-start | bytes 24584 | tf_op jit(solution)/shard_map/ppermute | solution.py:373
  119.3 1.9 %collective-permute-start.23 = (bf16[8,512]{1,0:T(8,128)(2,1)S(1)}, bf16[8,512]{1,0:T(8,128)(2,1)S(1)}, u32[]{:S(2)}, u32[]{:S(2)}) collective-permute-start(bf16[8,512]{1,0:T(8,128)(2,1)S(1)} %get-tuple-element.32), channel_id=1, source_target_pairs={{17,0},{18,1},{19,2},{20,3},{21,4},{22,5},{23,6},{24,7},{25,8},{26... | collective-permute-start | bytes 24584 | tf_op jit(solution)/shard_map/ppermute | solution.py:373
  121.3 1.8 %collective-permute-done.22.refs_6_ = bf16[8,512]{1,0:T(8,128)(2,1)S(1)} collective-permute-done((bf16[8,512]{1,0:T(8,128)(2,1)S(1)}, bf16[8,512]{1,0:T(8,128)(2,1)S(1)}, u32[]{:S(2)}, u32[]{:S(2)}) %collective-permute-start.22) | collective-permute-done | bytes 8224 | tf_op jit(solution)/shard_map/ppermute | solution.py:373
  123.1 5.4 %collective-permute-done.23.refs_7_ = bf16[8,512]{1,0:T(8,128)(2,1)S(1)} collective-permute-done((bf16[8,512]{1,0:T(8,128)(2,1)S(1)}, bf16[8,512]{1,0:T(8,128)(2,1)S(1)}, u32[]{:S(2)}, u32[]{:S(2)}) %collective-permute-start.23) | collective-permute-done | bytes 8224 | tf_op jit(solution)/shard_map/ppermute | solution.py:373
  132.0 4.7 %finish.1 = f32[2,32,32,512]{3,2,1,0:T(8,128)} custom-call(f32[2,32,32,512]{3,2,1,0:T(8,128)S(1)} %copy-done.3, bf16[2,32,32,512]{3,2,1,0:T(8,128)(2,1)S(1)} %copy-done.5, bf16[3,4,512,512]{3,2,1,0:T(8,128)(2,1)S(1)} %bitcast.21, f32[2,8,8,512]{3,2,1,0:T(8,128)S(1)} %coarsest.1.spread_ref), custom_call_target="tpu_custom_call" | custom-call | flops 1073741824 | bytes 10485760 | tf_op jit(solution)/shard_map/finish/pallas_call | solution.py:295
  (70 shorter events, 4.8 us)
Async XLA Ops:
  0.7 31.3 %copy-start.7 = (f32[3,512]{1,0:T(4,128)S(1)}, f32[3,512]{1,0:T(4,128)}, u32[]{:S(2)}) copy-start(f32[3,512]{1,0:T(4,128)} %refs_9_.3) | copy-start | bytes 18436
  5.1 21.6 %collective-permute-start.4 = (bf16[2,1,512]{2,1,0:T(2,128)(2,1)S(1)}, bf16[2,1,512]{2,1,0:T(2,128)(2,1)S(1)}, u32[]{:S(2)}, u32[]{:S(2)}) collective-permute-start(bf16[2,1,512]{2,1,0:T(2,128)(2,1)S(1)} %get-tuple-element.37), channel_id=1, source_target_pairs={{15,16},{0,17},{1,18},{2,19},{3,20},{4,21},{5,22},{6,23},{7,24},{8... | collective-permute-start | bytes 6152 | tf_op jit(solution)/shard_map/ppermute | solution.py:373
  11.4 17.3 %collective-permute-start.5 = (bf16[2,1,512]{2,1,0:T(2,128)(2,1)S(1)}, bf16[2,1,512]{2,1,0:T(2,128)(2,1)S(1)}, u32[]{:S(2)}, u32[]{:S(2)}) collective-permute-start(bf16[2,1,512]{2,1,0:T(2,128)(2,1)S(1)} %get-tuple-element.36), channel_id=1, source_target_pairs={{1,16},{2,17},{3,18},{4,19},{5,20},{6,21},{7,22},{8,23},{9,24},{10... | collective-permute-start | bytes 6152 | tf_op jit(solution)/shard_map/ppermute | solution.py:373
  13.3 18.6 %collective-permute-start.6 = (bf16[2,1,512]{2,1,0:T(2,128)(2,1)S(1)}, bf16[2,1,512]{2,1,0:T(2,128)(2,1)S(1)}, u32[]{:S(2)}, u32[]{:S(2)}) collective-permute-start(bf16[2,1,512]{2,1,0:T(2,128)(2,1)S(1)} %get-tuple-element.35), channel_id=1, source_target_pairs={{31,0},{16,1},{17,2},{18,3},{19,4},{20,5},{21,6},{22,7},{23,8},{24... | collective-permute-start | bytes 6152 | tf_op jit(solution)/shard_map/ppermute | solution.py:373
  19.1 21.5 %collective-permute-start.7 = (bf16[2,1,512]{2,1,0:T(2,128)(2,1)S(1)}, bf16[2,1,512]{2,1,0:T(2,128)(2,1)S(1)}, u32[]{:S(2)}, u32[]{:S(2)}) collective-permute-start(bf16[2,1,512]{2,1,0:T(2,128)(2,1)S(1)} %get-tuple-element.34), channel_id=1, source_target_pairs={{17,0},{18,1},{19,2},{20,3},{21,4},{22,5},{23,6},{24,7},{25,8},{26... | collective-permute-start | bytes 6152 | tf_op jit(solution)/shard_map/ppermute | solution.py:373
  21.3 19.3 %collective-permute-start = (bf16[2,32,512]{2,1,0:T(8,128)(2,1)S(1)}, bf16[2,32,512]{2,1,0:T(8,128)(2,1)S(1)}, u32[]{:S(2)}, u32[]{:S(2)}) collective-permute-start(bf16[2,32,512]{2,1,0:T(8,128)(2,1)S(1)} %bitcast.22), channel_id=1, source_target_pairs={{0,16},{1,17},{2,18},{3,19},{4,20},{5,21},{6,22},{7,23},{8,24},{9,... | collective-permute-start | bytes 196616 | tf_op jit(solution)/shard_map/ppermute | solution.py:373
  26.8 13.8 %collective-permute-start.1 = (bf16[2,32,512]{2,1,0:T(8,128)(2,1)S(1)}, bf16[2,32,512]{2,1,0:T(8,128)(2,1)S(1)}, u32[]{:S(2)}, u32[]{:S(2)}) collective-permute-start(bf16[2,32,512]{2,1,0:T(8,128)(2,1)S(1)} %bitcast.23), channel_id=1, source_target_pairs={{16,0},{17,1},{18,2},{19,3},{20,4},{21,5},{22,6},{23,7},{24,8},{25... | collective-permute-start | bytes 196616 | tf_op jit(solution)/shard_map/ppermute | solution.py:373
  28.7 11.9 %collective-permute-start.2 = (bf16[2,32,512]{2,1,0:T(8,128)(2,1)S(1)}, bf16[2,32,512]{2,1,0:T(8,128)(2,1)S(1)}, u32[]{:S(2)}, u32[]{:S(2)}) collective-permute-start(bf16[2,32,512]{2,1,0:T(8,128)(2,1)S(1)} %get-tuple-element.39), channel_id=1, source_target_pairs={{15,0},{0,1},{1,2},{2,3},{3,4},{4,5},{5,6},{6,7},{7,8},{8,9},{9,10... | collective-permute-start | bytes 196616 | tf_op jit(solution)/shard_map/ppermute | solution.py:373
  31.9 8.7 %collective-permute-start.3 = (bf16[2,32,512]{2,1,0:T(8,128)(2,1)S(1)}, bf16[2,32,512]{2,1,0:T(8,128)(2,1)S(1)}, u32[]{:S(2)}, u32[]{:S(2)}) collective-permute-start(bf16[2,32,512]{2,1,0:T(8,128)(2,1)S(1)} %get-tuple-element.38), channel_id=1, source_target_pairs={{1,0},{2,1},{3,2},{4,3},{5,4},{6,5},{7,6},{8,7},{9,8},{10,9},{11,1... | collective-permute-start | bytes 196616 | tf_op jit(solution)/shard_map/ppermute | solution.py:373
  42.9 49.2 %copy-start.14 = (f32[2,2,2,512]{3,2,1,0:T(2,128)S(1)}, f32[2,2,2,512]{3,2,1,0:T(2,128)}, u32[]{:S(2)}) copy-start(f32[2,2,2,512]{3,2,1,0:T(2,128)} %param.15) | copy-start | bytes 49156
  42.9 50.0 %copy-start.4 = (bf16[4,512,512]{2,1,0:T(8,128)(2,1)S(1)}, bf16[4,512,512]{2,1,0:T(8,128)(2,1)}, u32[]{:S(2)}) copy-start(bf16[4,512,512]{2,1,0:T(8,128)(2,1)} %refs_11_.1) | copy-start | bytes 6291460
  42.9 50.0 %copy-start.6 = (bf16[1024,256]{1,0:T(8,128)(2,1)S(1)}, bf16[1024,256]{1,0:T(8,128)(2,1)}, u32[]{:S(2)}) copy-start(bf16[1024,256]{1,0:T(8,128)(2,1)} %constant.28.clone.refs_12_) | copy-start | bytes 1572868
  42.9 49.9 %copy-start.10 = (f32[8,128]{1,0:T(8,128)S(1)}, f32[8,128]{1,0:T(8,128)}, u32[]{:S(2)}) copy-start(f32[8,128]{1,0:T(8,128)} %constant.29.clone.refs_13_) | copy-start | bytes 12292
  63.8 12.7 %collective-permute-start.10 = (bf16[16,512]{1,0:T(8,128)(2,1)S(1)}, bf16[16,512]{1,0:T(8,128)(2,1)S(1)}, u32[]{:S(2)}, u32[]{:S(2)}) collective-permute-start(bf16[16,512]{1,0:T(8,128)(2,1)S(1)} %get-tuple-element.25), channel_id=1, source_target_pairs={{1,16},{2,17},{3,18},{4,19},{5,20},{6,21},{7,22},{8,23},{9,24},{10... | collective-permute-start | bytes 49160 | tf_op jit(solution)/shard_map/ppermute | solution.py:373
  66.5 12.2 %collective-permute-start.11 = (bf16[16,512]{1,0:T(8,128)(2,1)S(1)}, bf16[16,512]{1,0:T(8,128)(2,1)S(1)}, u32[]{:S(2)}, u32[]{:S(2)}) collective-permute-start(bf16[16,512]{1,0:T(8,128)(2,1)S(1)} %get-tuple-element.26), channel_id=1, source_target_pairs={{15,0},{0,1},{1,2},{2,3},{3,4},{4,5},{5,6},{6,7},{7,8},{8,9},{9,10... | collective-permute-start | bytes 49160 | tf_op jit(solution)/shard_map/ppermute | solution.py:373
  72.2 14.2 %collective-permute-start.12 = (bf16[16,512]{1,0:T(8,128)(2,1)S(1)}, bf16[16,512]{1,0:T(8,128)(2,1)S(1)}, u32[]{:S(2)}, u32[]{:S(2)}) collective-permute-start(bf16[16,512]{1,0:T(8,128)(2,1)S(1)} %get-tuple-element.27), channel_id=1, source_target_pairs={{1,0},{2,1},{3,2},{4,3},{5,4},{6,5},{7,6},{8,7},{9,8},{10,9},{11,1... | collective-permute-start | bytes 49160 | tf_op jit(solution)/shard_map/ppermute | solution.py:373
  72.2 19.8 %collective-permute-start.13 = (bf16[16,512]{1,0:T(8,128)(2,1)S(1)}, bf16[16,512]{1,0:T(8,128)(2,1)S(1)}, u32[]{:S(2)}, u32[]{:S(2)}) collective-permute-start(bf16[16,512]{1,0:T(8,128)(2,1)S(1)} %get-tuple-element.28), channel_id=1, source_target_pairs={{31,0},{16,1},{17,2},{18,3},{19,4},{20,5},{21,6},{22,7},{23,8},{24... | collective-permute-start | bytes 49160 | tf_op jit(solution)/shard_map/ppermute | solution.py:373
  74.4 17.6 %collective-permute-start.14 = (bf16[16,512]{1,0:T(8,128)(2,1)S(1)}, bf16[16,512]{1,0:T(8,128)(2,1)S(1)}, u32[]{:S(2)}, u32[]{:S(2)}) collective-permute-start(bf16[16,512]{1,0:T(8,128)(2,1)S(1)} %get-tuple-element.29), channel_id=1, source_target_pairs={{16,0},{17,1},{18,2},{19,3},{20,4},{21,5},{22,6},{23,7},{24,8},{25... | collective-permute-start | bytes 49160 | tf_op jit(solution)/shard_map/ppermute | solution.py:373
  76.5 15.6 %collective-permute-start.15 = (bf16[16,512]{1,0:T(8,128)(2,1)S(1)}, bf16[16,512]{1,0:T(8,128)(2,1)S(1)}, u32[]{:S(2)}, u32[]{:S(2)}) collective-permute-start(bf16[16,512]{1,0:T(8,128)(2,1)S(1)} %get-tuple-element.30), channel_id=1, source_target_pairs={{17,0},{18,1},{19,2},{20,3},{21,4},{22,5},{23,6},{24,7},{25,8},{26... | collective-permute-start | bytes 49160 | tf_op jit(solution)/shard_map/ppermute | solution.py:373
  78.7 13.4 %collective-permute-start.8 = (bf16[16,512]{1,0:T(8,128)(2,1)S(1)}, bf16[16,512]{1,0:T(8,128)(2,1)S(1)}, u32[]{:S(2)}, u32[]{:S(2)}) collective-permute-start(bf16[16,512]{1,0:T(8,128)(2,1)S(1)} %get-tuple-element.23), channel_id=1, source_target_pairs={{15,16},{0,17},{1,18},{2,19},{3,20},{4,21},{5,22},{6,23},{7,24},{8... | collective-permute-start | bytes 49160 | tf_op jit(solution)/shard_map/ppermute | solution.py:373
  86.5 6.3 %collective-permute-start.9 = (bf16[16,512]{1,0:T(8,128)(2,1)S(1)}, bf16[16,512]{1,0:T(8,128)(2,1)S(1)}, u32[]{:S(2)}, u32[]{:S(2)}) collective-permute-start(bf16[16,512]{1,0:T(8,128)(2,1)S(1)} %get-tuple-element.24), channel_id=1, source_target_pairs={{0,16},{1,17},{2,18},{3,19},{4,20},{5,21},{6,22},{7,23},{8,24},{9,... | collective-permute-start | bytes 49160 | tf_op jit(solution)/shard_map/ppermute | solution.py:373
  95.6 32.9 %copy-start.8 = (bf16[128,16]{1,0:T(8,128)(2,1)S(1)}, bf16[128,16]{1,0:T(8,128)(2,1)}, u32[]{:S(2)}) copy-start(bf16[128,16]{1,0:T(8,128)(2,1)} %constant.31.clone.refs_14_) | copy-start | bytes 12292
  95.6 32.9 %copy-start.9 = (bf16[64,128]{1,0:T(8,128)(2,1)S(1)}, bf16[64,128]{1,0:T(8,128)(2,1)}, u32[]{:S(2)}) copy-start(bf16[64,128]{1,0:T(8,128)(2,1)} %constant.30.clone.refs_13_) | copy-start | bytes 49156
  95.6 34.8 %slice-start = ((s8[6291456]{0:T(1024)(128)(4,1)}), s8[4194304]{0:T(1024)(128)(4,1)S(1)}, s32[]{:S(2)}) async-start(s8[6291456]{0:T(1024)(128)(4,1)} %bitcast.20), calls=%async_computation | async-start | bytes 8388608
  98.3 12.8 %collective-permute-start.16 = (bf16[8,512]{1,0:T(8,128)(2,1)S(1)}, bf16[8,512]{1,0:T(8,128)(2,1)S(1)}, u32[]{:S(2)}, u32[]{:S(2)}) collective-permute-start(bf16[8,512]{1,0:T(8,128)(2,1)S(1)} %get-tuple-element.32), channel_id=1, source_target_pairs={{15,16},{0,17},{1,18},{2,19},{3,20},{4,21},{5,22},{6,23},{7,24},{8... | collective-permute-start | bytes 24584 | tf_op jit(solution)/shard_map/ppermute | solution.py:373
  103.4 13.2 %collective-permute-start.17 = (bf16[8,512]{1,0:T(8,128)(2,1)S(1)}, bf16[8,512]{1,0:T(8,128)(2,1)S(1)}, u32[]{:S(2)}, u32[]{:S(2)}) collective-permute-start(bf16[8,512]{1,0:T(8,128)(2,1)S(1)} %get-tuple-element.32), channel_id=1, source_target_pairs={{0,16},{1,17},{2,18},{3,19},{4,20},{5,21},{6,22},{7,23},{8,24},{9,... | collective-permute-start | bytes 24584 | tf_op jit(solution)/shard_map/ppermute | solution.py:373
  106.0 13.4 %collective-permute-start.18 = (bf16[8,512]{1,0:T(8,128)(2,1)S(1)}, bf16[8,512]{1,0:T(8,128)(2,1)S(1)}, u32[]{:S(2)}, u32[]{:S(2)}) collective-permute-start(bf16[8,512]{1,0:T(8,128)(2,1)S(1)} %get-tuple-element.32), channel_id=1, source_target_pairs={{1,16},{2,17},{3,18},{4,19},{5,20},{6,21},{7,22},{8,23},{9,24},{10... | collective-permute-start | bytes 24584 | tf_op jit(solution)/shard_map/ppermute | solution.py:373
  107.9 13.4 %collective-permute-start.19 = (bf16[8,512]{1,0:T(8,128)(2,1)S(1)}, bf16[8,512]{1,0:T(8,128)(2,1)S(1)}, u32[]{:S(2)}, u32[]{:S(2)}) collective-permute-start(bf16[8,512]{1,0:T(8,128)(2,1)S(1)} %get-tuple-element.32), channel_id=1, source_target_pairs={{15,0},{0,1},{1,2},{2,3},{3,4},{4,5},{5,6},{6,7},{7,8},{8,9},{9,10... | collective-permute-start | bytes 24584 | tf_op jit(solution)/shard_map/ppermute | solution.py:373
  111.1 10.2 %collective-permute-start.20 = (bf16[8,512]{1,0:T(8,128)(2,1)S(1)}, bf16[8,512]{1,0:T(8,128)(2,1)S(1)}, u32[]{:S(2)}, u32[]{:S(2)}) collective-permute-start(bf16[8,512]{1,0:T(8,128)(2,1)S(1)} %get-tuple-element.32), channel_id=1, source_target_pairs={{1,0},{2,1},{3,2},{4,3},{5,4},{6,5},{7,6},{8,7},{9,8},{10,9},{11,1... | collective-permute-start | bytes 24584 | tf_op jit(solution)/shard_map/ppermute | solution.py:373
  111.1 10.2 %collective-permute-start.21 = (bf16[8,512]{1,0:T(8,128)(2,1)S(1)}, bf16[8,512]{1,0:T(8,128)(2,1)S(1)}, u32[]{:S(2)}, u32[]{:S(2)}) collective-permute-start(bf16[8,512]{1,0:T(8,128)(2,1)S(1)} %get-tuple-element.32), channel_id=1, source_target_pairs={{31,0},{16,1},{17,2},{18,3},{19,4},{20,5},{21,6},{22,7},{23,8},{24... | collective-permute-start | bytes 24584 | tf_op jit(solution)/shard_map/ppermute | solution.py:373
  116.6 6.5 %collective-permute-start.22 = (bf16[8,512]{1,0:T(8,128)(2,1)S(1)}, bf16[8,512]{1,0:T(8,128)(2,1)S(1)}, u32[]{:S(2)}, u32[]{:S(2)}) collective-permute-start(bf16[8,512]{1,0:T(8,128)(2,1)S(1)} %get-tuple-element.32), channel_id=1, source_target_pairs={{16,0},{17,1},{18,2},{19,3},{20,4},{21,5},{22,6},{23,7},{24,8},{25... | collective-permute-start | bytes 24584 | tf_op jit(solution)/shard_map/ppermute | solution.py:373
  119.3 9.2 %collective-permute-start.23 = (bf16[8,512]{1,0:T(8,128)(2,1)S(1)}, bf16[8,512]{1,0:T(8,128)(2,1)S(1)}, u32[]{:S(2)}, u32[]{:S(2)}) collective-permute-start(bf16[8,512]{1,0:T(8,128)(2,1)S(1)} %get-tuple-element.32), channel_id=1, source_target_pairs={{17,0},{18,1},{19,2},{20,3},{21,4},{22,5},{23,6},{24,7},{25,8},{26... | collective-permute-start | bytes 24584 | tf_op jit(solution)/shard_map/ppermute | solution.py:373
  (10 other events, 72.3 us)

commit v2 on v1

--- a/solution.py
+++ b/solution.py
@@ -35,6 +35,33 @@
     return jnp.concatenate(parts, axis=1)
 
 
+def rims_kernel(top_ref, bottom_ref, west_ref, east_ref, top_out, bottom_out, west_out, east_out):
+    top_out[...] = top_ref[...].reshape(2, 32, D).astype(BF)
+    bottom_out[...] = bottom_ref[...].reshape(2, 32, D).astype(BF)
+    for b in range(2):
+        west_out[b] = west_ref[b, :, 0, :].astype(BF)
+        east_out[b] = east_ref[b, :, 7, :].astype(BF)
+
+
+def rims(fine):
+    out = pl.BlockSpec((2, 32, D), lambda i: (0, 0, 0))
+    return pl.pallas_call(
+        rims_kernel,
+        name="rims",
+        grid=(1,),
+        in_specs=[
+            pl.BlockSpec((2, 1, 32, D), lambda i: (0, 0, 0, 0)),
+            pl.BlockSpec((2, 1, 32, D), lambda i: (0, 31, 0, 0)),
+            pl.BlockSpec((2, 32, 8, D), lambda i: (0, 0, 0, 0)),
+            pl.BlockSpec((2, 32, 8, D), lambda i: (0, 0, 3, 0)),
+        ],
+        out_specs=[out] * 4,
+        out_shape=[jax.ShapeDtypeStruct((2, 32, D), BF)] * 4,
+        compiler_params=pltpu.CompilerParams(vmem_limit_bytes=24 << 20),
+        cost_estimate=pl.CostEstimate(flops=1 << 20, bytes_accessed=3 << 20, transcendentals=0),
+    )(fine, fine, fine, fine)
+
+
 def prep_kernel(s_ref, w_ref, c_ref, r_out, t_out, ps_out, tmp):
     x = s_ref[0]
     op = x.reshape(PRB * 32, D).astype(BF)
@@ -71,27 +98,17 @@
     )(fine, pw, pb)
 
 
-def stack_rows(parts, shape):
-    rows = lax.broadcasted_iota(jnp.int32, shape, 0)
-    out = jnp.zeros(shape, F32)
-    for i, part in enumerate(parts):
-        out = jnp.where(rows == i, jnp.broadcast_to(part.astype(F32), shape), out)
-    return out
-
-
-def edge_kernel(r_ref, t_ref, up_ref, down_ref, left_ref, right_ref, ul_ref, ur_ref, dl_ref, dr_ref,
+def edge_kernel(r_ref, t_ref, up_ref, down_ref, left_ref, right_ref,
                 mask_ref, w_ref, b0_ref, ps_ref, mid_ref, pick_ref,
                 avg_out, mz_out, *rest):
-    rim_outs, (sh, hs, tmp, pa) = rest[:8], rest[8:]
+    rim_outs, (sh, hs, tmp, pa) = rest[:4], rest[4:]
     b = pl.program_id(0)
     blk = pl.program_id(1)
 
     @pl.when(blk == 0)
     def _():
-        rim = jnp.concatenate([up_ref[0], down_ref[0], left_ref[0], right_ref[0]], axis=0)
-        hs[0:128, :] = (0.5 * mm(rim, w_ref[0, 1])).astype(BF).astype(F32)
-        corners = stack_rows([ul_ref[0], ur_ref[0], dl_ref[0], dr_ref[0]], (8, D)).astype(BF)
-        hs[128:136, :] = (0.5 * mm(corners, w_ref[0, 1])).astype(BF).astype(F32)
+        for n, ref in enumerate((up_ref, down_ref, left_ref, right_ref)):
+            hs[n, 0:ref.shape[1], :] = (0.5 * mm(ref[0], w_ref[0, 1])).astype(BF).astype(F32)
         rows = lax.broadcasted_iota(jnp.int32, (32, D), 0)
 
         def put(i, x, left, right):
@@ -99,12 +116,12 @@
             sh[0, i] = jnp.where(rows == 0, jnp.broadcast_to(left, (32, D)), pltpu.roll(x, 1, 0)).astype(BF)
             sh[2, i] = jnp.where(rows == 31, jnp.broadcast_to(right, (32, D)), pltpu.roll(x, 31, 0)).astype(BF)
 
-        put(0, hs[0:32, :], hs[128:129, :], hs[129:130, :])
-        put(33, hs[32:64, :], hs[130:131, :], hs[131:132, :])
+        put(0, hs[0, 0:32, :], hs[2, 32:33, :], hs[3, 32:33, :])
+        put(33, hs[1, 0:32, :], hs[2, 33:34, :], hs[3, 33:34, :])
 
         @pl.loop(0, 32)
         def _(i):
-            put(i + 1, t_ref[0, i].astype(F32), hs[pl.ds(64 + i, 1), :], hs[pl.ds(96 + i, 1), :])
+            put(i + 1, t_ref[0, i].astype(F32), hs[2, pl.ds(i, 1), :], hs[3, pl.ds(i, 1), :])
 
     row0 = blk * RB
     rv = r_ref[0].reshape(RB * 32, D)
@@ -131,7 +148,7 @@
         mz = mid_ref[...].reshape(128, D) + gate(0.5 * mm(pooled, b0_ref[0]))
         mz_out[...] = mz
         rims = mm(pick_ref[...], mz.astype(BF)).astype(BF)
-        for d in range(8):
+        for d in range(4):
             rim_outs[d][...] = rims[16 * d:16 * d + 16]
 
 
@@ -145,29 +162,29 @@
             pl.BlockSpec((1, RB, 32, D), lambda b, i: (b, i, 0, 0)),
             pl.BlockSpec((1, 32, 32, D), lambda b, i: (b, 0, 0, 0)),
         ]
-        + [pl.BlockSpec((1, 32, D), lambda b, i: (b, 0, 0))] * 4
-        + [pl.BlockSpec((1, 1, D), lambda b, i: (b, 0, 0))] * 4
+        + [pl.BlockSpec((1, 32, D), lambda b, i: (b, 0, 0))] * 2
+        + [pl.BlockSpec((1, 34, D), lambda b, i: (b, 0, 0))] * 2
         + [
             pl.BlockSpec((8, RB, 32, 128), lambda b, i: (0, i, 0, 0)),
             whole(1, 4, D, D),
             whole(1, D, D),
             whole(2, 8, 8, D),
             whole(2, 8, 8, D),
-            whole(128, 128),
+            whole(64, 128),
         ],
         out_specs=[
             pl.BlockSpec((1, RB, 32, D), lambda b, i: (b, i, 0, 0)),
             whole(128, D),
         ]
-        + [whole(16, D)] * 8,
+        + [whole(16, D)] * 4,
         out_shape=[
             jax.ShapeDtypeStruct((2, 32, 32, D), BF),
             jax.ShapeDtypeStruct((128, D), F32),
         ]
-        + [jax.ShapeDtypeStruct((16, D), BF)] * 8,
+        + [jax.ShapeDtypeStruct((16, D), BF)] * 4,
         scratch_shapes=[
             pltpu.VMEM((3, 34, 32, D), BF),
-            pltpu.VMEM((136, D), F32),
+            pltpu.VMEM((4, 40, D), F32),
             pltpu.VMEM((8, 4, 32, 128), F32),
             pltpu.VMEM((2, 8, 8, D), F32),
         ],
@@ -177,8 +194,8 @@
 
 
 def middle_kernel(inner_ref, mz_ref, *refs):
-    rim_refs = refs[:8]
-    w_ref, c_ref, b1_ref, coarse_ref, gather_ref, mean_ref, mo_out, cz_out, czb_out = refs[8:]
+    rim_refs = refs[:4]
+    w_ref, c_ref, b1_ref, coarse_ref, gather_ref, mean_ref, mo_out, cz_out, czb_out = refs[4:]
     mz = mz_ref[...]
     own = mz.astype(BF)
     recv = 0.5 * (mm(own, w_ref[0, 0]) + c_ref[1:2, :])
@@ -221,7 +238,8 @@
         name="middle",
         grid=(1,),
         in_specs=[pl.BlockSpec(memory_space=pltpu.SMEM), full(128, D)]
-        + [full(16, D)] * 8
+        + [full(16, D)] * 2
+        + [full(48, D)] * 2
         + [level_block(1), full(3, D), bridge_block(1), full(8, D), full(1024, 256), full(8, 128)],
         out_specs=[full(128, D), full(8, D), full(8, D)],
         out_shape=[
@@ -235,8 +253,8 @@
 
 
 def coarse_kernel(inner_ref, cz_ref, *refs):
-    rim_refs = refs[:8]
-    w_ref, c_ref, b2_ref, b3_ref, mo_ref, gather_ref, lift_ref, spread_out = refs[8:]
+    rim_refs = refs[:4]
+    w_ref, c_ref, b2_ref, b3_ref, mo_ref, gather_ref, lift_ref, spread_out = refs[4:]
     cz = cz_ref[...]
     own = cz.astype(BF)
     recv = 0.5 * (mm(own, w_ref[0, 0]) + c_ref[2:3, :])
@@ -264,7 +282,8 @@
         name="coarsest",
         grid=(1,),
         in_specs=[pl.BlockSpec(memory_space=pltpu.SMEM), full(8, D)]
-        + [full(8, D)] * 8
+        + [full(8, D)] * 2
+        + [full(24, D)] * 2
         + [level_block(2), full(3, D), bridge_block(2), bridge_block(3), full(128, D), full(64, 128), full(128, 16)],
         out_specs=full(2, 8, 8, D),
         out_shape=jax.ShapeDtypeStruct((2, 8, 8, D), F32),
@@ -310,12 +329,10 @@
 
 
 def place_middle():
-    pick = np.zeros((128, 128), np.float32)
-    for d, (p, q) in enumerate(OFFS):
-        for b in range(2):
-            rows = [0] if p < 0 else [7] if p > 0 else range(8)
-            cols = [0] if q < 0 else [7] if q > 0 else range(8)
-            for n, (i, j) in enumerate((i, j) for i in rows for j in cols):
+    pick = np.zeros((64, 128), np.float32)
+    for b in range(2):
+        for n in range(8):
+            for d, (i, j) in enumerate(((0, n), (7, n), (n, 0), (n, 7))):
                 pick[16 * d + 8 * b + n, 64 * b + 8 * i + j] = 1
     gather = np.zeros((1024, 256), np.float32)
     for k, (p, q) in enumerate(OFFS):
@@ -323,14 +340,12 @@
             for i in range(8):
                 for j in range(8):
                     y, x = i + p, j + q
-                    dy = (y > 7) - (y < 0)
-                    dx = (x > 7) - (x < 0)
-                    if (dy, dx) == (0, 0):
-                        source = 64 * b + 8 * y + x
+                    if 0 <= x < 8:
+                        n = 128 + 8 * b + x if y < 0 else 144 + 8 * b + x if y > 7 else 64 * b + 8 * y + x
                     else:
-                        n = 0 if dy and dx else x if dy else y
-                        source = 128 + 16 * OFFS.index((dy, dx)) + 8 * b + n
-                    gather[128 * k + 64 * b + 8 * i + j, source] = 1
+                        base = 160 + 8 * b if x < 0 else 208 + 8 * b
+                        n = base + 16 + x % 8 if y < 0 else base + 32 + x % 8 if y > 7 else base + y
+                    gather[128 * k + 64 * b + 8 * i + j, n] = 1
     mean = np.zeros((8, 128), np.float32)
     for b in range(2):
         for i in range(8):
@@ -346,9 +361,7 @@
             for i in range(2):
                 for j in range(2):
                     y, x = i + p, j + q
-                    dy = (y > 1) - (y < 0)
-                    dx = (x > 1) - (x < 0)
-                    base = 0 if (dy, dx) == (0, 0) else 8 + 8 * OFFS.index((dy, dx))
+                    base = (24 if x < 0 else 48 if x > 1 else 0) + (8 if y < 0 else 16 if y > 1 else 0)
                     gather[8 * k + 4 * b + 2 * i + j, base + 4 * b + 2 * (y % 2) + x % 2] = 1
     lift = np.zeros((128, 16), np.float32)
     for b in range(2):
@@ -360,27 +373,22 @@
     return gather, lift
 
 
-def exchange(pieces):
-    rows, cols = lax.axis_size("lat"), lax.axis_size("lon")
-    out = []
-    for d, (p, q) in enumerate(OFFS):
-        perm = []
-        for y in range(rows):
-            for x in range(cols):
-                source = y + p
-                if 0 <= source < rows:
-                    perm.append((source * cols + (x + q) % cols, y * cols + x))
-        out.append(lax.ppermute(pieces[7 - d], ("lat", "lon"), perm))
-    return out
+def trade(low_side, high_side, axis):
+    count = lax.axis_size(axis)
+    forward = [(i, (i + 1) % count) for i in range(count)]
+    backward = [(i, (i - 1) % count) for i in range(count)]
+    return lax.ppermute(high_side, axis, forward), lax.ppermute(low_side, axis, backward)
 
 
 def local(fine, mid, coarse, flags, pw, bw, pb):
-    edge_of = {-1: slice(0, 1), 1: slice(-1, None), 0: slice(None)}
-    pieces = []
-    for p, q in OFFS:
-        part = fine[:, edge_of[p], edge_of[q], :].astype(BF)
-        pieces.append(part.reshape(2, -1, D))
-    rim = exchange(pieces)
+    fine, pw, bw = (pltpu.with_memory_space_constraint(a, pltpu.HBM) for a in (fine, pw, bw))
+    top, bottom, west, east = rims(fine)
+    up, down = trade(top, bottom, "lat")
+    left, right = trade(
+        jnp.concatenate([west, up[:, :1], down[:, :1]], axis=1),
+        jnp.concatenate([east, up[:, 31:], down[:, 31:]], axis=1),
+        "lon",
+    )
     lat = lax.axis_index("lat")
     rows = lax.axis_size("lat")
     inner = jnp.stack([lat > 0, lat < rows - 1]).astype(F32)
@@ -392,12 +400,18 @@
     pick, gather, mean = place_middle()
     gather_c, lift = place_coarse()
     r, t, ps = prep(fine, pw, pb)
-    ul, up, ur, left, right, dl, down, dr = rim
-    avg, mz, *send = edge(r, t, (up, down, left, right, ul, ur, dl, dr), mask, pw, bw, ps, mid, jnp.asarray(pick, BF))
-    rim = exchange(send)
-    mo, cz, czb = middle(inner, mz, rim, pw, pb, bw, coarse.reshape(8, D), jnp.asarray(gather, BF), jnp.asarray(mean, F32))
-    rim = exchange([czb] * 8)
-    spread = coarsest(inner, cz, rim, pw, pb, bw, mo, jnp.asarray(gather_c, BF), jnp.asarray(lift, BF))
+    avg, mz, top, bottom, west, east = edge(r, t, (up, down, left, right), mask, pw, bw, ps, mid, jnp.asarray(pick, BF))
+    up, down = trade(top, bottom, "lat")
+    left, right = trade(jnp.concatenate([west, up, down]), jnp.concatenate([east, up, down]), "lon")
+    mo, cz, czb = middle(
+        inner, mz, (up, down, left, right), pw, pb, bw, coarse.reshape(8, D), jnp.asarray(gather, BF), jnp.asarray(mean, F32)
+    )
+    up, down = trade(czb, czb, "lat")
+    column = jnp.concatenate([czb, up, down])
+    left, right = trade(column, column, "lon")
+    spread = coarsest(
+        inner, cz, (up, down, left, right), pw, pb, bw, mo, jnp.asarray(gather_c, BF), jnp.asarray(lift, BF)
+    )
     return finish(fine, avg, pw, spread), avg
 
 

time: 137 us -> 86 us (0.63)
  the two profiles are of different devices: /device:TPU:111 before, /device:TPU:127 now
where the time goes in v2:
time: 86 us; the launch traced here: 85.6 us
  Pallas kernels  44.9 us (52%)
  waiting for transfers between devices  22.8 us (27%)
  starting transfers between devices  14.4 us (17%)
  local copies, waits for them, and re-layouts  2.31 us (3%)
    pallas_call x1, Pallas kernels, edge(): pl.pallas_call(edge_kernel, name='edge', grid=(2, 32 // RB), in_specs=[pl...  21.1 us
    ppermute x6, waiting for transfers between devices, trade(): lax.ppermute(low_side, axis, backward)  16.9 us
    ppermute x6, starting transfers between devices, trade(): lax.ppermute(high_side, axis, forward)  10 us
    pallas_call x1, Pallas kernels, finish(): pl.pallas_call(finish_kernel, name='finish', grid=(2, 32 // FRB), in_spec...  7.68 us
    pallas_call x1, Pallas kernels, prep(): pl.pallas_call(prep_kernel, name='prep', grid=(2, 32 // PRB), in_specs=[p...  6.99 us
    ppermute x6, waiting for transfers between devices, trade(): lax.ppermute(high_side, axis, forward)  5.94 us
    ppermute x6, starting transfers between devices, trade(): lax.ppermute(low_side, axis, backward)  4.38 us
    pallas_call x1, Pallas kernels, middle(): pl.pallas_call(middle_kernel, name='middle', grid=(1,), in_specs=[pl.Bloc...  3.84 us
  transfers between devices with their start and end apart: 12, of which 10 were waited for; matrix products, arithmetic and copies ran while one was open for 0% of the time, Pallas kernels for 8%

profile of v2, /device:TPU:127, one launch (start us, length us, event | category | flops | bytes accessed | tf_op | source)
XLA Modules:
  0.0 85.6 jit_solution(9126737175723659363)
XLA Ops:
  0.6 0.0 copy-start.10
  0.7 2.0 %rims.1 = (bf16[2,32,512]{2,1,0:T(8,128)(2,1)S(1)}, bf16[2,32,512]{2,1,0:T(8,128)(2,1)S(1)}, bf16[2,32,512]{2,1,0:T(8,128)(2,1)S(1)}, bf16[2,32,512]{2,1,0:T(8,128)(2,1)S(1)}) custom-call(f32[2,32,32,512]{3,2,1,0:T(8,128)} %s_ref.3, f32[2,32,32,512]{3,2,1,0:T(8,128)} %s_ref.3, f32[2,32,32,512]{3,2,1,0:T(8,128)} %s_ref.3, f32[2,32,32,512]{3,2,1,0:T(8,128)} %s_ref.3), custom_call_target="tpu_custom_call" | custom-call | flops 1048576 | bytes 3145728 | tf_op jit(solution)/shard_map/rims/pallas_call | solution.py:48
  2.7 0.1 collective-permute-start
  2.8 1.5 %collective-permute-start.1 = (bf16[2,32,512]{2,1,0:T(8,128)(2,1)S(1)}, bf16[2,32,512]{2,1,0:T(8,128)(2,1)S(1)}, u32[]{:S(2)}, u32[]{:S(2)}) collective-permute-start(bf16[2,32,512]{2,1,0:T(8,128)(2,1)S(1)} %get-tuple-element.21), channel_id=1, source_target_pairs={{0,240},{16,0},{32,16},{48,32},{64,48},{80,64},{96,80},{112,96},{1... | collective-permute-start | bytes 196616 | tf_op jit(solution)/shard_map/ppermute | solution.py:380
  4.2 0.1 fusion.1
  4.3 0.1 convert_multiply_fusion
  4.4 1.5 %collective-permute-done.up_ref = bf16[2,32,512]{2,1,0:T(8,128)(2,1)S(1)} collective-permute-done((bf16[2,32,512]{2,1,0:T(8,128)(2,1)S(1)}, bf16[2,32,512]{2,1,0:T(8,128)(2,1)S(1)}, u32[]{:S(2)}, u32[]{:S(2)}) %collective-permute-start) | collective-permute-done | bytes 65568 | tf_op jit(solution)/shard_map/ppermute | solution.py:380
  5.9 3.4 %collective-permute-done.1.down_ref = bf16[2,32,512]{2,1,0:T(8,128)(2,1)S(1)} collective-permute-done((bf16[2,32,512]{2,1,0:T(8,128)(2,1)S(1)}, bf16[2,32,512]{2,1,0:T(8,128)(2,1)S(1)}, u32[]{:S(2)}, u32[]{:S(2)}) %collective-permute-start.1) | collective-permute-done | bytes 65568 | tf_op jit(solution)/shard_map/ppermute | solution.py:380
  9.3 4.6 %collective-permute-start.2 = (bf16[2,34,512]{2,1,0:T(8,128)(2,1)S(1)}, bf16[2,34,512]{2,1,0:T(8,128)(2,1)S(1)}, u32[]{:S(2)}, u32[]{:S(2)}) collective-permute-start(bf16[2,34,512]{2,1,0:T(8,128)(2,1)S(1)} %pad_maximum_fusion), channel_id=1, source_target_pairs={{0,1},{1,2},{2,3},{3,4},{4,5},{5,6},{6,7},{7,8},{8,9},{9,10},{10,1... | collective-permute-start | bytes 208904 | tf_op jit(solution)/shard_map/ppermute | solution.py:380
  14.0 0.0 collective-permute-start.3
  14.0 7.0 %prep.1 = (bf16[2,32,32,512]{3,2,1,0:T(8,128)(2,1)S(1)}, bf16[2,32,32,512]{3,2,1,0:T(8,128)(2,1)S(1)}, f32[2,8,8,512]{3,2,1,0:T(8,128)S(1)}) custom-call(f32[2,32,32,512]{3,2,1,0:T(8,128)} %s_ref.3, bf16[3,4,512,512]{3,2,1,0:T(8,128)(2,1)} %w_ref.5, f32[3,512]{1,0:T(4,128)S(1)} %copy-done.2), custom_call_target="tpu_custom_call" | custom-call | flops 2147483648 | bytes 10485760 | tf_op jit(solution)/shard_map/prep/pallas_call | solution.py:76
  21.0 0.0 copy-start.7
  21.0 2.2 %broadcast_in_dim.2.mask_ref = bf16[8,32,32,128]{3,2,1,0:T(8,128)(2,1)} broadcast(bf16[8,32,32]{2,1,0:T(8,128)(2,1)S(1)} %convert_multiply_fusion), dimensions={0,1,2} | broadcast | bytes 2113536 | tf_op jit(solution)/shard_map/broadcast_in_dim | solution.py:399
  23.3 0.0 copy-start.5
  23.3 21.1 %edge.1 = (bf16[2,32,32,512]{3,2,1,0:T(8,128)(2,1)}, f32[128,512]{1,0:T(8,128)S(1)}, bf16[16,512]{1,0:T(8,128)(2,1)S(1)}, bf16[16,512]{1,0:T(8,128)(2,1)S(1)}, b...) custom-call(bf16[2,32,32,512]{3,2,1,0:T(8,128)(2,1)S(1)} %get-tuple-element.18.r_ref, ...), custom_call_target="tpu_custom_call" | custom-call | flops 8589934592 | bytes 16777216 | tf_op jit(solution)/shard_map/edge/pallas_call | solution.py:157
  44.4 1.5 %collective-permute-start.5 = (bf16[16,512]{1,0:T(8,128)(2,1)S(1)}, bf16[16,512]{1,0:T(8,128)(2,1)S(1)}, u32[]{:S(2)}, u32[]{:S(2)}) collective-permute-start(bf16[16,512]{1,0:T(8,128)(2,1)S(1)} %get-tuple-element.28), channel_id=1, source_target_pairs={{0,240},{16,0},{32,16},{48,32},{64,48},{80,64},{96,80},{112,96},{1... | collective-permute-start | bytes 49160 | tf_op jit(solution)/shard_map/ppermute | solution.py:380
  45.9 1.1 %collective-permute-done.4.refs_0_ = bf16[16,512]{1,0:T(8,128)(2,1)S(1)} collective-permute-done((bf16[16,512]{1,0:T(8,128)(2,1)S(1)}, bf16[16,512]{1,0:T(8,128)(2,1)S(1)}, u32[]{:S(2)}, u32[]{:S(2)}) %collective-permute-start.4) | collective-permute-done | bytes 16416 | tf_op jit(solution)/shard_map/ppermute | solution.py:380
  47.0 3.3 %collective-permute-done.5.refs_1_ = bf16[16,512]{1,0:T(8,128)(2,1)S(1)} collective-permute-done((bf16[16,512]{1,0:T(8,128)(2,1)S(1)}, bf16[16,512]{1,0:T(8,128)(2,1)S(1)}, u32[]{:S(2)}, u32[]{:S(2)}) %collective-permute-start.5) | collective-permute-done | bytes 16416 | tf_op jit(solution)/shard_map/ppermute | solution.py:380
  50.3 4.1 %collective-permute-start.6 = (bf16[48,512]{1,0:T(8,128)(2,1)S(1)}, bf16[48,512]{1,0:T(8,128)(2,1)S(1)}, u32[]{:S(2)}, u32[]{:S(2)}) collective-permute-start(bf16[48,512]{1,0:T(8,128)(2,1)S(1)} %get-tuple-element.39), channel_id=1, source_target_pairs={{0,1},{1,2},{2,3},{3,4},{4,5},{5,6},{6,7},{7,8},{8,9},{9,10},{10,1... | collective-permute-start | bytes 147464 | tf_op jit(solution)/shard_map/ppermute | solution.py:380
  54.4 0.1 add_convert_fusion.inner_ref
  54.5 1.1 %collective-permute-done.6.refs_2_ = bf16[48,512]{1,0:T(8,128)(2,1)S(1)} collective-permute-done((bf16[48,512]{1,0:T(8,128)(2,1)S(1)}, bf16[48,512]{1,0:T(8,128)(2,1)S(1)}, u32[]{:S(2)}, u32[]{:S(2)}) %collective-permute-start.6) | collective-permute-done | bytes 49184 | tf_op jit(solution)/shard_map/ppermute | solution.py:380
  55.6 3.5 %collective-permute-done.7.refs_3_ = bf16[48,512]{1,0:T(8,128)(2,1)S(1)} collective-permute-done((bf16[48,512]{1,0:T(8,128)(2,1)S(1)}, bf16[48,512]{1,0:T(8,128)(2,1)S(1)}, u32[]{:S(2)}, u32[]{:S(2)}) %collective-permute-start.7) | collective-permute-done | bytes 49184 | tf_op jit(solution)/shard_map/ppermute | solution.py:380
  59.2 3.8 %middle.1 = (f32[128,512]{1,0:T(8,128)S(1)}, f32[8,512]{1,0:T(8,128)S(1)}, bf16[8,512]{1,0:T(8,128)(2,1)S(1)}) custom-call(f32[2]{0:T(128)S(1)} %add_convert_fusion.inner_ref, f32[128,512]{1,0:T(8,128)S(1)} %get-tuple-element.26.mz_ref, bf16[16,512]{1,0:T(8,128)(2,1)S(1)} %collective-permute-done.4.refs_0_, ...), custom_call_target="tpu_custom_call" | custom-call | flops 805306368 | bytes 5242880 | tf_op jit(solution)/shard_map/middle/pallas_call | solution.py:236
  63.0 0.1 collective-permute-start.8
  63.1 1.4 %collective-permute-start.9 = (bf16[8,512]{1,0:T(8,128)(2,1)S(1)}, bf16[8,512]{1,0:T(8,128)(2,1)S(1)}, u32[]{:S(2)}, u32[]{:S(2)}) collective-permute-start(bf16[8,512]{1,0:T(8,128)(2,1)S(1)} %get-tuple-element.32), channel_id=1, source_target_pairs={{0,240},{16,0},{32,16},{48,32},{64,48},{80,64},{96,80},{112,96},{1... | collective-permute-start | bytes 24584 | tf_op jit(solution)/shard_map/ppermute | solution.py:380
  64.6 1.3 %collective-permute-done.8.refs_0_ = bf16[8,512]{1,0:T(8,128)(2,1)S(1)} collective-permute-done((bf16[8,512]{1,0:T(8,128)(2,1)S(1)}, bf16[8,512]{1,0:T(8,128)(2,1)S(1)}, u32[]{:S(2)}, u32[]{:S(2)}) %collective-permute-start.8) | collective-permute-done | bytes 8224 | tf_op jit(solution)/shard_map/ppermute | solution.py:380
  65.9 3.1 %collective-permute-done.9.refs_1_ = bf16[8,512]{1,0:T(8,128)(2,1)S(1)} collective-permute-done((bf16[8,512]{1,0:T(8,128)(2,1)S(1)}, bf16[8,512]{1,0:T(8,128)(2,1)S(1)}, u32[]{:S(2)}, u32[]{:S(2)}) %collective-permute-start.9) | collective-permute-done | bytes 8224 | tf_op jit(solution)/shard_map/ppermute | solution.py:380
  69.0 1.2 %collective-permute-start.10 = (bf16[24,512]{1,0:T(8,128)(2,1)S(1)}, bf16[24,512]{1,0:T(8,128)(2,1)S(1)}, u32[]{:S(2)}, u32[]{:S(2)}) collective-permute-start(bf16[24,512]{1,0:T(8,128)(2,1)S(1)} %constant_dynamic-update-slice_fusion), channel_id=1, source_target_pairs={{0,1},{1,2},{2,3},{3,4},{4,5},{5,6},{6,7},{7,8},{8,9},{9,10},{10,1... | collective-permute-start | bytes 73736 | tf_op jit(solution)/shard_map/ppermute | solution.py:380
  70.2 0.9 %collective-permute-done.10.refs_2_ = bf16[24,512]{1,0:T(8,128)(2,1)S(1)} collective-permute-done((bf16[24,512]{1,0:T(8,128)(2,1)S(1)}, bf16[24,512]{1,0:T(8,128)(2,1)S(1)}, u32[]{:S(2)}, u32[]{:S(2)}) %collective-permute-start.10) | collective-permute-done | bytes 24608 | tf_op jit(solution)/shard_map/ppermute | solution.py:380
  71.1 3.5 %collective-permute-done.11.refs_3_ = bf16[24,512]{1,0:T(8,128)(2,1)S(1)} collective-permute-done((bf16[24,512]{1,0:T(8,128)(2,1)S(1)}, bf16[24,512]{1,0:T(8,128)(2,1)S(1)}, u32[]{:S(2)}, u32[]{:S(2)}) %collective-permute-start.11) | collective-permute-done | bytes 24608 | tf_op jit(solution)/shard_map/ppermute | solution.py:380
  74.6 3.2 %coarsest.1.spread_ref = f32[2,8,8,512]{3,2,1,0:T(8,128)S(1)} custom-call(f32[2]{0:T(128)S(1)} %add_convert_fusion.inner_ref, f32[8,512]{1,0:T(8,128)S(1)} %get-tuple-element.31.cz_ref, bf16[8,512]{1,0:T(8,128)(2,1)S(1)} %collective-permute-done.8.refs_0_, bf16[8,512]{1,0:T(8,128)(2,1)S(1)} %collective-permute-done.9.refs_1_, ...), custom_call_target="tpu_custom_call" | custom-call | flops 134217728 | bytes 4194304 | tf_op jit(solution)/shard_map/coarsest/pallas_call | solution.py:280
  77.9 7.7 %finish.1 = f32[2,32,32,512]{3,2,1,0:T(8,128)} custom-call(f32[2,32,32,512]{3,2,1,0:T(8,128)} %s_ref.3, bf16[2,32,32,512]{3,2,1,0:T(8,128)(2,1)S(1)} %copy-done, bf16[3,4,512,512]{3,2,1,0:T(8,128)(2,1)} %w_ref.5, f32[2,8,8,512]{3,2,1,0:T(8,128)S(1)} %coarsest.1.spread_ref), custom_call_target="tpu_custom_call" | custom-call | flops 1073741824 | bytes 10485760 | tf_op jit(solution)/shard_map/finish/pallas_call | solution.py:314
  (34 shorter events, 0.1 us)
Async XLA Ops:
  0.6 3.6 %copy-start.10 = (s32[8]{0:T(128)S(1)}, s32[8]{0:T(128)}, u32[]{:S(2)}) copy-start(s32[8]{0:T(128)} %constant.26.clone) | copy-start | bytes 100
  0.6 3.7 %copy-start.8 = (s32[8,32,32]{2,1,0:T(8,128)S(1)}, s32[8,32,32]{2,1,0:T(8,128)}, u32[]{:S(2)}) copy-start(s32[8,32,32]{2,1,0:T(8,128)} %param.16) | copy-start | bytes 98308
  0.7 13.3 %copy-start.2 = (f32[3,512]{1,0:T(4,128)S(1)}, f32[3,512]{1,0:T(4,128)}, u32[]{:S(2)}) copy-start(f32[3,512]{1,0:T(4,128)} %refs_5_.3) | copy-start | bytes 18436
  2.7 3.2 %collective-permute-start = (bf16[2,32,512]{2,1,0:T(8,128)(2,1)S(1)}, bf16[2,32,512]{2,1,0:T(8,128)(2,1)S(1)}, u32[]{:S(2)}, u32[]{:S(2)}) collective-permute-start(bf16[2,32,512]{2,1,0:T(8,128)(2,1)S(1)} %get-tuple-element.20), channel_id=1, source_target_pairs={{0,16},{16,32},{32,48},{48,64},{64,80},{80,96},{96,112},{112,128},... | collective-permute-start | bytes 196616 | tf_op jit(solution)/shard_map/ppermute | solution.py:380
  2.8 6.5 %collective-permute-start.1 = (bf16[2,32,512]{2,1,0:T(8,128)(2,1)S(1)}, bf16[2,32,512]{2,1,0:T(8,128)(2,1)S(1)}, u32[]{:S(2)}, u32[]{:S(2)}) collective-permute-start(bf16[2,32,512]{2,1,0:T(8,128)(2,1)S(1)} %get-tuple-element.21), channel_id=1, source_target_pairs={{0,240},{16,0},{32,16},{48,32},{64,48},{80,64},{96,80},{112,96},{1... | collective-permute-start | bytes 196616 | tf_op jit(solution)/shard_map/ppermute | solution.py:380
  9.3 11.7 %collective-permute-start.2 = (bf16[2,34,512]{2,1,0:T(8,128)(2,1)S(1)}, bf16[2,34,512]{2,1,0:T(8,128)(2,1)S(1)}, u32[]{:S(2)}, u32[]{:S(2)}) collective-permute-start(bf16[2,34,512]{2,1,0:T(8,128)(2,1)S(1)} %pad_maximum_fusion), channel_id=1, source_target_pairs={{0,1},{1,2},{2,3},{3,4},{4,5},{5,6},{6,7},{7,8},{8,9},{9,10},{10,1... | collective-permute-start | bytes 208904 | tf_op jit(solution)/shard_map/ppermute | solution.py:380
  14.0 7.1 %collective-permute-start.3 = (bf16[2,34,512]{2,1,0:T(8,128)(2,1)S(1)}, bf16[2,34,512]{2,1,0:T(8,128)(2,1)S(1)}, u32[]{:S(2)}, u32[]{:S(2)}) collective-permute-start(bf16[2,34,512]{2,1,0:T(8,128)(2,1)S(1)} %pad_maximum_fusion.1), channel_id=1, source_target_pairs={{0,15},{1,0},{2,1},{3,2},{4,3},{5,4},{6,5},{7,6},{8,7},{9,8},{10,9... | collective-permute-start | bytes 208904 | tf_op jit(solution)/shard_map/ppermute | solution.py:380
  21.0 2.3 %copy-start.6 = (f32[2,8,8,512]{3,2,1,0:T(8,128)S(1)}, f32[2,8,8,512]{3,2,1,0:T(8,128)}, u32[]{:S(2)}) copy-start(f32[2,8,8,512]{3,2,1,0:T(8,128)} %mid_ref.1) | copy-start | bytes 786436
  21.0 2.3 %copy-start.7 = (bf16[64,128]{1,0:T(8,128)(2,1)S(1)}, bf16[64,128]{1,0:T(8,128)(2,1)}, u32[]{:S(2)}) copy-start(bf16[64,128]{1,0:T(8,128)(2,1)} %constant.27.clone.pick_ref) | copy-start | bytes 49156
  23.3 31.3 %copy-start.9 = (f32[2,2,2,512]{3,2,1,0:T(2,128)S(1)}, f32[2,2,2,512]{3,2,1,0:T(2,128)}, u32[]{:S(2)}) copy-start(f32[2,2,2,512]{3,2,1,0:T(2,128)} %param.15) | copy-start | bytes 49156
  23.3 35.9 %copy-start.1 = (bf16[1024,256]{1,0:T(8,128)(2,1)S(1)}, bf16[1024,256]{1,0:T(8,128)(2,1)}, u32[]{:S(2)}) copy-start(bf16[1024,256]{1,0:T(8,128)(2,1)} %constant.28.clone.refs_8_) | copy-start | bytes 1572868
  23.3 35.9 %copy-start.5 = (f32[8,128]{1,0:T(8,128)S(1)}, f32[8,128]{1,0:T(8,128)}, u32[]{:S(2)}) copy-start(f32[8,128]{1,0:T(8,128)} %constant.29.clone.refs_9_) | copy-start | bytes 12292
  44.4 2.6 %collective-permute-start.4 = (bf16[16,512]{1,0:T(8,128)(2,1)S(1)}, bf16[16,512]{1,0:T(8,128)(2,1)S(1)}, u32[]{:S(2)}, u32[]{:S(2)}) collective-permute-start(bf16[16,512]{1,0:T(8,128)(2,1)S(1)} %get-tuple-element.27), channel_id=1, source_target_pairs={{0,16},{16,32},{32,48},{48,64},{64,80},{80,96},{96,112},{112,128},... | collective-permute-start | bytes 49160 | tf_op jit(solution)/shard_map/ppermute | solution.py:380
  44.4 5.9 %collective-permute-start.5 = (bf16[16,512]{1,0:T(8,128)(2,1)S(1)}, bf16[16,512]{1,0:T(8,128)(2,1)S(1)}, u32[]{:S(2)}, u32[]{:S(2)}) collective-permute-start(bf16[16,512]{1,0:T(8,128)(2,1)S(1)} %get-tuple-element.28), channel_id=1, source_target_pairs={{0,240},{16,0},{32,16},{48,32},{64,48},{80,64},{96,80},{112,96},{1... | collective-permute-start | bytes 49160 | tf_op jit(solution)/shard_map/ppermute | solution.py:380
  50.3 5.3 %collective-permute-start.6 = (bf16[48,512]{1,0:T(8,128)(2,1)S(1)}, bf16[48,512]{1,0:T(8,128)(2,1)S(1)}, u32[]{:S(2)}, u32[]{:S(2)}) collective-permute-start(bf16[48,512]{1,0:T(8,128)(2,1)S(1)} %get-tuple-element.39), channel_id=1, source_target_pairs={{0,1},{1,2},{2,3},{3,4},{4,5},{5,6},{6,7},{7,8},{8,9},{9,10},{10,1... | collective-permute-start | bytes 147464 | tf_op jit(solution)/shard_map/ppermute | solution.py:380
  54.4 4.7 %collective-permute-start.7 = (bf16[48,512]{1,0:T(8,128)(2,1)S(1)}, bf16[48,512]{1,0:T(8,128)(2,1)S(1)}, u32[]{:S(2)}, u32[]{:S(2)}) collective-permute-start(bf16[48,512]{1,0:T(8,128)(2,1)S(1)} %get-tuple-element.38), channel_id=1, source_target_pairs={{0,15},{1,0},{2,1},{3,2},{4,3},{5,4},{6,5},{7,6},{8,7},{9,8},{10,9... | collective-permute-start | bytes 147464 | tf_op jit(solution)/shard_map/ppermute | solution.py:380
  59.2 15.5 %copy-start.3 = (bf16[128,16]{1,0:T(8,128)(2,1)S(1)}, bf16[128,16]{1,0:T(8,128)(2,1)}, u32[]{:S(2)}) copy-start(bf16[128,16]{1,0:T(8,128)(2,1)} %constant.31.clone.refs_10_) | copy-start | bytes 12292
  59.2 15.5 %copy-start.4 = (bf16[64,128]{1,0:T(8,128)(2,1)S(1)}, bf16[64,128]{1,0:T(8,128)(2,1)}, u32[]{:S(2)}) copy-start(bf16[64,128]{1,0:T(8,128)(2,1)} %constant.30.clone.refs_9_) | copy-start | bytes 49156
  63.0 2.9 %collective-permute-start.8 = (bf16[8,512]{1,0:T(8,128)(2,1)S(1)}, bf16[8,512]{1,0:T(8,128)(2,1)S(1)}, u32[]{:S(2)}, u32[]{:S(2)}) collective-permute-start(bf16[8,512]{1,0:T(8,128)(2,1)S(1)} %get-tuple-element.32), channel_id=1, source_target_pairs={{0,16},{16,32},{32,48},{48,64},{64,80},{80,96},{96,112},{112,128},... | collective-permute-start | bytes 24584 | tf_op jit(solution)/shard_map/ppermute | solution.py:380
  63.1 5.9 %collective-permute-start.9 = (bf16[8,512]{1,0:T(8,128)(2,1)S(1)}, bf16[8,512]{1,0:T(8,128)(2,1)S(1)}, u32[]{:S(2)}, u32[]{:S(2)}) collective-permute-start(bf16[8,512]{1,0:T(8,128)(2,1)S(1)} %get-tuple-element.32), channel_id=1, source_target_pairs={{0,240},{16,0},{32,16},{48,32},{64,48},{80,64},{96,80},{112,96},{1... | collective-permute-start | bytes 24584 | tf_op jit(solution)/shard_map/ppermute | solution.py:380
  69.0 2.1 %collective-permute-start.10 = (bf16[24,512]{1,0:T(8,128)(2,1)S(1)}, bf16[24,512]{1,0:T(8,128)(2,1)S(1)}, u32[]{:S(2)}, u32[]{:S(2)}) collective-permute-start(bf16[24,512]{1,0:T(8,128)(2,1)S(1)} %constant_dynamic-update-slice_fusion), channel_id=1, source_target_pairs={{0,1},{1,2},{2,3},{3,4},{4,5},{5,6},{6,7},{7,8},{8,9},{9,10},{10,1... | collective-permute-start | bytes 73736 | tf_op jit(solution)/shard_map/ppermute | solution.py:380
  70.2 4.5 %collective-permute-start.11 = (bf16[24,512]{1,0:T(8,128)(2,1)S(1)}, bf16[24,512]{1,0:T(8,128)(2,1)S(1)}, u32[]{:S(2)}, u32[]{:S(2)}) collective-permute-start(bf16[24,512]{1,0:T(8,128)(2,1)S(1)} %constant_dynamic-update-slice_fusion), channel_id=1, source_target_pairs={{0,15},{1,0},{2,1},{3,2},{4,3},{5,4},{6,5},{7,6},{8,7},{9,8},{10,9... | collective-permute-start | bytes 73736 | tf_op jit(solution)/shard_map/ppermute | solution.py:380
  74.6 3.3 %copy-start = (bf16[2,32,32,512]{3,2,1,0:T(8,128)(2,1)S(1)}, bf16[2,32,32,512]{3,2,1,0:T(8,128)(2,1)}, u32[]{:S(2)}) copy-start(bf16[2,32,32,512]{3,2,1,0:T(8,128)(2,1)} %get-tuple-element.17.avg_ref) | copy-start | bytes 6291460

commit v3 on v2

v3 whole, which is shorter than its diff:
```python
import functools
import jax
import jax.numpy as jnp
import numpy as np
from jax import lax
from jax.experimental import pallas as pl
from jax.experimental.pallas import tpu as pltpu
from jax.sharding import PartitionSpec as P

D = 512
ANY = pl.BlockSpec(memory_space=pl.ANY)
BF = jnp.bfloat16
F32 = jnp.float32
OFFS = ((-1, -1), (-1, 0), (-1, 1), (0, -1), (0, 1), (1, -1), (1, 0), (1, 1))
PRB = 8
EDGE_VMEM = 28
RB = 8
EDGE_VMEM = 28


def mm(a, b):
    return jnp.dot(a, b, preferred_element_type=F32)


def gate(half):
    return half + half * jnp.tanh(half)


def pool_rows(x, g, tmp):
    tall = (x[4 * g] + x[4 * g + 1]) + (x[4 * g + 2] + x[4 * g + 3])
    parts = []
    for lane in range(4):
        tmp[g, lane] = tall[:, lane * 128:(lane + 1) * 128]
        part = tmp[g, lane, pl.ds(0, 8, stride=4), :]
        for t in range(1, 4):
            part = part + tmp[g, lane, pl.ds(t, 8, stride=4), :]
        parts.append(part)
    return jnp.concatenate(parts, axis=1)


def rims_kernel(top_ref, bottom_ref, west_ref, east_ref, top_out, bottom_out, west_out, east_out):
    top_out[...] = top_ref[...].reshape(2, 32, D).astype(BF)
    bottom_out[...] = bottom_ref[...].reshape(2, 32, D).astype(BF)
    for b in range(2):
        west_out[b] = west_ref[b, :, 0, :].astype(BF)
        east_out[b] = east_ref[b, :, 7, :].astype(BF)


def rims(fine):
    out = pl.BlockSpec((2, 32, D), lambda i: (0, 0, 0))
    return pl.pallas_call(
        rims_kernel,
        name="rims",
        grid=(1,),
        in_specs=[
            pl.BlockSpec((2, 1, 32, D), lambda i: (0, 0, 0, 0)),
            pl.BlockSpec((2, 1, 32, D), lambda i: (0, 31, 0, 0)),
            pl.BlockSpec((2, 32, 8, D), lambda i: (0, 0, 0, 0)),
            pl.BlockSpec((2, 32, 8, D), lambda i: (0, 0, 3, 0)),
        ],
        out_specs=[out] * 4,
        out_shape=[jax.ShapeDtypeStruct((2, 32, D), BF)] * 4,
        compiler_params=pltpu.CompilerParams(vmem_limit_bytes=24 << 20),
        cost_estimate=pl.CostEstimate(flops=1 << 20, bytes_accessed=3 << 20, transcendentals=0),
    )(fine, fine, fine, fine)


def prep_kernel(s_hbm, w_hbm, c_ref, rt_out, s_ref, w_ref, sems, w_sem):
    weights = pltpu.make_async_copy(w_hbm.at[0, 0:2], w_ref, w_sem)
    weights.start()
    copies = []
    for n in range(8):
        at = (n // 4, pl.ds(8 * (n % 4), 8))
        copies.append(pltpu.make_async_copy(s_hbm.at[at], s_ref.at[n], sems.at[n]))
        copies[-1].start()
    weights.wait()
    for n in range(8):
        copies[n].wait()
        b, i = n // 4, n % 4
        x = s_ref[n]
        op = x.reshape(256, D).astype(BF)
        rt_out[0, b, 8 * i:8 * i + 8] = (0.5 * (mm(op, w_ref[0]) + c_ref[0:1, :])).astype(BF).reshape(8, 32, D)
        rt_out[1, b, 8 * i:8 * i + 8] = (0.5 * mm(op, w_ref[1])).astype(BF).reshape(8, 32, D)


def prep(fine, pw, pb):
    full4 = lambda *shape: pl.BlockSpec(shape, lambda i: (0,) * len(shape))
    return pl.pallas_call(
        prep_kernel,
        name="prep",
        grid=(1,),
        in_specs=[ANY, ANY, full4(3, D)],
        out_specs=full4(2, 2, 32, 32, D),
        out_shape=pltpu.VMEM((2, 2, 32, 32, D), BF),
        scratch_shapes=[
            pltpu.VMEM((8, 8, 32, D), F32),
            pltpu.VMEM((2, D, D), BF),
            pltpu.SemaphoreType.DMA((8,)),
            pltpu.SemaphoreType.DMA,
        ],
        compiler_params=pltpu.CompilerParams(vmem_limit_bytes=24 << 20),
        cost_estimate=pl.CostEstimate(flops=2 * 2 * 2048 * D * D, bytes_accessed=5 << 20, transcendentals=0),
    )(fine, pw, pb)


def edge_kernel(rt_ref, up_ref, down_ref, left_ref, right_ref,
                live_ref, w_ref, b0_ref, mid_ref, pick_ref, s_ref, pw_hbm, bw_hbm,
                avg_out, one_out, mz_out, *rest):
    rim_outs, (w1_out, w2_out, b1_out, b23_out, sh, hs, tmp, pa, hid, w2_half, sems) = rest[:4], rest[4:]
    b = pl.program_id(0)
    blk = pl.program_id(1)

    ahead = [
        pltpu.make_async_copy(pw_hbm.at[1], w1_out, sems.at[0]),
        pltpu.make_async_copy(pw_hbm.at[2], w2_out, sems.at[1]),
        pltpu.make_async_copy(bw_hbm.at[1], b1_out, sems.at[2]),
        pltpu.make_async_copy(bw_hbm.at[2:4], b23_out, sems.at[3]),
    ]

    @pl.when((b == 0) & (blk == 0))
    def _():
        for copy in ahead:
            copy.start()
        w2_half[...] = (w_ref[0, 2].astype(F32) * 0.5).astype(BF)

    @pl.when(blk == 0)
    def _():
        for n, ref in enumerate((up_ref, down_ref, left_ref, right_ref)):
            hs[n, 0:ref.shape[1], :] = (0.5 * mm(ref[0], w_ref[0, 1])).astype(BF).astype(F32)
        rows = lax.broadcasted_iota(jnp.int32, (32, D), 0)

        def put(i, x, left, right):
            sh[1, i] = x.astype(BF)
            sh[0, i] = jnp.where(rows == 0, jnp.broadcast_to(left, (32, D)), pltpu.roll(x, 1, 0)).astype(BF)
            sh[2, i] = jnp.where(rows == 31, jnp.broadcast_to(right, (32, D)), pltpu.roll(x, 31, 0)).astype(BF)

        put(0, hs[0, 0:32, :], hs[2, 32:33, :], hs[3, 32:33, :])
        put(33, hs[1, 0:32, :], hs[2, 33:34, :], hs[3, 33:34, :])

        @pl.loop(0, 32)
        def _(i):
            put(i + 1, rt_ref[1, b, i].astype(F32), hs[2, pl.ds(i, 1), :], hs[3, pl.ds(i, 1), :])

    row0 = blk * RB
    rv = rt_ref[0, b, pl.ds(row0, RB)].reshape(RB * 32, D)
    live = live_ref[...].reshape(RB * 32, 8)
    span = RB * 32
    for k, (p, q) in enumerate(OFFS):
        sv = sh[q + 1, pl.ds(row0 + 1 + p, RB)].reshape(span, D)
        m = jnp.broadcast_to(live[:, k:k + 1], (span, 128)).astype(BF)
        hid[k * span:(k + 1) * span] = gate(rv + sv) * jnp.concatenate([m] * 4, axis=1)
    msg = gate(mm(hid[...], w2_half[...])).reshape(8, span, D)
    avg = (jnp.sum(msg, axis=0) * 0.125).astype(BF)
    avg_out[0] = avg.reshape(RB, 32, D)
    one = s_ref[0] + mm(avg, w_ref[0, 3]).reshape(RB, 32, D)
    one_out[0] = one
    for g in range(RB // 4):
        pa[b, blk * (RB // 4) + g] = pool_rows(one, g, tmp)

    @pl.when((b == 1) & (blk == 32 // RB - 1))
    def _():
        pooled = (pa[...].reshape(128, D) * 0.0625).astype(BF)
        mz = mid_ref[...].reshape(128, D) + gate(0.5 * mm(pooled, b0_ref[0]))
        mz_out[...] = mz
        rims = mm(pick_ref[...], mz.astype(BF)).astype(BF)
        for d in range(4):
            rim_outs[d][...] = rims[16 * d:16 * d + 16]
        for copy in ahead:
            copy.wait()


def edge(rt, rim, mask, pw, bw, mid, pick, fine):
    whole = lambda *shape: pl.BlockSpec(shape, lambda b, i: (0,) * len(shape))
    return pl.pallas_call(
        edge_kernel,
        name="edge",
        grid=(2, 32 // RB),
        in_specs=[
            VM,
        ]
        + [pl.BlockSpec((1, 32, D), lambda b, i: (b, 0, 0))] * 2
        + [pl.BlockSpec((1, 34, D), lambda b, i: (b, 0, 0))] * 2
        + [
            pl.BlockSpec((RB, 32, 8), lambda b, i: (i, 0, 0)),
            whole(1, 4, D, D),
            whole(1, D, D),
            whole(2, 8, 8, D),
            whole(64, 128),
            pl.BlockSpec((1, RB, 32, D), lambda b, i: (b, i, 0, 0)),
            ANY,
            ANY,
        ],
        out_specs=[
            pl.BlockSpec((1, RB, 32, D), lambda b, i: (b, i, 0, 0)),
            pl.BlockSpec((1, RB, 32, D), lambda b, i: (b, i, 0, 0)),
            whole(128, D),
        ]
        + [whole(16, D)] * 4
        + [pl.BlockSpec(memory_space=pltpu.VMEM)] * 4,
        out_shape=[
            jax.ShapeDtypeStruct((2, 32, 32, D), BF),
            jax.ShapeDtypeStruct((2, 32, 32, D), F32),
            jax.ShapeDtypeStruct((128, D), F32),
        ]
        + [jax.ShapeDtypeStruct((16, D), BF)] * 4
        + [
            pltpu.VMEM((4, D, D), BF),
            pltpu.VMEM((4, D, D), BF),
            pltpu.VMEM((D, D), BF),
            pltpu.VMEM((2, D, D), BF),
        ],
        scratch_shapes=[
            pltpu.VMEM((3, 34, 32, D), BF),
            pltpu.VMEM((4, 40, D), F32),
            pltpu.VMEM((8, 4, 32, 128), F32),
            pltpu.VMEM((2, 8, 8, D), F32),
            pltpu.VMEM((8 * RB * 32, D), BF),
            pltpu.VMEM((D, D), BF),
            pltpu.SemaphoreType.DMA((4,)),
        ],
        compiler_params=pltpu.CompilerParams(vmem_limit_bytes=EDGE_VMEM << 20),
        cost_estimate=pl.CostEstimate(flops=2 * 8 * 2048 * D * D, bytes_accessed=16 << 20, transcendentals=16 << 20),
    )(rt, *rim, mask, pw, bw, mid, pick, fine, pw, bw)


def live_sides(first, last):
    at, count = lax.axis_index("lat"), lax.axis_size("lat")
    up = jnp.where(at > 0, 1.0, 0.0).astype(F32)
    down = jnp.where(at < count - 1, 1.0, 0.0).astype(F32)
    return jnp.where(first, up, 1.0), jnp.where(last, down, 1.0)


def middle_kernel(mz_ref, *refs):
    rim_refs = refs[:4]
    w_ref, c_ref, b1_ref, coarse_ref, gather_ref, mean_ref, mo_out, cz_out, czb_out, flat = refs[4:]
    for n in range(4):
        flat[2 * n:2 * n + 2, :] = coarse_ref[n // 2, n % 2]
    mz = mz_ref[...]
    own = mz.astype(BF)
    recv = 0.5 * (mm(own, w_ref[0]) + c_ref[1:2, :])
    states = jnp.concatenate([own] + [ref[...] for ref in rim_refs], axis=0)
    send = (0.5 * mm(states, w_ref[1])).astype(BF)
    near = mm(gather_ref[...], send)
    hidden = gate(near.reshape(8, 128, D) + recv[None]).astype(BF).reshape(1024, D)
    msg = gate(0.5 * mm(hidden, w_ref[2])).reshape(8, 128, D)
    lat = (lax.broadcasted_iota(jnp.int32, (128, D), 0) // 8) % 8
    up, down = live_sides(lat == 0, lat == 7)
    total = up * (msg[0] + msg[1] + msg[2]) + (msg[3] + msg[4]) + down * (msg[5] + msg[6] + msg[7])
    avg = (0.125 * total).astype(BF)
    mo = mz + mm(avg, w_ref[3])
    mo_out[...] = mo
    pooled = jnp.dot(mean_ref[...], mo, preferred_element_type=F32, precision=lax.Precision.HIGHEST)
    cz = flat[...] + gate(0.5 * mm(pooled.astype(BF), b1_ref[...]))
    cz_out[...] = cz
    czb_out[...] = cz.astype(BF)


VM = pl.BlockSpec(memory_space=pltpu.VMEM)


def full(*shape):
    return pl.BlockSpec(shape, lambda i: (0,) * len(shape))


def middle(mz, rim, pw, pb, bw, coarse, gather, mean):
    return pl.pallas_call(
        middle_kernel,
        name="middle",
        grid=(1,),
        in_specs=[full(128, D)]
        + [full(16, D)] * 2
        + [full(48, D)] * 2
        + [VM, full(3, D), VM, full(2, 2, 2, D), full(1024, 256), full(8, 128)],
        out_specs=[full(128, D), full(8, D), full(8, D)],
        out_shape=[
            jax.ShapeDtypeStruct((128, D), F32),
            jax.ShapeDtypeStruct((8, D), F32),
            jax.ShapeDtypeStruct((8, D), BF),
        ],
        scratch_shapes=[pltpu.VMEM((8, D), F32)],
        compiler_params=pltpu.CompilerParams(vmem_limit_bytes=24 << 20),
        cost_estimate=pl.CostEstimate(flops=2 * 12 * 128 * D * D, bytes_accessed=5 << 20, transcendentals=1 << 20),
    )(mz, *rim, pw, pb, bw, coarse, gather, mean)


def coarse_kernel(cz_ref, *refs):
    rim_refs = refs[:4]
    w_ref, c_ref, b23_ref, mo_ref, gather_ref, lift_ref, one_hbm, out_hbm, buf, sems = refs[4:]
    loads = []
    for n in range(8):
        at = (n // 4, pl.ds(8 * (n % 4), 8))
        loads.append(pltpu.make_async_copy(one_hbm.at[at], buf.at[n], sems.at[n, 0]))
        loads[-1].start()
    cz = cz_ref[...]
    own = cz.astype(BF)
    recv = 0.5 * (mm(own, w_ref[0]) + c_ref[2:3, :])
    pieces = [cz] + [ref[...].astype(F32) for ref in rim_refs] + [jnp.zeros((56, D), F32)]
    send = (0.5 * mm(jnp.concatenate(pieces, axis=0).astype(BF), w_ref[1])).astype(BF)
    near = mm(gather_ref[...], send)
    hidden = gate(near.reshape(8, 8, D) + recv[None]).astype(BF).reshape(64, D)
    msg = gate(0.5 * mm(hidden, w_ref[2])).reshape(8, 8, D)
    lat = (lax.broadcasted_iota(jnp.int32, (8, D), 0) // 2) % 2
    up, down = live_sides(lat == 0, lat == 1)
    total = up * (msg[0] + msg[1] + msg[2]) + (msg[3] + msg[4]) + down * (msg[5] + msg[6] + msg[7])
    avg = (0.125 * total).astype(BF)
    co = cz + mm(avg, w_ref[3])
    lifted = gate(0.5 * mm(co.astype(BF), b23_ref[0]))
    high = lifted.astype(BF).astype(F32)
    both = jnp.concatenate([high, lifted - high], axis=0).astype(BF)
    two = mo_ref[...] + mm(lift_ref[...], both)
    spread = gate(0.5 * mm(two.astype(BF), b23_ref[1])).reshape(16, 8, D)
    first = lax.broadcasted_iota(jnp.int32, (8, D), 0) < 4
    copies = []
    for n in range(8):
        loads[n].wait()
        for g in range(2):
            parts = []
            for t in range(4):
                low = jnp.broadcast_to(spread[2 * n + g, 2 * t:2 * t + 1, :], (8, D))
                high = jnp.broadcast_to(spread[2 * n + g, 2 * t + 1:2 * t + 2, :], (8, D))
                parts.append(jnp.where(first, low, high))
            wide = jnp.concatenate(parts, axis=0)
            for i in range(4 * g, 4 * g + 4):
                buf[n, i] = buf[n, i] + wide
        copies.append(pltpu.make_async_copy(buf.at[n], out_hbm.at[n // 4, pl.ds(8 * (n % 4), 8)], sems.at[n, 1]))
        copies[-1].start()
    for copy in copies:
        copy.wait()


def coarsest(cz, rim, pw, pb, bw, mo, gather, lift, one):
    return pl.pallas_call(
        coarse_kernel,
        name="coarsest",
        grid=(1,),
        in_specs=[full(8, D)]
        + [full(8, D)] * 2
        + [full(24, D)] * 2
        + [VM, full(3, D), VM, full(128, D), full(64, 128), full(128, 16), ANY],
        out_specs=ANY,
        out_shape=jax.ShapeDtypeStruct((2, 32, 32, D), F32),
        scratch_shapes=[pltpu.VMEM((8, 8, 32, D), F32), pltpu.SemaphoreType.DMA((8, 2))],
        compiler_params=pltpu.CompilerParams(vmem_limit_bytes=24 << 20),
        cost_estimate=pl.CostEstimate(flops=2 * 2 * 128 * D * D, bytes_accessed=4 << 20, transcendentals=1 << 18),
    )(cz, *rim, pw, pb, bw, mo, gather, lift, one)


def place_middle():
    pick = np.zeros((64, 128), np.float32)
    for b in range(2):
        for n in range(8):
            for d, (i, j) in enumerate(((0, n), (7, n), (n, 0), (n, 7))):
                pick[16 * d + 8 * b + n, 64 * b + 8 * i + j] = 1
    gather = np.zeros((1024, 256), np.float32)
    for k, (p, q) in enumerate(OFFS):
        for b in range(2):
            for i in range(8):
                for j in range(8):
                    y, x = i + p, j + q
                    if 0 <= x < 8:
                        n = 128 + 8 * b + x if y < 0 else 144 + 8 * b + x if y > 7 else 64 * b + 8 * y + x
                    else:
                        base = 160 + 8 * b if x < 0 else 208 + 8 * b
                        n = base + 16 + x % 8 if y < 0 else base + 32 + x % 8 if y > 7 else base + y
                    gather[128 * k + 64 * b + 8 * i + j, n] = 1
    mean = np.zeros((8, 128), np.float32)
    for b in range(2):
        for i in range(8):
            for j in range(8):
                mean[4 * b + 2 * (i // 4) + j // 4, 64 * b + 8 * i + j] = 1 / 16
    return pick, gather, mean


def place_coarse():
    gather = np.zeros((64, 128), np.float32)
    for k, (p, q) in enumerate(OFFS):
        for b in range(2):
            for i in range(2):
                for j in range(2):
                    y, x = i + p, j + q
                    base = (24 if x < 0 else 48 if x > 1 else 0) + (8 if y < 0 else 16 if y > 1 else 0)
                    gather[8 * k + 4 * b + 2 * i + j, base + 4 * b + 2 * (y % 2) + x % 2] = 1
    lift = np.zeros((128, 16), np.float32)
    for b in range(2):
        for i in range(8):
            for j in range(8):
                source = 4 * b + 2 * (i // 4) + j // 4
                lift[64 * b + 8 * i + j, source] = 1
                lift[64 * b + 8 * i + j, 8 + source] = 1
    return gather, lift


def trade(low_side, high_side, axis):
    count = lax.axis_size(axis)
    forward = [(i, (i + 1) % count) for i in range(count)]
    backward = [(i, (i - 1) % count) for i in range(count)]
    return lax.ppermute(high_side, axis, forward), lax.ppermute(low_side, axis, backward)


def local(fine, mid, coarse, flags, pw, bw, pb):
    fine, pw, bw = (pltpu.with_memory_space_constraint(a, pltpu.HBM) for a in (fine, pw, bw))
    top, bottom, west, east = rims(fine)
    up, down = trade(top, bottom, "lat")
    left, right = trade(
        jnp.concatenate([west, up[:, :1], down[:, :1]], axis=1),
        jnp.concatenate([east, up[:, 31:], down[:, 31:]], axis=1),
        "lon",
    )
    lat = lax.axis_index("lat")
    rows = lax.axis_size("lat")
    index = jnp.arange(32)
    step = jnp.asarray([p for p, q in OFFS])[:, None]
    where = lat * 32 + index[None, :] + step
    live = flags.astype(F32) * ((where >= 0) & (where < rows * 32)).astype(F32)[:, :, None]
    mask = jnp.transpose(live, (1, 2, 0))
    pick, gather, mean = place_middle()
    gather_c, lift = place_coarse()
    rt = prep(fine, pw, pb)
    avg, one, mz, top, bottom, west, east, w1, w2, b1, b23 = edge(
        rt, (up, down, left, right), mask, pw, bw, mid, jnp.asarray(pick, BF), fine
    )
    one = pltpu.with_memory_space_constraint(one, pltpu.HBM)
    up, down = trade(top, bottom, "lat")
    left, right = trade(jnp.concatenate([west, up, down]), jnp.concatenate([east, up, down]), "lon")
    mo, cz, czb = middle(
        mz, (up, down, left, right), w1, pb, b1, coarse, jnp.asarray(gather, BF), jnp.asarray(mean, F32)
    )
    up, down = trade(czb, czb, "lat")
    column = jnp.concatenate([czb, up, down])
    left, right = trade(column, column, "lon")
    refined = coarsest(
        cz, (up, down, left, right), w2, pb, b23, mo, jnp.asarray(gather_c, BF), jnp.asarray(lift, BF), one
    )
    return refined, avg


def solution(mesh):
    node = P(None, "lat", "lon", None)
    return jax.shard_map(
        local,
        mesh=mesh,
        in_specs=(node, node, node, P(None, "lat", "lon"), P(), P(), P()),
        out_specs=(node, node),
        check_vma=False,
    )
```

time: 86 us -> 77.5 us (0.901)
  the two profiles are of different devices: /device:TPU:127 before, /device:TPU:0 now
where the time goes in v3:
time: 77.5 us; the launch traced here: 77.1 us
  Pallas kernels  34.7 us (45%)
  starting transfers between devices  19.9 us (26%)
  waiting for transfers between devices  19.1 us (25%)
  local copies, waits for them, and re-layouts  2.35 us (3%)
  between operations  0.87 us (1%)
    pallas_call x1, Pallas kernels, edge(): pl.pallas_call(edge_kernel, name='edge', grid=(2, 32 // RB), in_specs=[VM...  20 us
    ppermute x6, starting transfers between devices, trade(): lax.ppermute(low_side, axis, backward)  19.2 us
    ppermute x6, waiting for transfers between devices, trade(): lax.ppermute(high_side, axis, forward)  16.4 us
    pallas_call x1, Pallas kernels, prep(): pl.pallas_call(prep_kernel, name='prep', grid=(1,), in_specs=[ANY, ANY, f...  5.95 us
    pallas_call x1, Pallas kernels, coarsest(): pl.pallas_call(coarse_kernel, name='coarsest', grid=(1,), in_specs=[full(...  4.61 us
    ppermute x6, waiting for transfers between devices, trade(): lax.ppermute(low_side, axis, backward)  2.7 us
    pallas_call x1, Pallas kernels, middle(): pl.pallas_call(middle_kernel, name='middle', grid=(1,), in_specs=[full(12...  2.12 us
    pallas_call x1, Pallas kernels, rims(): pl.pallas_call(rims_kernel, name='rims', grid=(1,), in_specs=[pl.BlockSpe...  2.01 us
  transfers between devices with their start and end apart: 12, of which 7 were waited for; matrix products, arithmetic and copies ran while one was open for 1% of the time, Pallas kernels for 8%

profile of v3, /device:TPU:0, one launch (start us, length us, event | category | flops | bytes accessed | tf_op | source)
XLA Modules:
  0.0 77.1 jit_solution(6347414242267423297)
XLA Ops:
  0.6 0.0 copy-start.10
  0.7 2.0 %rims.1 = (bf16[2,32,512]{2,1,0:T(8,128)(2,1)S(1)}, bf16[2,32,512]{2,1,0:T(8,128)(2,1)S(1)}, bf16[2,32,512]{2,1,0:T(8,128)(2,1)S(1)}, bf16[2,32,512]{2,1,0:T(8,128)(2,1)S(1)}) custom-call(f32[2,32,32,512]{3,2,1,0:T(8,128)} %s_ref.1, f32[2,32,32,512]{3,2,1,0:T(8,128)} %s_ref.1, f32[2,32,32,512]{3,2,1,0:T(8,128)} %s_ref.1, f32[2,32,32,512]{3,2,1,0:T(8,128)} %s_ref.1), custom_call_target="tpu_custom_call" | custom-call | flops 1048576 | bytes 3145728 | tf_op jit(solution)/shard_map/rims/pallas_call | solution.py:51
  2.7 0.1 collective-permute-start
  2.8 5.3 %collective-permute-start.1 = (bf16[2,32,512]{2,1,0:T(8,128)(2,1)S(1)}, bf16[2,32,512]{2,1,0:T(8,128)(2,1)S(1)}, u32[]{:S(2)}, u32[]{:S(2)}) collective-permute-start(bf16[2,32,512]{2,1,0:T(8,128)(2,1)S(1)} %get-tuple-element.21), channel_id=1, source_target_pairs={{0,240},{16,0},{32,16},{48,32},{64,48},{80,64},{96,80},{112,96},{1... | collective-permute-start | bytes 196616 | tf_op jit(solution)/shard_map/ppermute | solution.py:397
  8.1 0.1 fusion.1
  8.2 0.1 copy.16
  8.3 0.2 copy.17
  8.6 1.8 %collective-permute-done.up_ref = bf16[2,32,512]{2,1,0:T(8,128)(2,1)S(1)} collective-permute-done((bf16[2,32,512]{2,1,0:T(8,128)(2,1)S(1)}, bf16[2,32,512]{2,1,0:T(8,128)(2,1)S(1)}, u32[]{:S(2)}, u32[]{:S(2)}) %collective-permute-start) | collective-permute-done | bytes 65568 | tf_op jit(solution)/shard_map/ppermute | solution.py:397
  10.4 0.0 collective-permute-start.2
  10.5 0.0 copy-start.8
  10.5 3.0 %collective-permute-start.3 = (bf16[2,34,512]{2,1,0:T(8,128)(2,1)S(1)}, bf16[2,34,512]{2,1,0:T(8,128)(2,1)S(1)}, u32[]{:S(2)}, u32[]{:S(2)}) collective-permute-start(bf16[2,34,512]{2,1,0:T(8,128)(2,1)S(1)} %pad_maximum_fusion.1), channel_id=1, source_target_pairs={{0,15},{1,0},{2,1},{3,2},{4,3},{5,4},{6,5},{7,6},{8,7},{9,8},{10,9... | collective-permute-start | bytes 208904 | tf_op jit(solution)/shard_map/ppermute | solution.py:397
  13.4 5.9 %prep.1.rt_ref = bf16[2,2,32,32,512]{4,3,2,1,0:T(8,128)(2,1)S(1)} custom-call(f32[2,32,32,512]{3,2,1,0:T(8,128)} %s_ref.1, bf16[3,4,512,512]{3,2,1,0:T(8,128)(2,1)} %pw_hbm.1, f32[3,512]{1,0:T(4,128)S(1)} %copy-done.2), custom_call_target="tpu_custom_call" | custom-call | flops 2147483648 | bytes 5242880 | tf_op jit(solution)/shard_map/prep/pallas_call | solution.py:88
  19.4 0.0 copy-start.1
  19.4 0.0 copy-start.6
  19.4 0.0 copy-start.3
  19.4 0.0 copy-start.5
  19.5 20.0 %edge.1 = (bf16[2,32,32,512]{3,2,1,0:T(8,128)(2,1)}, f32[2,32,32,512]{3,2,1,0:T(8,128)S(1)}, f32[128,512]{1,0:T(8,128)S(1)}, bf16[16,512]{1,0:T(8,128)(2,1)S(1)}...) custom-call(bf16[2,2,32,32,512]{4,3,2,1,0:T(8,128)(2,1)S(1)} %prep.1, ...), custom_call_target="tpu_custom_call" | custom-call | flops 8589934592 | bytes 16777216 | tf_op jit(solution)/shard_map/edge/pallas_call | solution.py:174
  39.5 1.9 %copy-done = f32[2,32,32,512]{3,2,1,0:T(8,128)} copy-done((f32[2,32,32,512]{3,2,1,0:T(8,128)}, f32[2,32,32,512]{3,2,1,0:T(8,128)S(1)}, u32[]{:S(2)}) %copy-start) | copy-done | bytes 4194328
  41.5 5.3 %collective-permute-start.5 = (bf16[16,512]{1,0:T(8,128)(2,1)S(1)}, bf16[16,512]{1,0:T(8,128)(2,1)S(1)}, u32[]{:S(2)}, u32[]{:S(2)}) collective-permute-start(bf16[16,512]{1,0:T(8,128)(2,1)S(1)} %get-tuple-element.26), channel_id=1, source_target_pairs={{0,240},{16,0},{32,16},{48,32},{64,48},{80,64},{96,80},{112,96},{1... | collective-permute-start | bytes 49160 | tf_op jit(solution)/shard_map/ppermute | solution.py:397
  46.8 1.7 %collective-permute-done.4.refs_0_ = bf16[16,512]{1,0:T(8,128)(2,1)S(1)} collective-permute-done((bf16[16,512]{1,0:T(8,128)(2,1)S(1)}, bf16[16,512]{1,0:T(8,128)(2,1)S(1)}, u32[]{:S(2)}, u32[]{:S(2)}) %collective-permute-start.4) | collective-permute-done | bytes 16416 | tf_op jit(solution)/shard_map/ppermute | solution.py:397
  48.5 0.4 collective-permute-start.7
  49.0 0.1 collective-permute-start.6
  49.0 1.7 %collective-permute-done.7.refs_3_ = bf16[48,512]{1,0:T(8,128)(2,1)S(1)} collective-permute-done((bf16[48,512]{1,0:T(8,128)(2,1)S(1)}, bf16[48,512]{1,0:T(8,128)(2,1)S(1)}, u32[]{:S(2)}, u32[]{:S(2)}) %collective-permute-start.7) | collective-permute-done | bytes 49184 | tf_op jit(solution)/shard_map/ppermute | solution.py:397
  50.7 3.0 %collective-permute-done.6.refs_2_ = bf16[48,512]{1,0:T(8,128)(2,1)S(1)} collective-permute-done((bf16[48,512]{1,0:T(8,128)(2,1)S(1)}, bf16[48,512]{1,0:T(8,128)(2,1)S(1)}, u32[]{:S(2)}, u32[]{:S(2)}) %collective-permute-start.6) | collective-permute-done | bytes 49184 | tf_op jit(solution)/shard_map/ppermute | solution.py:397
  53.7 2.1 %middle.1 = (f32[128,512]{1,0:T(8,128)S(1)}, f32[8,512]{1,0:T(8,128)S(1)}, bf16[8,512]{1,0:T(8,128)(2,1)S(1)}) custom-call(f32[128,512]{1,0:T(8,128)S(1)} %get-tuple-element.24.mz_ref, bf16[16,512]{1,0:T(8,128)(2,1)S(1)} %collective-permute-done.4.refs_0_, bf16[16,512]{1,0:T(8,128)(2,1)S(1)} %collective-permute-done.5.refs_1_, ...), custom_call_target="tpu_custom_call" | custom-call | flops 805306368 | bytes 5242880 | tf_op jit(solution)/shard_map/middle/pallas_call | solution.py:266
  55.8 5.1 %collective-permute-start.9 = (bf16[8,512]{1,0:T(8,128)(2,1)S(1)}, bf16[8,512]{1,0:T(8,128)(2,1)S(1)}, u32[]{:S(2)}, u32[]{:S(2)}) collective-permute-start(bf16[8,512]{1,0:T(8,128)(2,1)S(1)} %get-tuple-element.32), channel_id=1, source_target_pairs={{0,240},{16,0},{32,16},{48,32},{64,48},{80,64},{96,80},{112,96},{1... | collective-permute-start | bytes 24584 | tf_op jit(solution)/shard_map/ppermute | solution.py:397
  61.0 7.0 %collective-permute-done.8.refs_0_ = bf16[8,512]{1,0:T(8,128)(2,1)S(1)} collective-permute-done((bf16[8,512]{1,0:T(8,128)(2,1)S(1)}, bf16[8,512]{1,0:T(8,128)(2,1)S(1)}, u32[]{:S(2)}, u32[]{:S(2)}) %collective-permute-start.8) | collective-permute-done | bytes 8224 | tf_op jit(solution)/shard_map/ppermute | solution.py:397
  67.9 0.0 collective-permute-start.11
  68.0 0.5 collective-permute-start.10
  68.5 1.0 %collective-permute-done.11.refs_3_ = bf16[24,512]{1,0:T(8,128)(2,1)S(1)} collective-permute-done((bf16[24,512]{1,0:T(8,128)(2,1)S(1)}, bf16[24,512]{1,0:T(8,128)(2,1)S(1)}, u32[]{:S(2)}, u32[]{:S(2)}) %collective-permute-start.11) | collective-permute-done | bytes 24608 | tf_op jit(solution)/shard_map/ppermute | solution.py:397
  69.5 3.0 %collective-permute-done.10.refs_2_ = bf16[24,512]{1,0:T(8,128)(2,1)S(1)} collective-permute-done((bf16[24,512]{1,0:T(8,128)(2,1)S(1)}, bf16[24,512]{1,0:T(8,128)(2,1)S(1)}, u32[]{:S(2)}, u32[]{:S(2)}) %collective-permute-start.10) | collective-permute-done | bytes 24608 | tf_op jit(solution)/shard_map/ppermute | solution.py:397
  72.4 4.6 %coarsest.1 = f32[2,32,32,512]{3,2,1,0:T(8,128)} custom-call(f32[8,512]{1,0:T(8,128)S(1)} %get-tuple-element.31.cz_ref, bf16[8,512]{1,0:T(8,128)(2,1)S(1)} %collective-permute-done.8.refs_0_, bf16[8,512]{1,0:T(8,128)(2,1)S(1)} %collective-permute-done.9.refs_1_, bf16[24,512]{1,0:T(8,128)(2,1)S(1)} %collective-permute-done.10.refs_2_, ...), custom_call_target="tpu_custom_call" | custom-call | flops 134217728 | bytes 4194304 | tf_op jit(solution)/shard_map/coarsest/pallas_call | solution.py:332
  (33 shorter events, 0.2 us)
Async XLA Ops:
  0.6 7.5 %copy-start.10 = (s32[8]{0:T(128)S(1)}, s32[8]{0:T(128)}, u32[]{:S(2)}) copy-start(s32[8]{0:T(128)} %constant.23.clone) | copy-start | bytes 100
  0.6 7.6 %copy-start.9 = (s32[8,32,32]{2,1,0:T(8,128)S(1)}, s32[8,32,32]{2,1,0:T(8,128)}, u32[]{:S(2)}) copy-start(s32[8,32,32]{2,1,0:T(8,128)} %param.16) | copy-start | bytes 98308
  0.7 12.8 %copy-start.2 = (f32[3,512]{1,0:T(4,128)S(1)}, f32[3,512]{1,0:T(4,128)}, u32[]{:S(2)}) copy-start(f32[3,512]{1,0:T(4,128)} %refs_5_.3) | copy-start | bytes 18436
  2.7 7.7 %collective-permute-start = (bf16[2,32,512]{2,1,0:T(8,128)(2,1)S(1)}, bf16[2,32,512]{2,1,0:T(8,128)(2,1)S(1)}, u32[]{:S(2)}, u32[]{:S(2)}) collective-permute-start(bf16[2,32,512]{2,1,0:T(8,128)(2,1)S(1)} %get-tuple-element.20), channel_id=1, source_target_pairs={{0,16},{16,32},{32,48},{48,64},{64,80},{80,96},{96,112},{112,128},... | collective-permute-start | bytes 196616 | tf_op jit(solution)/shard_map/ppermute | solution.py:397
  2.8 7.6 %collective-permute-start.1 = (bf16[2,32,512]{2,1,0:T(8,128)(2,1)S(1)}, bf16[2,32,512]{2,1,0:T(8,128)(2,1)S(1)}, u32[]{:S(2)}, u32[]{:S(2)}) collective-permute-start(bf16[2,32,512]{2,1,0:T(8,128)(2,1)S(1)} %get-tuple-element.21), channel_id=1, source_target_pairs={{0,240},{16,0},{32,16},{48,32},{64,48},{80,64},{96,80},{112,96},{1... | collective-permute-start | bytes 196616 | tf_op jit(solution)/shard_map/ppermute | solution.py:397
  10.4 9.0 %collective-permute-start.2 = (bf16[2,34,512]{2,1,0:T(8,128)(2,1)S(1)}, bf16[2,34,512]{2,1,0:T(8,128)(2,1)S(1)}, u32[]{:S(2)}, u32[]{:S(2)}) collective-permute-start(bf16[2,34,512]{2,1,0:T(8,128)(2,1)S(1)} %pad_maximum_fusion), channel_id=1, source_target_pairs={{0,1},{1,2},{2,3},{3,4},{4,5},{5,6},{6,7},{7,8},{8,9},{9,10},{10,1... | collective-permute-start | bytes 208904 | tf_op jit(solution)/shard_map/ppermute | solution.py:397
  10.5 9.0 %copy-start.7 = (f32[2,8,8,512]{3,2,1,0:T(8,128)S(1)}, f32[2,8,8,512]{3,2,1,0:T(8,128)}, u32[]{:S(2)}) copy-start(f32[2,8,8,512]{3,2,1,0:T(8,128)} %mid_ref.1) | copy-start | bytes 786436
  10.5 9.0 %copy-start.8 = (bf16[64,128]{1,0:T(8,128)(2,1)S(1)}, bf16[64,128]{1,0:T(8,128)(2,1)}, u32[]{:S(2)}) copy-start(bf16[64,128]{1,0:T(8,128)(2,1)} %constant.24.clone.pick_ref) | copy-start | bytes 49156
  10.5 9.0 %collective-permute-start.3 = (bf16[2,34,512]{2,1,0:T(8,128)(2,1)S(1)}, bf16[2,34,512]{2,1,0:T(8,128)(2,1)S(1)}, u32[]{:S(2)}, u32[]{:S(2)}) collective-permute-start(bf16[2,34,512]{2,1,0:T(8,128)(2,1)S(1)} %pad_maximum_fusion.1), channel_id=1, source_target_pairs={{0,15},{1,0},{2,1},{3,2},{4,3},{5,4},{6,5},{7,6},{8,7},{9,8},{10,9... | collective-permute-start | bytes 208904 | tf_op jit(solution)/shard_map/ppermute | solution.py:397
  19.4 34.3 %copy-start.1 = (bf16[1024,256]{1,0:T(8,128)(2,1)S(1)}, bf16[1024,256]{1,0:T(8,128)(2,1)}, u32[]{:S(2)}) copy-start(bf16[1024,256]{1,0:T(8,128)(2,1)} %constant.25.clone.refs_8_) | copy-start | bytes 1572868
  19.4 34.3 %copy-start.4 = (f32[2,2,2,512]{3,2,1,0:T(2,128)S(1)}, f32[2,2,2,512]{3,2,1,0:T(2,128)}, u32[]{:S(2)}) copy-start(f32[2,2,2,512]{3,2,1,0:T(2,128)} %refs_7_.1) | copy-start | bytes 49156
  19.4 34.3 %copy-start.6 = (f32[8,128]{1,0:T(8,128)S(1)}, f32[8,128]{1,0:T(8,128)}, u32[]{:S(2)}) copy-start(f32[8,128]{1,0:T(8,128)} %constant.26.clone.refs_9_) | copy-start | bytes 12292
  19.4 53.0 %copy-start.3 = (bf16[128,16]{1,0:T(8,128)(2,1)S(1)}, bf16[128,16]{1,0:T(8,128)(2,1)}, u32[]{:S(2)}) copy-start(bf16[128,16]{1,0:T(8,128)(2,1)} %constant.28.clone.refs_9_) | copy-start | bytes 12292
  19.4 53.0 %copy-start.5 = (bf16[64,128]{1,0:T(8,128)(2,1)S(1)}, bf16[64,128]{1,0:T(8,128)(2,1)}, u32[]{:S(2)}) copy-start(bf16[64,128]{1,0:T(8,128)(2,1)} %constant.27.clone.refs_8_) | copy-start | bytes 49156
  39.5 1.9 %copy-start = (f32[2,32,32,512]{3,2,1,0:T(8,128)}, f32[2,32,32,512]{3,2,1,0:T(8,128)S(1)}, u32[]{:S(2)}) copy-start(f32[2,32,32,512]{3,2,1,0:T(8,128)S(1)} %get-tuple-element.36.refs_10_) | copy-start | bytes 12582916
  41.4 7.1 %collective-permute-start.4 = (bf16[16,512]{1,0:T(8,128)(2,1)S(1)}, bf16[16,512]{1,0:T(8,128)(2,1)S(1)}, u32[]{:S(2)}, u32[]{:S(2)}) collective-permute-start(bf16[16,512]{1,0:T(8,128)(2,1)S(1)} %get-tuple-element.25), channel_id=1, source_target_pairs={{0,16},{16,32},{32,48},{48,64},{64,80},{80,96},{96,112},{112,128},... | collective-permute-start | bytes 49160 | tf_op jit(solution)/shard_map/ppermute | solution.py:397
  41.5 7.1 %collective-permute-start.5 = (bf16[16,512]{1,0:T(8,128)(2,1)S(1)}, bf16[16,512]{1,0:T(8,128)(2,1)S(1)}, u32[]{:S(2)}, u32[]{:S(2)}) collective-permute-start(bf16[16,512]{1,0:T(8,128)(2,1)S(1)} %get-tuple-element.26), channel_id=1, source_target_pairs={{0,240},{16,0},{32,16},{48,32},{64,48},{80,64},{96,80},{112,96},{1... | collective-permute-start | bytes 49160 | tf_op jit(solution)/shard_map/ppermute | solution.py:397
  48.5 2.2 %collective-permute-start.7 = (bf16[48,512]{1,0:T(8,128)(2,1)S(1)}, bf16[48,512]{1,0:T(8,128)(2,1)S(1)}, u32[]{:S(2)}, u32[]{:S(2)}) collective-permute-start(bf16[48,512]{1,0:T(8,128)(2,1)S(1)} %get-tuple-element.42), channel_id=1, source_target_pairs={{0,15},{1,0},{2,1},{3,2},{4,3},{5,4},{6,5},{7,6},{8,7},{9,8},{10,9... | collective-permute-start | bytes 147464 | tf_op jit(solution)/shard_map/ppermute | solution.py:397
  49.0 4.7 %collective-permute-start.6 = (bf16[48,512]{1,0:T(8,128)(2,1)S(1)}, bf16[48,512]{1,0:T(8,128)(2,1)S(1)}, u32[]{:S(2)}, u32[]{:S(2)}) collective-permute-start(bf16[48,512]{1,0:T(8,128)(2,1)S(1)} %get-tuple-element.43), channel_id=1, source_target_pairs={{0,1},{1,2},{2,3},{3,4},{4,5},{5,6},{6,7},{7,8},{8,9},{9,10},{10,1... | collective-permute-start | bytes 147464 | tf_op jit(solution)/shard_map/ppermute | solution.py:397
  55.8 12.1 %collective-permute-start.9 = (bf16[8,512]{1,0:T(8,128)(2,1)S(1)}, bf16[8,512]{1,0:T(8,128)(2,1)S(1)}, u32[]{:S(2)}, u32[]{:S(2)}) collective-permute-start(bf16[8,512]{1,0:T(8,128)(2,1)S(1)} %get-tuple-element.32), channel_id=1, source_target_pairs={{0,240},{16,0},{32,16},{48,32},{64,48},{80,64},{96,80},{112,96},{1... | collective-permute-start | bytes 24584 | tf_op jit(solution)/shard_map/ppermute | solution.py:397
  61.0 7.0 %collective-permute-start.8 = (bf16[8,512]{1,0:T(8,128)(2,1)S(1)}, bf16[8,512]{1,0:T(8,128)(2,1)S(1)}, u32[]{:S(2)}, u32[]{:S(2)}) collective-permute-start(bf16[8,512]{1,0:T(8,128)(2,1)S(1)} %get-tuple-element.32), channel_id=1, source_target_pairs={{0,16},{16,32},{32,48},{48,64},{64,80},{80,96},{96,112},{112,128},... | collective-permute-start | bytes 24584 | tf_op jit(solution)/shard_map/ppermute | solution.py:397
  67.9 1.5 %collective-permute-start.11 = (bf16[24,512]{1,0:T(8,128)(2,1)S(1)}, bf16[24,512]{1,0:T(8,128)(2,1)S(1)}, u32[]{:S(2)}, u32[]{:S(2)}) collective-permute-start(bf16[24,512]{1,0:T(8,128)(2,1)S(1)} %constant_dynamic-update-slice_fusion), channel_id=1, source_target_pairs={{0,15},{1,0},{2,1},{3,2},{4,3},{5,4},{6,5},{7,6},{8,7},{9,8},{10,9... | collective-permute-start | bytes 73736 | tf_op jit(solution)/shard_map/ppermute | solution.py:397
  68.0 4.5 %collective-permute-start.10 = (bf16[24,512]{1,0:T(8,128)(2,1)S(1)}, bf16[24,512]{1,0:T(8,128)(2,1)S(1)}, u32[]{:S(2)}, u32[]{:S(2)}) collective-permute-start(bf16[24,512]{1,0:T(8,128)(2,1)S(1)} %constant_dynamic-update-slice_fusion), channel_id=1, source_target_pairs={{0,1},{1,2},{2,3},{3,4},{4,5},{5,6},{6,7},{7,8},{8,9},{9,10},{10,1... | collective-permute-start | bytes 73736 | tf_op jit(solution)/shard_map/ppermute | solution.py:397

commit v4 on v3

--- a/solution.py
+++ b/solution.py
@@ -38,49 +38,47 @@
     return jnp.concatenate(parts, axis=1)
 
 
-def rims_kernel(top_ref, bottom_ref, west_ref, east_ref, top_out, bottom_out, west_out, east_out):
+def rows_kernel(top_ref, bottom_ref, top_out, bottom_out):
     top_out[...] = top_ref[...].reshape(2, 32, D).astype(BF)
     bottom_out[...] = bottom_ref[...].reshape(2, 32, D).astype(BF)
+
+
+def columns_kernel(west_ref, east_ref, west_out, east_out):
     for b in range(2):
         west_out[b] = west_ref[b, :, 0, :].astype(BF)
         east_out[b] = east_ref[b, :, 7, :].astype(BF)
 
 
-def rims(fine):
+def rims(body, shape, first, last, fine):
     out = pl.BlockSpec((2, 32, D), lambda i: (0, 0, 0))
     return pl.pallas_call(
-        rims_kernel,
-        name="rims",
+        body,
+        name=body.__name__,
         grid=(1,),
-        in_specs=[
-            pl.BlockSpec((2, 1, 32, D), lambda i: (0, 0, 0, 0)),
-            pl.BlockSpec((2, 1, 32, D), lambda i: (0, 31, 0, 0)),
-            pl.BlockSpec((2, 32, 8, D), lambda i: (0, 0, 0, 0)),
-            pl.BlockSpec((2, 32, 8, D), lambda i: (0, 0, 3, 0)),
-        ],
-        out_specs=[out] * 4,
-        out_shape=[jax.ShapeDtypeStruct((2, 32, D), BF)] * 4,
+        in_specs=[pl.BlockSpec(shape, lambda i: first), pl.BlockSpec(shape, lambda i: last)],
+        out_specs=[out] * 2,
+        out_shape=[jax.ShapeDtypeStruct((2, 32, D), BF)] * 2,
         compiler_params=pltpu.CompilerParams(vmem_limit_bytes=24 << 20),
-        cost_estimate=pl.CostEstimate(flops=1 << 20, bytes_accessed=3 << 20, transcendentals=0),
-    )(fine, fine, fine, fine)
+        cost_estimate=pl.CostEstimate(flops=1 << 24, bytes_accessed=3 << 20, transcendentals=0),
+    )(fine, fine)
 
 
 def prep_kernel(s_hbm, w_hbm, c_ref, rt_out, s_ref, w_ref, sems, w_sem):
     weights = pltpu.make_async_copy(w_hbm.at[0, 0:2], w_ref, w_sem)
     weights.start()
     copies = []
-    for n in range(8):
-        at = (n // 4, pl.ds(8 * (n % 4), 8))
+    for n in range(4):
+        at = (n // 2, pl.ds(16 * (n % 2), 16))
         copies.append(pltpu.make_async_copy(s_hbm.at[at], s_ref.at[n], sems.at[n]))
         copies[-1].start()
     weights.wait()
-    for n in range(8):
+    for n in range(4):
         copies[n].wait()
-        b, i = n // 4, n % 4
+        b, i = n // 2, n % 2
         x = s_ref[n]
-        op = x.reshape(256, D).astype(BF)
-        rt_out[0, b, 8 * i:8 * i + 8] = (0.5 * (mm(op, w_ref[0]) + c_ref[0:1, :])).astype(BF).reshape(8, 32, D)
-        rt_out[1, b, 8 * i:8 * i + 8] = (0.5 * mm(op, w_ref[1])).astype(BF).reshape(8, 32, D)
+        op = x.reshape(512, D).astype(BF)
+        rt_out[0, b, 16 * i:16 * i + 16] = (0.5 * (mm(op, w_ref[0]) + c_ref[0:1, :])).astype(BF).reshape(16, 32, D)
+        rt_out[1, b, 16 * i:16 * i + 16] = (0.5 * mm(op, w_ref[1])).astype(BF).reshape(16, 32, D)
 
 
 def prep(fine, pw, pb):
@@ -93,9 +91,9 @@
         out_specs=full4(2, 2, 32, 32, D),
         out_shape=pltpu.VMEM((2, 2, 32, 32, D), BF),
         scratch_shapes=[
-            pltpu.VMEM((8, 8, 32, D), F32),
+            pltpu.VMEM((4, 16, 32, D), F32),
             pltpu.VMEM((2, D, D), BF),
-            pltpu.SemaphoreType.DMA((8,)),
+            pltpu.SemaphoreType.DMA((4,)),
             pltpu.SemaphoreType.DMA,
         ],
         compiler_params=pltpu.CompilerParams(vmem_limit_bytes=24 << 20),
@@ -137,7 +135,7 @@
         put(0, hs[0, 0:32, :], hs[2, 32:33, :], hs[3, 32:33, :])
         put(33, hs[1, 0:32, :], hs[2, 33:34, :], hs[3, 33:34, :])
 
-        @pl.loop(0, 32)
+        @pl.loop(0, 32, unroll=4)
         def _(i):
             put(i + 1, rt_ref[1, b, i].astype(F32), hs[2, pl.ds(i, 1), :], hs[3, pl.ds(i, 1), :])
 
@@ -199,7 +197,7 @@
         + [pl.BlockSpec(memory_space=pltpu.VMEM)] * 4,
         out_shape=[
             jax.ShapeDtypeStruct((2, 32, 32, D), BF),
-            jax.ShapeDtypeStruct((2, 32, 32, D), F32),
+            pltpu.HBM((2, 32, 32, D), F32),
             jax.ShapeDtypeStruct((128, D), F32),
         ]
         + [jax.ShapeDtypeStruct((16, D), BF)] * 4
@@ -399,8 +397,9 @@
 
 def local(fine, mid, coarse, flags, pw, bw, pb):
     fine, pw, bw = (pltpu.with_memory_space_constraint(a, pltpu.HBM) for a in (fine, pw, bw))
-    top, bottom, west, east = rims(fine)
+    top, bottom = rims(rows_kernel, (2, 1, 32, D), (0, 0, 0, 0), (0, 31, 0, 0), fine)
     up, down = trade(top, bottom, "lat")
+    west, east = rims(columns_kernel, (2, 32, 8, D), (0, 0, 0, 0), (0, 0, 3, 0), fine)
     left, right = trade(
         jnp.concatenate([west, up[:, :1], down[:, :1]], axis=1),
         jnp.concatenate([east, up[:, 31:], down[:, 31:]], axis=1),

time: 77.5 us -> 75 us (0.968)
  local copies, waits for them, and re-layouts: 2.35 us -> 0.41 us
  waiting for transfers between devices: 19.1 us -> 17.4 us
  starting transfers between devices: 19.9 us -> 21.5 us
    unnamed x24 -> x22, local copies, waits for them, and re-layouts: 2 us -> 0.07 us
    ppermute x6, waiting for transfers between devices: 16.4 us -> 14.6 us  [trade(): lax.ppermute(high_side, axis, forward)]
    ppermute x6, starting transfers between devices: 19.2 us -> 20.9 us  [trade(): lax.ppermute(low_side, axis, backward)]
    pallas_call x1, Pallas kernels: 5.95 us -> 5.11 us  [prep(): pl.pallas_call(prep_kernel, name='prep', grid=(1,), in_specs=[ANY, ANY, f...]
    pallas_call x1 -> x2, Pallas kernels: 2.01 us -> 2.84 us  [rims(): pl.pallas_call(body, name=body.__name__, grid=(1,), in_specs=[pl.BlockSpe...]
  transfers between devices with their start and end apart: 12 -> 12, of which waited for: 7 -> 6; matrix products, arithmetic and copies ran while one was open for 1% -> 1% of each run, Pallas kernels for 8% -> 9%
where the time goes in v4:
time: 75 us; the launch traced here: 74.9 us
  Pallas kernels  34.5 us (46%)
  starting transfers between devices  21.5 us (29%)
  waiting for transfers between devices  17.4 us (23%)
  between operations  0.89 us (1%)
    ppermute x6, starting transfers between devices, trade(): lax.ppermute(low_side, axis, backward)  20.9 us
    pallas_call x1, Pallas kernels, edge(): pl.pallas_call(edge_kernel, name='edge', grid=(2, 32 // RB), in_specs=[VM...  19.8 us
    ppermute x6, waiting for transfers between devices, trade(): lax.ppermute(high_side, axis, forward)  14.6 us
    pallas_call x1, Pallas kernels, prep(): pl.pallas_call(prep_kernel, name='prep', grid=(1,), in_specs=[ANY, ANY, f...  5.11 us
    pallas_call x1, Pallas kernels, coarsest(): pl.pallas_call(coarse_kernel, name='coarsest', grid=(1,), in_specs=[full(...  4.61 us
    pallas_call x2, Pallas kernels, rims(): pl.pallas_call(body, name=body.__name__, grid=(1,), in_specs=[pl.BlockSpe...  2.84 us
    ppermute x6, waiting for transfers between devices, trade(): lax.ppermute(low_side, axis, backward)  2.77 us
    pallas_call x1, Pallas kernels, middle(): pl.pallas_call(middle_kernel, name='middle', grid=(1,), in_specs=[full(12...  2.12 us
  transfers between devices with their start and end apart: 12, of which 6 were waited for; matrix products, arithmetic and copies ran while one was open for 1% of the time, Pallas kernels for 9%

profile of v4, /device:TPU:0, one launch (start us, length us, event | category | flops | bytes accessed | tf_op | source)
XLA Modules:
  0.0 74.9 jit_solution(2746386505990507823)
XLA Ops:
  0.6 0.0 copy-start.9
  0.7 1.0 %rows_kernel.1 = (bf16[2,32,512]{2,1,0:T(8,128)(2,1)S(1)}, bf16[2,32,512]{2,1,0:T(8,128)(2,1)S(1)}) custom-call(f32[2,32,32,512]{3,2,1,0:T(8,128)} %s_ref.1, f32[2,32,32,512]{3,2,1,0:T(8,128)} %s_ref.1), custom_call_target="tpu_custom_call" | custom-call | flops 16777216 | bytes 3145728 | tf_op jit(solution)/shard_map/rows_kernel/pallas_call | solution.py:54
  1.7 0.1 collective-permute-start
  1.8 5.3 %collective-permute-start.1 = (bf16[2,32,512]{2,1,0:T(8,128)(2,1)S(1)}, bf16[2,32,512]{2,1,0:T(8,128)(2,1)S(1)}, u32[]{:S(2)}, u32[]{:S(2)}) collective-permute-start(bf16[2,32,512]{2,1,0:T(8,128)(2,1)S(1)} %get-tuple-element.21), channel_id=1, source_target_pairs={{0,240},{16,0},{32,16},{48,32},{64,48},{80,64},{96,80},{112,96},{1... | collective-permute-start | bytes 196616 | tf_op jit(solution)/shard_map/ppermute | solution.py:395
  7.1 0.1 fusion.1
  7.2 0.1 copy.16
  7.3 0.2 copy.17
  7.6 1.8 %columns_kernel.1 = (bf16[2,32,512]{2,1,0:T(8,128)(2,1)S(1)}, bf16[2,32,512]{2,1,0:T(8,128)(2,1)S(1)}) custom-call(f32[2,32,32,512]{3,2,1,0:T(8,128)} %s_ref.1, f32[2,32,32,512]{3,2,1,0:T(8,128)} %s_ref.1), custom_call_target="tpu_custom_call" | custom-call | flops 16777216 | bytes 3145728 | tf_op jit(solution)/shard_map/columns_kernel/pallas_call | solution.py:54
  9.5 3.3 %collective-permute-start.3 = (bf16[2,34,512]{2,1,0:T(8,128)(2,1)S(1)}, bf16[2,34,512]{2,1,0:T(8,128)(2,1)S(1)}, u32[]{:S(2)}, u32[]{:S(2)}) collective-permute-start(bf16[2,34,512]{2,1,0:T(8,128)(2,1)S(1)} %pad_maximum_fusion.1), channel_id=1, source_target_pairs={{0,15},{1,0},{2,1},{3,2},{4,3},{5,4},{6,5},{7,6},{8,7},{9,8},{10,9... | collective-permute-start | bytes 208904 | tf_op jit(solution)/shard_map/ppermute | solution.py:395
  12.8 0.0 copy-start.7
  12.8 0.0 collective-permute-start.2
  12.8 5.1 %prep.1.rt_ref = bf16[2,2,32,32,512]{4,3,2,1,0:T(8,128)(2,1)S(1)} custom-call(f32[2,32,32,512]{3,2,1,0:T(8,128)} %s_ref.1, bf16[3,4,512,512]{3,2,1,0:T(8,128)(2,1)} %pw_hbm.1, f32[3,512]{1,0:T(4,128)S(1)} %copy-done.1), custom_call_target="tpu_custom_call" | custom-call | flops 2147483648 | bytes 5242880 | tf_op jit(solution)/shard_map/prep/pallas_call | solution.py:86
  18.0 0.0 copy-start
  18.0 0.0 copy-start.3
  18.0 0.0 copy-start.5
  18.0 0.0 copy-start.2
  18.0 0.0 copy-start.4
  18.1 19.8 %edge.1 = (bf16[2,32,32,512]{3,2,1,0:T(8,128)(2,1)}, f32[2,32,32,512]{3,2,1,0:T(8,128)}, f32[128,512]{1,0:T(8,128)S(1)}, bf16[16,512]{1,0:T(8,128)(2,1)S(1)}, bf...) custom-call(bf16[2,2,32,32,512]{4,3,2,1,0:T(8,128)(2,1)S(1)} %prep.1, ...), custom_call_target="tpu_custom_call" | custom-call | flops 8589934592 | bytes 16777216 | tf_op jit(solution)/shard_map/edge/pallas_call | solution.py:172
  37.9 0.1 collective-permute-start.4
  38.0 5.3 %collective-permute-start.5 = (bf16[16,512]{1,0:T(8,128)(2,1)S(1)}, bf16[16,512]{1,0:T(8,128)(2,1)S(1)}, u32[]{:S(2)}, u32[]{:S(2)}) collective-permute-start(bf16[16,512]{1,0:T(8,128)(2,1)S(1)} %get-tuple-element.26), channel_id=1, source_target_pairs={{0,240},{16,0},{32,16},{48,32},{64,48},{80,64},{96,80},{112,96},{1... | collective-permute-start | bytes 49160 | tf_op jit(solution)/shard_map/ppermute | solution.py:395
  43.3 1.7 %collective-permute-done.4.refs_0_ = bf16[16,512]{1,0:T(8,128)(2,1)S(1)} collective-permute-done((bf16[16,512]{1,0:T(8,128)(2,1)S(1)}, bf16[16,512]{1,0:T(8,128)(2,1)S(1)}, u32[]{:S(2)}, u32[]{:S(2)}) %collective-permute-start.4) | collective-permute-done | bytes 16416 | tf_op jit(solution)/shard_map/ppermute | solution.py:395
  45.0 1.8 %collective-permute-start.7 = (bf16[48,512]{1,0:T(8,128)(2,1)S(1)}, bf16[48,512]{1,0:T(8,128)(2,1)S(1)}, u32[]{:S(2)}, u32[]{:S(2)}) collective-permute-start(bf16[48,512]{1,0:T(8,128)(2,1)S(1)} %get-tuple-element.42), channel_id=1, source_target_pairs={{0,15},{1,0},{2,1},{3,2},{4,3},{5,4},{6,5},{7,6},{8,7},{9,8},{10,9... | collective-permute-start | bytes 147464 | tf_op jit(solution)/shard_map/ppermute | solution.py:395
  46.8 1.7 %collective-permute-done.7.refs_3_ = bf16[48,512]{1,0:T(8,128)(2,1)S(1)} collective-permute-done((bf16[48,512]{1,0:T(8,128)(2,1)S(1)}, bf16[48,512]{1,0:T(8,128)(2,1)S(1)}, u32[]{:S(2)}, u32[]{:S(2)}) %collective-permute-start.7) | collective-permute-done | bytes 49184 | tf_op jit(solution)/shard_map/ppermute | solution.py:395
  48.5 3.0 %collective-permute-done.6.refs_2_ = bf16[48,512]{1,0:T(8,128)(2,1)S(1)} collective-permute-done((bf16[48,512]{1,0:T(8,128)(2,1)S(1)}, bf16[48,512]{1,0:T(8,128)(2,1)S(1)}, u32[]{:S(2)}, u32[]{:S(2)}) %collective-permute-start.6) | collective-permute-done | bytes 49184 | tf_op jit(solution)/shard_map/ppermute | solution.py:395
  51.5 2.1 %middle.1 = (f32[128,512]{1,0:T(8,128)S(1)}, f32[8,512]{1,0:T(8,128)S(1)}, bf16[8,512]{1,0:T(8,128)(2,1)S(1)}) custom-call(f32[128,512]{1,0:T(8,128)S(1)} %get-tuple-element.24.mz_ref, bf16[16,512]{1,0:T(8,128)(2,1)S(1)} %collective-permute-done.4.refs_0_, bf16[16,512]{1,0:T(8,128)(2,1)S(1)} %collective-permute-done.5.refs_1_, ...), custom_call_target="tpu_custom_call" | custom-call | flops 805306368 | bytes 5242880 | tf_op jit(solution)/shard_map/middle/pallas_call | solution.py:264
  53.6 5.1 %collective-permute-start.9 = (bf16[8,512]{1,0:T(8,128)(2,1)S(1)}, bf16[8,512]{1,0:T(8,128)(2,1)S(1)}, u32[]{:S(2)}, u32[]{:S(2)}) collective-permute-start(bf16[8,512]{1,0:T(8,128)(2,1)S(1)} %get-tuple-element.32), channel_id=1, source_target_pairs={{0,240},{16,0},{32,16},{48,32},{64,48},{80,64},{96,80},{112,96},{1... | collective-permute-start | bytes 24584 | tf_op jit(solution)/shard_map/ppermute | solution.py:395
  58.8 7.0 %collective-permute-done.8.refs_0_ = bf16[8,512]{1,0:T(8,128)(2,1)S(1)} collective-permute-done((bf16[8,512]{1,0:T(8,128)(2,1)S(1)}, bf16[8,512]{1,0:T(8,128)(2,1)S(1)}, u32[]{:S(2)}, u32[]{:S(2)}) %collective-permute-start.8) | collective-permute-done | bytes 8224 | tf_op jit(solution)/shard_map/ppermute | solution.py:395
  65.8 0.0 collective-permute-start.11
  65.8 0.5 collective-permute-start.10
  66.3 1.0 %collective-permute-done.11.refs_3_ = bf16[24,512]{1,0:T(8,128)(2,1)S(1)} collective-permute-done((bf16[24,512]{1,0:T(8,128)(2,1)S(1)}, bf16[24,512]{1,0:T(8,128)(2,1)S(1)}, u32[]{:S(2)}, u32[]{:S(2)}) %collective-permute-start.11) | collective-permute-done | bytes 24608 | tf_op jit(solution)/shard_map/ppermute | solution.py:395
  67.3 3.0 %collective-permute-done.10.refs_2_ = bf16[24,512]{1,0:T(8,128)(2,1)S(1)} collective-permute-done((bf16[24,512]{1,0:T(8,128)(2,1)S(1)}, bf16[24,512]{1,0:T(8,128)(2,1)S(1)}, u32[]{:S(2)}, u32[]{:S(2)}) %collective-permute-start.10) | collective-permute-done | bytes 24608 | tf_op jit(solution)/shard_map/ppermute | solution.py:395
  70.3 4.6 %coarsest.1 = f32[2,32,32,512]{3,2,1,0:T(8,128)} custom-call(f32[8,512]{1,0:T(8,128)S(1)} %get-tuple-element.31.cz_ref, bf16[8,512]{1,0:T(8,128)(2,1)S(1)} %collective-permute-done.8.refs_0_, bf16[8,512]{1,0:T(8,128)(2,1)S(1)} %collective-permute-done.9.refs_1_, bf16[24,512]{1,0:T(8,128)(2,1)S(1)} %collective-permute-done.10.refs_2_, ...), custom_call_target="tpu_custom_call" | custom-call | flops 134217728 | bytes 4194304 | tf_op jit(solution)/shard_map/coarsest/pallas_call | solution.py:330
  (32 shorter events, 0.2 us)
Async XLA Ops:
  0.6 6.5 %copy-start.9 = (s32[8]{0:T(128)S(1)}, s32[8]{0:T(128)}, u32[]{:S(2)}) copy-start(s32[8]{0:T(128)} %constant.23.clone) | copy-start | bytes 100
  0.6 6.6 %copy-start.8 = (s32[8,32,32]{2,1,0:T(8,128)S(1)}, s32[8,32,32]{2,1,0:T(8,128)}, u32[]{:S(2)}) copy-start(s32[8,32,32]{2,1,0:T(8,128)} %param.16) | copy-start | bytes 98308
  1.7 7.7 %collective-permute-start = (bf16[2,32,512]{2,1,0:T(8,128)(2,1)S(1)}, bf16[2,32,512]{2,1,0:T(8,128)(2,1)S(1)}, u32[]{:S(2)}, u32[]{:S(2)}) collective-permute-start(bf16[2,32,512]{2,1,0:T(8,128)(2,1)S(1)} %get-tuple-element.20), channel_id=1, source_target_pairs={{0,16},{16,32},{32,48},{48,64},{64,80},{80,96},{96,112},{112,128},... | collective-permute-start | bytes 196616 | tf_op jit(solution)/shard_map/ppermute | solution.py:395
  1.8 7.7 %collective-permute-start.1 = (bf16[2,32,512]{2,1,0:T(8,128)(2,1)S(1)}, bf16[2,32,512]{2,1,0:T(8,128)(2,1)S(1)}, u32[]{:S(2)}, u32[]{:S(2)}) collective-permute-start(bf16[2,32,512]{2,1,0:T(8,128)(2,1)S(1)} %get-tuple-element.21), channel_id=1, source_target_pairs={{0,240},{16,0},{32,16},{48,32},{64,48},{80,64},{96,80},{112,96},{1... | collective-permute-start | bytes 196616 | tf_op jit(solution)/shard_map/ppermute | solution.py:395
  7.6 5.3 %copy-start.1 = (f32[3,512]{1,0:T(4,128)S(1)}, f32[3,512]{1,0:T(4,128)}, u32[]{:S(2)}) copy-start(f32[3,512]{1,0:T(4,128)} %refs_5_.3) | copy-start | bytes 18436
  9.5 8.5 %collective-permute-start.3 = (bf16[2,34,512]{2,1,0:T(8,128)(2,1)S(1)}, bf16[2,34,512]{2,1,0:T(8,128)(2,1)S(1)}, u32[]{:S(2)}, u32[]{:S(2)}) collective-permute-start(bf16[2,34,512]{2,1,0:T(8,128)(2,1)S(1)} %pad_maximum_fusion.1), channel_id=1, source_target_pairs={{0,15},{1,0},{2,1},{3,2},{4,3},{5,4},{6,5},{7,6},{8,7},{9,8},{10,9... | collective-permute-start | bytes 208904 | tf_op jit(solution)/shard_map/ppermute | solution.py:395
  12.8 5.3 %copy-start.6 = (f32[2,8,8,512]{3,2,1,0:T(8,128)S(1)}, f32[2,8,8,512]{3,2,1,0:T(8,128)}, u32[]{:S(2)}) copy-start(f32[2,8,8,512]{3,2,1,0:T(8,128)} %mid_ref.1) | copy-start | bytes 786436
  12.8 5.3 %copy-start.7 = (bf16[64,128]{1,0:T(8,128)(2,1)S(1)}, bf16[64,128]{1,0:T(8,128)(2,1)}, u32[]{:S(2)}) copy-start(bf16[64,128]{1,0:T(8,128)(2,1)} %constant.24.clone.pick_ref) | copy-start | bytes 49156
  12.8 5.2 %collective-permute-start.2 = (bf16[2,34,512]{2,1,0:T(8,128)(2,1)S(1)}, bf16[2,34,512]{2,1,0:T(8,128)(2,1)S(1)}, u32[]{:S(2)}, u32[]{:S(2)}) collective-permute-start(bf16[2,34,512]{2,1,0:T(8,128)(2,1)S(1)} %pad_maximum_fusion), channel_id=1, source_target_pairs={{0,1},{1,2},{2,3},{3,4},{4,5},{5,6},{6,7},{7,8},{8,9},{9,10},{10,1... | collective-permute-start | bytes 208904 | tf_op jit(solution)/shard_map/ppermute | solution.py:395
  18.0 33.6 %copy-start = (bf16[1024,256]{1,0:T(8,128)(2,1)S(1)}, bf16[1024,256]{1,0:T(8,128)(2,1)}, u32[]{:S(2)}) copy-start(bf16[1024,256]{1,0:T(8,128)(2,1)} %constant.25.clone.refs_8_) | copy-start | bytes 1572868
  18.0 33.5 %copy-start.3 = (f32[2,2,2,512]{3,2,1,0:T(2,128)S(1)}, f32[2,2,2,512]{3,2,1,0:T(2,128)}, u32[]{:S(2)}) copy-start(f32[2,2,2,512]{3,2,1,0:T(2,128)} %refs_7_.1) | copy-start | bytes 49156
  18.0 33.5 %copy-start.5 = (f32[8,128]{1,0:T(8,128)S(1)}, f32[8,128]{1,0:T(8,128)}, u32[]{:S(2)}) copy-start(f32[8,128]{1,0:T(8,128)} %constant.26.clone.refs_9_) | copy-start | bytes 12292
  18.0 52.3 %copy-start.2 = (bf16[128,16]{1,0:T(8,128)(2,1)S(1)}, bf16[128,16]{1,0:T(8,128)(2,1)}, u32[]{:S(2)}) copy-start(bf16[128,16]{1,0:T(8,128)(2,1)} %constant.28.clone.refs_9_) | copy-start | bytes 12292
  18.0 52.3 %copy-start.4 = (bf16[64,128]{1,0:T(8,128)(2,1)S(1)}, bf16[64,128]{1,0:T(8,128)(2,1)}, u32[]{:S(2)}) copy-start(bf16[64,128]{1,0:T(8,128)(2,1)} %constant.27.clone.refs_8_) | copy-start | bytes 49156
  37.9 7.1 %collective-permute-start.4 = (bf16[16,512]{1,0:T(8,128)(2,1)S(1)}, bf16[16,512]{1,0:T(8,128)(2,1)S(1)}, u32[]{:S(2)}, u32[]{:S(2)}) collective-permute-start(bf16[16,512]{1,0:T(8,128)(2,1)S(1)} %get-tuple-element.25), channel_id=1, source_target_pairs={{0,16},{16,32},{32,48},{48,64},{64,80},{80,96},{96,112},{112,128},... | collective-permute-start | bytes 49160 | tf_op jit(solution)/shard_map/ppermute | solution.py:395
  38.0 7.0 %collective-permute-start.5 = (bf16[16,512]{1,0:T(8,128)(2,1)S(1)}, bf16[16,512]{1,0:T(8,128)(2,1)S(1)}, u32[]{:S(2)}, u32[]{:S(2)}) collective-permute-start(bf16[16,512]{1,0:T(8,128)(2,1)S(1)} %get-tuple-element.26), channel_id=1, source_target_pairs={{0,240},{16,0},{32,16},{48,32},{64,48},{80,64},{96,80},{112,96},{1... | collective-permute-start | bytes 49160 | tf_op jit(solution)/shard_map/ppermute | solution.py:395
  45.0 3.5 %collective-permute-start.7 = (bf16[48,512]{1,0:T(8,128)(2,1)S(1)}, bf16[48,512]{1,0:T(8,128)(2,1)S(1)}, u32[]{:S(2)}, u32[]{:S(2)}) collective-permute-start(bf16[48,512]{1,0:T(8,128)(2,1)S(1)} %get-tuple-element.42), channel_id=1, source_target_pairs={{0,15},{1,0},{2,1},{3,2},{4,3},{5,4},{6,5},{7,6},{8,7},{9,8},{10,9... | collective-permute-start | bytes 147464 | tf_op jit(solution)/shard_map/ppermute | solution.py:395
  46.8 4.7 %collective-permute-start.6 = (bf16[48,512]{1,0:T(8,128)(2,1)S(1)}, bf16[48,512]{1,0:T(8,128)(2,1)S(1)}, u32[]{:S(2)}, u32[]{:S(2)}) collective-permute-start(bf16[48,512]{1,0:T(8,128)(2,1)S(1)} %get-tuple-element.43), channel_id=1, source_target_pairs={{0,1},{1,2},{2,3},{3,4},{4,5},{5,6},{6,7},{7,8},{8,9},{9,10},{10,1... | collective-permute-start | bytes 147464 | tf_op jit(solution)/shard_map/ppermute | solution.py:395
  53.6 12.1 %collective-permute-start.9 = (bf16[8,512]{1,0:T(8,128)(2,1)S(1)}, bf16[8,512]{1,0:T(8,128)(2,1)S(1)}, u32[]{:S(2)}, u32[]{:S(2)}) collective-permute-start(bf16[8,512]{1,0:T(8,128)(2,1)S(1)} %get-tuple-element.32), channel_id=1, source_target_pairs={{0,240},{16,0},{32,16},{48,32},{64,48},{80,64},{96,80},{112,96},{1... | collective-permute-start | bytes 24584 | tf_op jit(solution)/shard_map/ppermute | solution.py:395
  58.8 7.0 %collective-permute-start.8 = (bf16[8,512]{1,0:T(8,128)(2,1)S(1)}, bf16[8,512]{1,0:T(8,128)(2,1)S(1)}, u32[]{:S(2)}, u32[]{:S(2)}) collective-permute-start(bf16[8,512]{1,0:T(8,128)(2,1)S(1)} %get-tuple-element.32), channel_id=1, source_target_pairs={{0,16},{16,32},{32,48},{48,64},{64,80},{80,96},{96,112},{112,128},... | collective-permute-start | bytes 24584 | tf_op jit(solution)/shard_map/ppermute | solution.py:395
  65.8 1.5 %collective-permute-start.11 = (bf16[24,512]{1,0:T(8,128)(2,1)S(1)}, bf16[24,512]{1,0:T(8,128)(2,1)S(1)}, u32[]{:S(2)}, u32[]{:S(2)}) collective-permute-start(bf16[24,512]{1,0:T(8,128)(2,1)S(1)} %constant_dynamic-update-slice_fusion), channel_id=1, source_target_pairs={{0,15},{1,0},{2,1},{3,2},{4,3},{5,4},{6,5},{7,6},{8,7},{9,8},{10,9... | collective-permute-start | bytes 73736 | tf_op jit(solution)/shard_map/ppermute | solution.py:395
  65.8 4.5 %collective-permute-start.10 = (bf16[24,512]{1,0:T(8,128)(2,1)S(1)}, bf16[24,512]{1,0:T(8,128)(2,1)S(1)}, u32[]{:S(2)}, u32[]{:S(2)}) collective-permute-start(bf16[24,512]{1,0:T(8,128)(2,1)S(1)} %constant_dynamic-update-slice_fusion), channel_id=1, source_target_pairs={{0,1},{1,2},{2,3},{3,4},{4,5},{5,6},{6,7},{7,8},{8,9},{9,10},{10,1... | collective-permute-start | bytes 73736 | tf_op jit(solution)/shard_map/ppermute | solution.py:395

commit v5 on v4

--- a/solution.py
+++ b/solution.py
@@ -9,6 +9,7 @@
 
 D = 512
 ANY = pl.BlockSpec(memory_space=pl.ANY)
+VM = pl.BlockSpec(memory_space=pltpu.VMEM)
 BF = jnp.bfloat16
 F32 = jnp.float32
 OFFS = ((-1, -1), (-1, 0), (-1, 1), (0, -1), (0, 1), (1, -1), (1, 0), (1, 1))
@@ -101,50 +102,14 @@
     )(fine, pw, pb)
 
 
-def edge_kernel(rt_ref, up_ref, down_ref, left_ref, right_ref,
-                live_ref, w_ref, b0_ref, mid_ref, pick_ref, s_ref, pw_hbm, bw_hbm,
-                avg_out, one_out, mz_out, *rest):
-    rim_outs, (w1_out, w2_out, b1_out, b23_out, sh, hs, tmp, pa, hid, w2_half, sems) = rest[:4], rest[4:]
-    b = pl.program_id(0)
-    blk = pl.program_id(1)
-
-    ahead = [
-        pltpu.make_async_copy(pw_hbm.at[1], w1_out, sems.at[0]),
-        pltpu.make_async_copy(pw_hbm.at[2], w2_out, sems.at[1]),
-        pltpu.make_async_copy(bw_hbm.at[1], b1_out, sems.at[2]),
-        pltpu.make_async_copy(bw_hbm.at[2:4], b23_out, sems.at[3]),
-    ]
-
-    @pl.when((b == 0) & (blk == 0))
-    def _():
-        for copy in ahead:
-            copy.start()
-        w2_half[...] = (w_ref[0, 2].astype(F32) * 0.5).astype(BF)
-
-    @pl.when(blk == 0)
-    def _():
-        for n, ref in enumerate((up_ref, down_ref, left_ref, right_ref)):
-            hs[n, 0:ref.shape[1], :] = (0.5 * mm(ref[0], w_ref[0, 1])).astype(BF).astype(F32)
-        rows = lax.broadcasted_iota(jnp.int32, (32, D), 0)
-
-        def put(i, x, left, right):
-            sh[1, i] = x.astype(BF)
-            sh[0, i] = jnp.where(rows == 0, jnp.broadcast_to(left, (32, D)), pltpu.roll(x, 1, 0)).astype(BF)
-            sh[2, i] = jnp.where(rows == 31, jnp.broadcast_to(right, (32, D)), pltpu.roll(x, 31, 0)).astype(BF)
-
-        put(0, hs[0, 0:32, :], hs[2, 32:33, :], hs[3, 32:33, :])
-        put(33, hs[1, 0:32, :], hs[2, 33:34, :], hs[3, 33:34, :])
-
-        @pl.loop(0, 32, unroll=4)
-        def _(i):
-            put(i + 1, rt_ref[1, b, i].astype(F32), hs[2, pl.ds(i, 1), :], hs[3, pl.ds(i, 1), :])
-
+def messages(rt_ref, live_ref, w_ref, s_ref, sh, w2_half, avg_out, one_out, hid, tmp, pa, blk):
+    b, half = pl.program_id(0), pl.program_id(1)
     row0 = blk * RB
-    rv = rt_ref[0, b, pl.ds(row0, RB)].reshape(RB * 32, D)
-    live = live_ref[...].reshape(RB * 32, 8)
     span = RB * 32
+    rv = rt_ref[0, b, pl.ds(row0, RB)].reshape(span, D)
+    live = live_ref[...].reshape(span, 8)
     for k, (p, q) in enumerate(OFFS):
-        sv = sh[q + 1, pl.ds(row0 + 1 + p, RB)].reshape(span, D)
+        sv = sh[b, q + 1, pl.ds(row0 + 1 + p, RB)].reshape(span, D)
         m = jnp.broadcast_to(live[:, k:k + 1], (span, 128)).astype(BF)
         hid[k * span:(k + 1) * span] = gate(rv + sv) * jnp.concatenate([m] * 4, axis=1)
     msg = gate(mm(hid[...], w2_half[...])).reshape(8, span, D)
@@ -153,72 +118,144 @@
     one = s_ref[0] + mm(avg, w_ref[0, 3]).reshape(RB, 32, D)
     one_out[0] = one
     for g in range(RB // 4):
-        pa[b, blk * (RB // 4) + g] = pool_rows(one, g, tmp)
-
-    @pl.when((b == 1) & (blk == 32 // RB - 1))
+        pa[b, half, g] = pool_rows(one, g, tmp)
+
+
+def parents(pa, mid, b0_ref):
+    pooled = (pa[...].reshape(64, D) * 0.0625).astype(BF)
+    return mid.reshape(64, D) + gate(0.5 * mm(pooled, b0_ref[0]))
+
+
+def outer_kernel(rt_ref, up_ref, down_ref, left_ref, right_ref, live_ref, w_ref, b0_ref, mid_ref, s_ref, pw_hbm, bw_hbm,
+                 avg_out, one_out, mz_out, top_out, bottom_out, w1_out, w2_out, b1_out, b23_out, sh, w2_half,
+                 hs, tmp, pa, hid, sems):
+    b, half = pl.program_id(0), pl.program_id(1)
+    ahead = [
+        pltpu.make_async_copy(pw_hbm.at[1], w1_out, sems.at[0]),
+        pltpu.make_async_copy(pw_hbm.at[2], w2_out, sems.at[1]),
+        pltpu.make_async_copy(bw_hbm.at[1], b1_out, sems.at[2]),
+        pltpu.make_async_copy(bw_hbm.at[2:4], b23_out, sems.at[3]),
+    ]
+
+    @pl.when((b == 0) & (half == 0))
     def _():
-        pooled = (pa[...].reshape(128, D) * 0.0625).astype(BF)
-        mz = mid_ref[...].reshape(128, D) + gate(0.5 * mm(pooled, b0_ref[0]))
+        for copy in ahead:
+            copy.start()
+        w2_half[...] = (w_ref[0, 2].astype(F32) * 0.5).astype(BF)
+
+    @pl.when(half == 0)
+    def _():
+        for n, ref in enumerate((up_ref, down_ref, left_ref, right_ref)):
+            hs[n, 0:ref.shape[1], :] = (0.5 * mm(ref[0], w_ref[0, 1])).astype(BF).astype(F32)
+        rows = lax.broadcasted_iota(jnp.int32, (32, D), 0)
+
+        def put(i, x, left, right):
+            sh[b, 1, i] = x.astype(BF)
+            sh[b, 0, i] = jnp.where(rows == 0, jnp.broadcast_to(left, (32, D)), pltpu.roll(x, 1, 0)).astype(BF)
+            sh[b, 2, i] = jnp.where(rows == 31, jnp.broadcast_to(right, (32, D)), pltpu.roll(x, 31, 0)).astype(BF)
+
+        put(0, hs[0, 0:32, :], hs[2, 32:33, :], hs[3, 32:33, :])
+        put(33, hs[1, 0:32, :], hs[2, 33:34, :], hs[3, 33:34, :])
+
+        @pl.loop(0, 32, unroll=4)
+        def _(i):
+            put(i + 1, rt_ref[1, b, i].astype(F32), hs[2, pl.ds(i, 1), :], hs[3, pl.ds(i, 1), :])
+
+    messages(rt_ref, live_ref, w_ref, s_ref, sh, w2_half, avg_out, one_out, hid, tmp, pa, 3 * half)
+
+    @pl.when((b == 1) & (half == 1))
+    def _():
+        mid = [mid_ref[n // 2, 6 * (n % 2):6 * (n % 2) + 2] for n in range(4)]
+        mz = parents(pa, jnp.concatenate(mid, axis=0), b0_ref)
         mz_out[...] = mz
-        rims = mm(pick_ref[...], mz.astype(BF)).astype(BF)
-        for d in range(4):
-            rim_outs[d][...] = rims[16 * d:16 * d + 16]
+        top_out[...] = jnp.concatenate([mz[0:8], mz[32:40]], axis=0).astype(BF)
+        bottom_out[...] = jnp.concatenate([mz[24:32], mz[56:64]], axis=0).astype(BF)
         for copy in ahead:
             copy.wait()
 
 
-def edge(rt, rim, mask, pw, bw, mid, pick, fine):
+def inner_kernel(rt_ref, live_ref, w_ref, b0_ref, mid_ref, s_ref, sh, w2_half, mzo_ref, pick_ref, avg_in, one_in,
+                 avg_out, one_out, mz_out, west_out, east_out, tmp, pa, hid):
+    b, half = pl.program_id(0), pl.program_id(1)
+    messages(rt_ref, live_ref, w_ref, s_ref, sh, w2_half, avg_out, one_out, hid, tmp, pa, half + 1)
+
+    @pl.when((b == 1) & (half == 1))
+    def _():
+        mzi = parents(pa, mid_ref[:, 2:6], b0_ref)
+        mzo = mzo_ref[...]
+        mz = jnp.concatenate([mzo[0:16], mzi[0:32], mzo[16:48], mzi[32:64], mzo[48:64]], axis=0)
+        mz_out[...] = mz
+        sides = mm(pick_ref[...], mz.astype(BF)).astype(BF)
+        west_out[...] = sides[0:16]
+        east_out[...] = sides[16:32]
+
+
+def edge_specs(place):
     whole = lambda *shape: pl.BlockSpec(shape, lambda b, i: (0,) * len(shape))
-    return pl.pallas_call(
-        edge_kernel,
-        name="edge",
-        grid=(2, 32 // RB),
-        in_specs=[
-            VM,
-        ]
+    tile = pl.BlockSpec((1, RB, 32, D), lambda b, i: (b, place(i), 0, 0))
+    live = pl.BlockSpec((RB, 32, 8), lambda b, i: (place(i), 0, 0))
+    return whole, tile, live
+
+
+EDGE = dict(
+    compiler_params=pltpu.CompilerParams(vmem_limit_bytes=EDGE_VMEM << 20),
+    cost_estimate=pl.CostEstimate(flops=8 * 2048 * D * D, bytes_accessed=8 << 20, transcendentals=8 << 20),
+)
+SCRATCH = [
+    pltpu.VMEM((8, 4, 32, 128), F32),
+    pltpu.VMEM((2, 2, 2, 8, D), F32),
+    pltpu.VMEM((8 * RB * 32, D), BF),
+]
+SHARED = [pltpu.HBM((2, 32, 32, D), BF), pltpu.HBM((2, 32, 32, D), F32)]
+
+
+def outer(rt, rim, mask, pw, bw, mid, fine):
+    whole, tile, live = edge_specs(lambda i: 3 * i)
+    return pl.pallas_call(
+        outer_kernel,
+        name="outer",
+        grid=(2, 2),
+        in_specs=[VM]
         + [pl.BlockSpec((1, 32, D), lambda b, i: (b, 0, 0))] * 2
         + [pl.BlockSpec((1, 34, D), lambda b, i: (b, 0, 0))] * 2
+        + [live, whole(1, 4, D, D), whole(1, D, D), whole(2, 8, 8, D), tile, ANY, ANY],
+        out_specs=[tile, tile, whole(64, D), whole(16, D), whole(16, D)] + [VM] * 6,
+        out_shape=SHARED
         + [
-            pl.BlockSpec((RB, 32, 8), lambda b, i: (i, 0, 0)),
-            whole(1, 4, D, D),
-            whole(1, D, D),
-            whole(2, 8, 8, D),
-            whole(64, 128),
-            pl.BlockSpec((1, RB, 32, D), lambda b, i: (b, i, 0, 0)),
-            ANY,
-            ANY,
-        ],
-        out_specs=[
-            pl.BlockSpec((1, RB, 32, D), lambda b, i: (b, i, 0, 0)),
-            pl.BlockSpec((1, RB, 32, D), lambda b, i: (b, i, 0, 0)),
-            whole(128, D),
-        ]
-        + [whole(16, D)] * 4
-        + [pl.BlockSpec(memory_space=pltpu.VMEM)] * 4,
-        out_shape=[
-            jax.ShapeDtypeStruct((2, 32, 32, D), BF),
-            pltpu.HBM((2, 32, 32, D), F32),
-            jax.ShapeDtypeStruct((128, D), F32),
-        ]
-        + [jax.ShapeDtypeStruct((16, D), BF)] * 4
-        + [
+            jax.ShapeDtypeStruct((64, D), F32),
+            jax.ShapeDtypeStruct((16, D), BF),
+            jax.ShapeDtypeStruct((16, D), BF),
             pltpu.VMEM((4, D, D), BF),
             pltpu.VMEM((4, D, D), BF),
             pltpu.VMEM((D, D), BF),
             pltpu.VMEM((2, D, D), BF),
+            pltpu.VMEM((2, 3, 34, 32, D), BF),
+            pltpu.VMEM((D, D), BF),
         ],
-        scratch_shapes=[
-            pltpu.VMEM((3, 34, 32, D), BF),
-            pltpu.VMEM((4, 40, D), F32),
-            pltpu.VMEM((8, 4, 32, 128), F32),
-            pltpu.VMEM((2, 8, 8, D), F32),
-            pltpu.VMEM((8 * RB * 32, D), BF),
-            pltpu.VMEM((D, D), BF),
-            pltpu.SemaphoreType.DMA((4,)),
+        scratch_shapes=[pltpu.VMEM((4, 40, D), F32)] + SCRATCH + [pltpu.SemaphoreType.DMA((4,))],
+        **EDGE,
+    )(rt, *rim, mask, pw, bw, mid, fine, pw, bw)
+
+
+def inner(rt, mask, pw, bw, mid, fine, sh, w2_half, mzo, pick, avg, one):
+    whole, tile, live = edge_specs(lambda i: i + 1)
+    return pl.pallas_call(
+        inner_kernel,
+        name="inner",
+        grid=(2, 2),
+        in_specs=[VM, live, whole(1, 4, D, D), whole(1, D, D), whole(2, 8, 8, D), tile, VM, VM]
+        + [whole(64, D), whole(32, 128), ANY, ANY],
+        out_specs=[tile, tile, whole(128, D), whole(16, D), whole(16, D)],
+        out_shape=SHARED
+        + [
+            jax.ShapeDtypeStruct((128, D), F32),
+            jax.ShapeDtypeStruct((16, D), BF),
+            jax.ShapeDtypeStruct((16, D), BF),
         ],
-        compiler_params=pltpu.CompilerParams(vmem_limit_bytes=EDGE_VMEM << 20),
-        cost_estimate=pl.CostEstimate(flops=2 * 8 * 2048 * D * D, bytes_accessed=16 << 20, transcendentals=16 << 20),
-    )(rt, *rim, mask, pw, bw, mid, pick, fine, pw, bw)
+        input_output_aliases={10: 0, 11: 1},
+        scratch_shapes=SCRATCH,
+        **EDGE,
+    )(rt, mask, pw, bw, mid, fine, sh, w2_half, mzo, pick, avg, one)
 
 
 def live_sides(first, last):
@@ -251,9 +288,6 @@
     cz = flat[...] + gate(0.5 * mm(pooled.astype(BF), b1_ref[...]))
     cz_out[...] = cz
     czb_out[...] = cz.astype(BF)
-
-
-VM = pl.BlockSpec(memory_space=pltpu.VMEM)
 
 
 def full(*shape):
@@ -344,10 +378,10 @@
 
 
 def place_middle():
-    pick = np.zeros((64, 128), np.float32)
+    pick = np.zeros((32, 128), np.float32)
     for b in range(2):
         for n in range(8):
-            for d, (i, j) in enumerate(((0, n), (7, n), (n, 0), (n, 7))):
+            for d, (i, j) in enumerate(((n, 0), (n, 7))):
                 pick[16 * d + 8 * b + n, 64 * b + 8 * i + j] = 1
     gather = np.zeros((1024, 256), np.float32)
     for k, (p, q) in enumerate(OFFS):
@@ -415,11 +449,10 @@
     pick, gather, mean = place_middle()
     gather_c, lift = place_coarse()
     rt = prep(fine, pw, pb)
-    avg, one, mz, top, bottom, west, east, w1, w2, b1, b23 = edge(
-        rt, (up, down, left, right), mask, pw, bw, mid, jnp.asarray(pick, BF), fine
-    )
+    avg, one, mzo, top, bottom, w1, w2, b1, b23, sh, w2_half = outer(rt, (up, down, left, right), mask, pw, bw, mid, fine)
+    up, down = trade(top, bottom, "lat")
+    avg, one, mz, west, east = inner(rt, mask, pw, bw, mid, fine, sh, w2_half, mzo, jnp.asarray(pick, BF), avg, one)
     one = pltpu.with_memory_space_constraint(one, pltpu.HBM)
-    up, down = trade(top, bottom, "lat")
     left, right = trade(jnp.concatenate([west, up, down]), jnp.concatenate([east, up, down]), "lon")
     mo, cz, czb = middle(
         mz, (up, down, left, right), w1, pb, b1, coarse, jnp.asarray(gather, BF), jnp.asarray(mean, F32)

time: 75 us -> 71.6 us (0.955)
  starting transfers between devices: 21.5 us -> 17.4 us
  Pallas kernels: 34.5 us -> 37.3 us
  waiting for transfers between devices: 17.4 us -> 15.3 us
    ppermute x6, starting transfers between devices: 20.9 us -> 16.4 us  [trade(): lax.ppermute(low_side, axis, backward)]
    pallas_call x1 -> x2, Pallas kernels: 19.8 us -> 22.6 us  [the longest x1 12.3 us: outer(): pl.pallas_call(outer_kernel, name='outer', grid=(2, 2), in_specs=[VM] + [...]
    ppermute x6, waiting for transfers between devices: 14.6 us -> 12.5 us  [trade(): lax.ppermute(high_side, axis, forward)]
  transfers between devices with their start and end apart: 12 -> 12, of which waited for: 6 -> 5; matrix products, arithmetic and copies ran while one was open for 1% -> 1% of each run, Pallas kernels for 9% -> 24%
where the time goes in v5:
time: 71.6 us; the launch traced here: 71.5 us
  Pallas kernels  37.3 us (52%)
  starting transfers between devices  17.4 us (24%)
  waiting for transfers between devices  15.3 us (21%)
  between operations  0.87 us (1%)
    ppermute x6, starting transfers between devices, trade(): lax.ppermute(low_side, axis, backward)  16.4 us
    ppermute x6, waiting for transfers between devices, trade(): lax.ppermute(high_side, axis, forward)  12.5 us
    pallas_call x1, Pallas kernels, outer(): pl.pallas_call(outer_kernel, name='outer', grid=(2, 2), in_specs=[VM] + [...  12.3 us
    pallas_call x1, Pallas kernels, inner(): pl.pallas_call(inner_kernel, name='inner', grid=(2, 2), in_specs=[VM, liv...  10.3 us
    pallas_call x1, Pallas kernels, prep(): pl.pallas_call(prep_kernel, name='prep', grid=(1,), in_specs=[ANY, ANY, f...  5.07 us
    pallas_call x1, Pallas kernels, coarsest(): pl.pallas_call(coarse_kernel, name='coarsest', grid=(1,), in_specs=[full(...  4.61 us
    pallas_call x2, Pallas kernels, rims(): pl.pallas_call(body, name=body.__name__, grid=(1,), in_specs=[pl.BlockSpe...  2.84 us
    ppermute x6, waiting for transfers between devices, trade(): lax.ppermute(low_side, axis, backward)  2.77 us
  transfers between devices with their start and end apart: 12, of which 5 were waited for; matrix products, arithmetic and copies ran while one was open for 1% of the time, Pallas kernels for 24%

profile of v5, /device:TPU:0, one launch (start us, length us, event | category | flops | bytes accessed | tf_op | source)
XLA Modules:
  0.0 71.5 jit_solution(11942613558650708605)
XLA Ops:
  0.6 0.0 copy-start.9
  0.7 1.0 %rows_kernel.1 = (bf16[2,32,512]{2,1,0:T(8,128)(2,1)S(1)}, bf16[2,32,512]{2,1,0:T(8,128)(2,1)S(1)}) custom-call(f32[2,32,32,512]{3,2,1,0:T(8,128)} %s_ref.3, f32[2,32,32,512]{3,2,1,0:T(8,128)} %s_ref.3), custom_call_target="tpu_custom_call" | custom-call | flops 16777216 | bytes 3145728 | tf_op jit(solution)/shard_map/rows_kernel/pallas_call | solution.py:55
  1.7 0.1 collective-permute-start
  1.8 5.3 %collective-permute-start.1 = (bf16[2,32,512]{2,1,0:T(8,128)(2,1)S(1)}, bf16[2,32,512]{2,1,0:T(8,128)(2,1)S(1)}, u32[]{:S(2)}, u32[]{:S(2)}) collective-permute-start(bf16[2,32,512]{2,1,0:T(8,128)(2,1)S(1)} %get-tuple-element.26), channel_id=1, source_target_pairs={{0,240},{16,0},{32,16},{48,32},{64,48},{80,64},{96,80},{112,96},{1... | collective-permute-start | bytes 196616 | tf_op jit(solution)/shard_map/ppermute | solution.py:429
  7.1 0.1 fusion.1
  7.2 0.1 copy.18
  7.3 0.2 copy.19
  7.6 0.0 copy-start.2
  7.6 1.8 %columns_kernel.1 = (bf16[2,32,512]{2,1,0:T(8,128)(2,1)S(1)}, bf16[2,32,512]{2,1,0:T(8,128)(2,1)S(1)}) custom-call(f32[2,32,32,512]{3,2,1,0:T(8,128)} %s_ref.3, f32[2,32,32,512]{3,2,1,0:T(8,128)} %s_ref.3), custom_call_target="tpu_custom_call" | custom-call | flops 16777216 | bytes 3145728 | tf_op jit(solution)/shard_map/columns_kernel/pallas_call | solution.py:55
  9.5 0.0 collective-permute-start.2
  9.5 0.0 copy-start
  9.6 3.3 %collective-permute-start.3 = (bf16[2,34,512]{2,1,0:T(8,128)(2,1)S(1)}, bf16[2,34,512]{2,1,0:T(8,128)(2,1)S(1)}, u32[]{:S(2)}, u32[]{:S(2)}) collective-permute-start(bf16[2,34,512]{2,1,0:T(8,128)(2,1)S(1)} %pad_maximum_fusion.1), channel_id=1, source_target_pairs={{0,15},{1,0},{2,1},{3,2},{4,3},{5,4},{6,5},{7,6},{8,7},{9,8},{10,9... | collective-permute-start | bytes 208904 | tf_op jit(solution)/shard_map/ppermute | solution.py:429
  12.8 5.1 %prep.1.rt_ref = bf16[2,2,32,32,512]{4,3,2,1,0:T(8,128)(2,1)S(1)} custom-call(f32[2,32,32,512]{3,2,1,0:T(8,128)} %s_ref.3, bf16[3,4,512,512]{3,2,1,0:T(8,128)(2,1)} %w_ref.3, f32[3,512]{1,0:T(4,128)S(1)} %copy-done.2), custom_call_target="tpu_custom_call" | custom-call | flops 2147483648 | bytes 5242880 | tf_op jit(solution)/shard_map/prep/pallas_call | solution.py:87
  17.9 0.0 copy-start.6
  18.0 12.3 %outer.1 = (bf16[2,32,32,512]{3,2,1,0:T(8,128)(2,1)}, f32[2,32,32,512]{3,2,1,0:T(8,128)}, f32[64,512]{1,0:T(8,128)S(1)}, bf16[16,512]{1,0:T(8,128)(2,1)S(1)}, bf...) custom-call(bf16[2,2,32,32,512]{4,3,2,1,0:T(8,128)(2,1)S(1)} %prep.1, ...), custom_call_target="tpu_custom_call" | custom-call | flops 4294967296 | bytes 8388608 | tf_op jit(solution)/shard_map/outer/pallas_call | solution.py:214
  30.3 0.1 collective-permute-start.4
  30.3 5.3 %collective-permute-start.5 = (bf16[16,512]{1,0:T(8,128)(2,1)S(1)}, bf16[16,512]{1,0:T(8,128)(2,1)S(1)}, u32[]{:S(2)}, u32[]{:S(2)}) collective-permute-start(bf16[16,512]{1,0:T(8,128)(2,1)S(1)} %get-tuple-element.36), channel_id=1, source_target_pairs={{0,240},{16,0},{32,16},{48,32},{64,48},{80,64},{96,80},{112,96},{1... | collective-permute-start | bytes 49160 | tf_op jit(solution)/shard_map/ppermute | solution.py:429
  35.7 0.0 copy-start.3
  35.7 0.0 copy-start.5
  35.7 10.3 %inner.1 = (bf16[2,32,32,512]{3,2,1,0:T(8,128)(2,1)}, f32[2,32,32,512]{3,2,1,0:T(8,128)}, f32[128,512]{1,0:T(8,128)S(1)}, bf16[16,512]{1,0:T(8,128)(2,1)S(1)}, bf16[16,512]{1,0:T(8,128)(2,1)S(1)}) custom-call(bf16[2,2,32,32,512]{4,3,2,1,0:T(8,128)(2,1)S(1)} %prep.1.rt_ref, ...), custom_call_target="tpu_custom_call", output_to_operand_aliasing={{0}: (10, {}), {1}: (11, {})} | custom-call | flops 4294967296 | bytes 8388608 | tf_op jit(solution)/shard_map/inner/pallas_call | solution.py:242
  46.1 0.7 collective-permute-start.7
  46.8 1.7 %collective-permute-done.7.refs_3_ = bf16[48,512]{1,0:T(8,128)(2,1)S(1)} collective-permute-done((bf16[48,512]{1,0:T(8,128)(2,1)S(1)}, bf16[48,512]{1,0:T(8,128)(2,1)S(1)}, u32[]{:S(2)}, u32[]{:S(2)}) %collective-permute-start.7) | collective-permute-done | bytes 49184 | tf_op jit(solution)/shard_map/ppermute | solution.py:429
  48.5 3.0 %collective-permute-done.6.refs_2_ = bf16[48,512]{1,0:T(8,128)(2,1)S(1)} collective-permute-done((bf16[48,512]{1,0:T(8,128)(2,1)S(1)}, bf16[48,512]{1,0:T(8,128)(2,1)S(1)}, u32[]{:S(2)}, u32[]{:S(2)}) %collective-permute-start.6) | collective-permute-done | bytes 49184 | tf_op jit(solution)/shard_map/ppermute | solution.py:429
  51.5 2.1 %middle.1 = (f32[128,512]{1,0:T(8,128)S(1)}, f32[8,512]{1,0:T(8,128)S(1)}, bf16[8,512]{1,0:T(8,128)(2,1)S(1)}) custom-call(f32[128,512]{1,0:T(8,128)S(1)} %get-tuple-element.34.mz_ref, bf16[16,512]{1,0:T(8,128)(2,1)S(1)} %collective-permute-done.4.refs_0_, bf16[16,512]{1,0:T(8,128)(2,1)S(1)} %collective-permute-done.5.refs_1_, ...), custom_call_target="tpu_custom_call" | custom-call | flops 805306368 | bytes 5242880 | tf_op jit(solution)/shard_map/middle/pallas_call | solution.py:298
  53.6 1.7 %collective-permute-start.9 = (bf16[8,512]{1,0:T(8,128)(2,1)S(1)}, bf16[8,512]{1,0:T(8,128)(2,1)S(1)}, u32[]{:S(2)}, u32[]{:S(2)}) collective-permute-start(bf16[8,512]{1,0:T(8,128)(2,1)S(1)} %get-tuple-element.42), channel_id=1, source_target_pairs={{0,240},{16,0},{32,16},{48,32},{64,48},{80,64},{96,80},{112,96},{1... | collective-permute-start | bytes 24584 | tf_op jit(solution)/shard_map/ppermute | solution.py:429
  55.4 0.4 collective-permute-start.8
  55.8 6.6 %collective-permute-done.8.refs_0_ = bf16[8,512]{1,0:T(8,128)(2,1)S(1)} collective-permute-done((bf16[8,512]{1,0:T(8,128)(2,1)S(1)}, bf16[8,512]{1,0:T(8,128)(2,1)S(1)}, u32[]{:S(2)}, u32[]{:S(2)}) %collective-permute-start.8) | collective-permute-done | bytes 8224 | tf_op jit(solution)/shard_map/ppermute | solution.py:429
  62.4 0.0 collective-permute-start.11
  62.4 0.5 collective-permute-start.10
  62.9 1.0 %collective-permute-done.11.refs_3_ = bf16[24,512]{1,0:T(8,128)(2,1)S(1)} collective-permute-done((bf16[24,512]{1,0:T(8,128)(2,1)S(1)}, bf16[24,512]{1,0:T(8,128)(2,1)S(1)}, u32[]{:S(2)}, u32[]{:S(2)}) %collective-permute-start.11) | collective-permute-done | bytes 24608 | tf_op jit(solution)/shard_map/ppermute | solution.py:429
  63.9 3.0 %collective-permute-done.10.refs_2_ = bf16[24,512]{1,0:T(8,128)(2,1)S(1)} collective-permute-done((bf16[24,512]{1,0:T(8,128)(2,1)S(1)}, bf16[24,512]{1,0:T(8,128)(2,1)S(1)}, u32[]{:S(2)}, u32[]{:S(2)}) %collective-permute-start.10) | collective-permute-done | bytes 24608 | tf_op jit(solution)/shard_map/ppermute | solution.py:429
  66.9 4.6 %coarsest.1 = f32[2,32,32,512]{3,2,1,0:T(8,128)} custom-call(f32[8,512]{1,0:T(8,128)S(1)} %get-tuple-element.41.cz_ref, bf16[8,512]{1,0:T(8,128)(2,1)S(1)} %collective-permute-done.8.refs_0_, bf16[8,512]{1,0:T(8,128)(2,1)S(1)} %collective-permute-done.9.refs_1_, bf16[24,512]{1,0:T(8,128)(2,1)S(1)} %collective-permute-done.10.refs_2_, ...), custom_call_target="tpu_custom_call" | custom-call | flops 134217728 | bytes 4194304 | tf_op jit(solution)/shard_map/coarsest/pallas_call | solution.py:364
  (33 shorter events, 0.2 us)
Async XLA Ops:
  0.6 6.5 %copy-start.9 = (s32[8]{0:T(128)S(1)}, s32[8]{0:T(128)}, u32[]{:S(2)}) copy-start(s32[8]{0:T(128)} %constant.23.clone) | copy-start | bytes 100
  0.6 6.6 %copy-start.8 = (s32[8,32,32]{2,1,0:T(8,128)S(1)}, s32[8,32,32]{2,1,0:T(8,128)}, u32[]{:S(2)}) copy-start(s32[8,32,32]{2,1,0:T(8,128)} %param.16) | copy-start | bytes 98308
  1.7 7.7 %collective-permute-start = (bf16[2,32,512]{2,1,0:T(8,128)(2,1)S(1)}, bf16[2,32,512]{2,1,0:T(8,128)(2,1)S(1)}, u32[]{:S(2)}, u32[]{:S(2)}) collective-permute-start(bf16[2,32,512]{2,1,0:T(8,128)(2,1)S(1)} %get-tuple-element.25), channel_id=1, source_target_pairs={{0,16},{16,32},{32,48},{48,64},{64,80},{80,96},{96,112},{112,128},... | collective-permute-start | bytes 196616 | tf_op jit(solution)/shard_map/ppermute | solution.py:429
  1.8 7.7 %collective-permute-start.1 = (bf16[2,32,512]{2,1,0:T(8,128)(2,1)S(1)}, bf16[2,32,512]{2,1,0:T(8,128)(2,1)S(1)}, u32[]{:S(2)}, u32[]{:S(2)}) collective-permute-start(bf16[2,32,512]{2,1,0:T(8,128)(2,1)S(1)} %get-tuple-element.26), channel_id=1, source_target_pairs={{0,240},{16,0},{32,16},{48,32},{64,48},{80,64},{96,80},{112,96},{1... | collective-permute-start | bytes 196616 | tf_op jit(solution)/shard_map/ppermute | solution.py:429
  7.6 5.2 %copy-start.2 = (f32[3,512]{1,0:T(4,128)S(1)}, f32[3,512]{1,0:T(4,128)}, u32[]{:S(2)}) copy-start(f32[3,512]{1,0:T(4,128)} %refs_5_.3) | copy-start | bytes 18436
  9.5 8.4 %collective-permute-start.2 = (bf16[2,34,512]{2,1,0:T(8,128)(2,1)S(1)}, bf16[2,34,512]{2,1,0:T(8,128)(2,1)S(1)}, u32[]{:S(2)}, u32[]{:S(2)}) collective-permute-start(bf16[2,34,512]{2,1,0:T(8,128)(2,1)S(1)} %pad_maximum_fusion), channel_id=1, source_target_pairs={{0,1},{1,2},{2,3},{3,4},{4,5},{5,6},{6,7},{7,8},{8,9},{9,10},{10,1... | collective-permute-start | bytes 208904 | tf_op jit(solution)/shard_map/ppermute | solution.py:429
  9.5 8.4 %copy-start = (f32[2,8,8,512]{3,2,1,0:T(8,128)S(1)}, f32[2,8,8,512]{3,2,1,0:T(8,128)}, u32[]{:S(2)}) copy-start(f32[2,8,8,512]{3,2,1,0:T(8,128)} %mid_ref.3) | copy-start | bytes 786436
  9.6 8.4 %collective-permute-start.3 = (bf16[2,34,512]{2,1,0:T(8,128)(2,1)S(1)}, bf16[2,34,512]{2,1,0:T(8,128)(2,1)S(1)}, u32[]{:S(2)}, u32[]{:S(2)}) collective-permute-start(bf16[2,34,512]{2,1,0:T(8,128)(2,1)S(1)} %pad_maximum_fusion.1), channel_id=1, source_target_pairs={{0,15},{1,0},{2,1},{3,2},{4,3},{5,4},{6,5},{7,6},{8,7},{9,8},{10,9... | collective-permute-start | bytes 208904 | tf_op jit(solution)/shard_map/ppermute | solution.py:429
  17.9 17.8 %copy-start.6 = (bf16[32,128]{1,0:T(8,128)(2,1)S(1)}, bf16[32,128]{1,0:T(8,128)(2,1)}, u32[]{:S(2)}) copy-start(bf16[32,128]{1,0:T(8,128)(2,1)} %constant.24.clone.pick_ref) | copy-start | bytes 24580
  30.3 15.8 %collective-permute-start.4 = (bf16[16,512]{1,0:T(8,128)(2,1)S(1)}, bf16[16,512]{1,0:T(8,128)(2,1)S(1)}, u32[]{:S(2)}, u32[]{:S(2)}) collective-permute-start(bf16[16,512]{1,0:T(8,128)(2,1)S(1)} %get-tuple-element.35), channel_id=1, source_target_pairs={{0,16},{16,32},{32,48},{48,64},{64,80},{80,96},{96,112},{112,128},... | collective-permute-start | bytes 49160 | tf_op jit(solution)/shard_map/ppermute | solution.py:429
  30.3 15.7 %collective-permute-start.5 = (bf16[16,512]{1,0:T(8,128)(2,1)S(1)}, bf16[16,512]{1,0:T(8,128)(2,1)S(1)}, u32[]{:S(2)}, u32[]{:S(2)}) collective-permute-start(bf16[16,512]{1,0:T(8,128)(2,1)S(1)} %get-tuple-element.36), channel_id=1, source_target_pairs={{0,240},{16,0},{32,16},{48,32},{64,48},{80,64},{96,80},{112,96},{1... | collective-permute-start | bytes 49160 | tf_op jit(solution)/shard_map/ppermute | solution.py:429
  35.7 15.8 %copy-start.1 = (bf16[1024,256]{1,0:T(8,128)(2,1)S(1)}, bf16[1024,256]{1,0:T(8,128)(2,1)}, u32[]{:S(2)}) copy-start(bf16[1024,256]{1,0:T(8,128)(2,1)} %constant.25.clone.refs_8_) | copy-start | bytes 1572868
  35.7 15.8 %copy-start.4 = (f32[2,2,2,512]{3,2,1,0:T(2,128)S(1)}, f32[2,2,2,512]{3,2,1,0:T(2,128)}, u32[]{:S(2)}) copy-start(f32[2,2,2,512]{3,2,1,0:T(2,128)} %refs_7_.1) | copy-start | bytes 49156
  35.7 15.8 %copy-start.7 = (f32[8,128]{1,0:T(8,128)S(1)}, f32[8,128]{1,0:T(8,128)}, u32[]{:S(2)}) copy-start(f32[8,128]{1,0:T(8,128)} %constant.26.clone.refs_9_) | copy-start | bytes 12292
  35.7 31.2 %copy-start.3 = (bf16[128,16]{1,0:T(8,128)(2,1)S(1)}, bf16[128,16]{1,0:T(8,128)(2,1)}, u32[]{:S(2)}) copy-start(bf16[128,16]{1,0:T(8,128)(2,1)} %constant.28.clone.refs_9_) | copy-start | bytes 12292
  35.7 31.2 %copy-start.5 = (bf16[64,128]{1,0:T(8,128)(2,1)S(1)}, bf16[64,128]{1,0:T(8,128)(2,1)}, u32[]{:S(2)}) copy-start(bf16[64,128]{1,0:T(8,128)(2,1)} %constant.27.clone.refs_8_) | copy-start | bytes 49156
  46.1 2.5 %collective-permute-start.7 = (bf16[48,512]{1,0:T(8,128)(2,1)S(1)}, bf16[48,512]{1,0:T(8,128)(2,1)S(1)}, u32[]{:S(2)}, u32[]{:S(2)}) collective-permute-start(bf16[48,512]{1,0:T(8,128)(2,1)S(1)} %get-tuple-element.52), channel_id=1, source_target_pairs={{0,15},{1,0},{2,1},{3,2},{4,3},{5,4},{6,5},{7,6},{8,7},{9,8},{10,9... | collective-permute-start | bytes 147464 | tf_op jit(solution)/shard_map/ppermute | solution.py:429
  46.8 4.7 %collective-permute-start.6 = (bf16[48,512]{1,0:T(8,128)(2,1)S(1)}, bf16[48,512]{1,0:T(8,128)(2,1)S(1)}, u32[]{:S(2)}, u32[]{:S(2)}) collective-permute-start(bf16[48,512]{1,0:T(8,128)(2,1)S(1)} %get-tuple-element.53), channel_id=1, source_target_pairs={{0,1},{1,2},{2,3},{3,4},{4,5},{5,6},{6,7},{7,8},{8,9},{9,10},{10,1... | collective-permute-start | bytes 147464 | tf_op jit(solution)/shard_map/ppermute | solution.py:429
  53.6 8.7 %collective-permute-start.9 = (bf16[8,512]{1,0:T(8,128)(2,1)S(1)}, bf16[8,512]{1,0:T(8,128)(2,1)S(1)}, u32[]{:S(2)}, u32[]{:S(2)}) collective-permute-start(bf16[8,512]{1,0:T(8,128)(2,1)S(1)} %get-tuple-element.42), channel_id=1, source_target_pairs={{0,240},{16,0},{32,16},{48,32},{64,48},{80,64},{96,80},{112,96},{1... | collective-permute-start | bytes 24584 | tf_op jit(solution)/shard_map/ppermute | solution.py:429
  55.4 7.0 %collective-permute-start.8 = (bf16[8,512]{1,0:T(8,128)(2,1)S(1)}, bf16[8,512]{1,0:T(8,128)(2,1)S(1)}, u32[]{:S(2)}, u32[]{:S(2)}) collective-permute-start(bf16[8,512]{1,0:T(8,128)(2,1)S(1)} %get-tuple-element.42), channel_id=1, source_target_pairs={{0,16},{16,32},{32,48},{48,64},{64,80},{80,96},{96,112},{112,128},... | collective-permute-start | bytes 24584 | tf_op jit(solution)/shard_map/ppermute | solution.py:429
  62.4 1.5 %collective-permute-start.11 = (bf16[24,512]{1,0:T(8,128)(2,1)S(1)}, bf16[24,512]{1,0:T(8,128)(2,1)S(1)}, u32[]{:S(2)}, u32[]{:S(2)}) collective-permute-start(bf16[24,512]{1,0:T(8,128)(2,1)S(1)} %constant_dynamic-update-slice_fusion), channel_id=1, source_target_pairs={{0,15},{1,0},{2,1},{3,2},{4,3},{5,4},{6,5},{7,6},{8,7},{9,8},{10,9... | collective-permute-start | bytes 73736 | tf_op jit(solution)/shard_map/ppermute | solution.py:429
  62.4 4.5 %collective-permute-start.10 = (bf16[24,512]{1,0:T(8,128)(2,1)S(1)}, bf16[24,512]{1,0:T(8,128)(2,1)S(1)}, u32[]{:S(2)}, u32[]{:S(2)}) collective-permute-start(bf16[24,512]{1,0:T(8,128)(2,1)S(1)} %constant_dynamic-update-slice_fusion), channel_id=1, source_target_pairs={{0,1},{1,2},{2,3},{3,4},{4,5},{5,6},{6,7},{7,8},{8,9},{9,10},{10,1... | collective-permute-start | bytes 73736 | tf_op jit(solution)/shard_map/ppermute | solution.py:429
